TPU v7x, 256 devices: a whole 4x4x8 slice. The times are simulated.
256 devices in a mesh: dp: 64 (over x, y_hi, z), mp: 4 (over y_lo, core).
Axes of the slice: x: 4, y: 4 (y_hi: 2, y_lo: 2; y = y_hi * 2 + y_lo), z: 8, core: 2. Of those that a mesh axis runs over, the one named last changes fastest.
Arguments:
- z_star: bfloat16 [64, 257, 1280], P('dp', None, 'mp'), may hold values from -24 to 24
- cotangent: float32 [64, 257, 1280], P('dp', None, 'mp'), may hold values from -16 to 16
- w_qkv: bfloat16 [3, 1280, 1280], P(None, None, 'mp'), may hold values from -1 to 1
- w_out: bfloat16 [1280, 1280], P('mp'), may hold values from -0.15625 to 0.15625
Outputs:
- implicit: float32 [64, 257, 1280], P('dp', None, 'mp')
- grad_qkv: float32 [3, 1280, 1280], P(None, 'dp', 'mp')
- grad_out: float32 [1280, 1280], P('mp', 'dp')
All inputs are finite; a program needn't handle non-finite values.
Results may differ from a plain program's by a relative error of at most 0.0091.
Values may be sent and summed in bfloat16 or wider, within the bound.
No kernel may reach another device: no remote copies, remote signals or barrier semaphores. Data moves between devices by JAX's collectives and lax.ppermute only.
A program may use at most 128 MiB of HBM per device.

v0:
```python
import functools
import math

import jax
import jax.numpy as jnp
from jax import lax
from jax.experimental import pallas as pl
from jax.experimental.pallas import tpu as pltpu
from jax.sharding import Mesh
from jax.sharding import PartitionSpec as P

HD = 80
AXES = ("x", "yh", "z", "yl", "c")
DP = ("x", "yh", "z")
MP = ("yl", "c")
SWAP = [(0, 1), (1, 0)]

epsilon = 1e-06
f32 = jnp.float32
bf16 = jnp.bfloat16
SCALE = HD ** (-0.5)
ROWS = (((0,), (0,)), ((), ()))
COLS = (((1,), (1,)), ((), ()))


def dot(a, b, dims=(((1,), (0,)), ((), ()))):
    return lax.dot_general(a, b, dims, preferred_element_type=f32)


def call(body, outs, ins, scratch=(), flops=0, name=None):
    vmem = pl.BlockSpec(memory_space=pltpu.VMEM)
    smem = pl.BlockSpec(memory_space=pltpu.SMEM)
    size = sum(math.prod(o.shape) * o.dtype.itemsize for o in list(outs) + list(ins))
    return pl.pallas_call(
        body,
        out_shape=outs,
        in_specs=[smem] + [vmem] * (len(ins) - 1),
        out_specs=[vmem] * len(outs),
        scratch_shapes=list(scratch),
        compiler_params=pltpu.CompilerParams(vmem_limit_bytes=28 * 2**20),
        cost_estimate=pl.CostEstimate(flops=flops, bytes_accessed=size, transcendentals=0),
        name=name,
    )(*ins)


def like(shape, dtype):
    return jax.ShapeDtypeStruct(shape, dtype)


def put_pieces(where, spot, pieces):
    narrow = pieces[0].shape[1]
    for g in range(4):

        @pl.when(where[0] == g)
        def _():
            for r, piece in zip((0, 2, 1, 3), pieces):
                at = (g ^ r) * narrow
                spot[:, at : at + narrow] = piece[...].astype(spot.dtype)


def put_halves(where, spot, own, oth):
    narrow = own.shape[1] // 2
    for c in range(2):

        @pl.when(where[1] == c)
        def _():
            for half, core in ((own, c), (oth, 1 - c)):
                for y in range(2):
                    at = (2 * y + core) * narrow
                    spot[:, at : at + narrow] = half[:, y * narrow : (y + 1) * narrow].astype(spot.dtype)


def forward_body(where, z0, zy, zc, zcy, w, normal_o, xt_o, inv_o, qkv_o, probs_o, att_o, zs):
    put_pieces(where, zs, (z0, zy, zc, zcy))
    width = zs.shape[1]
    narrow = w.shape[2]
    values = zs[...].astype(f32)
    centred = values - jnp.sum(values, axis=-1, keepdims=True) * (1.0 / width)
    inv = lax.rsqrt(jnp.sum(centred * centred, axis=-1, keepdims=True) * (1.0 / width) + epsilon)
    inv_o[...] = jnp.broadcast_to(inv, inv_o.shape)
    normal_o[...] = (centred * inv).astype(bf16)
    heads = narrow // HD
    for s in range(3):
        got = dot(normal_o[...], w[s]).astype(bf16)
        for h in range(heads):
            qkv_o[s * heads + h] = got[:, h * HD : (h + 1) * HD]
    for h in range(heads):
        scores = dot(qkv_o[h], qkv_o[heads + h], COLS) * SCALE
        top = jnp.max(scores, axis=-1, keepdims=True)
        e = jnp.exp(scores - top)
        probs = e / jnp.sum(e, axis=-1, keepdims=True)
        probs_o[h] = probs
        att_o[:, h * HD : (h + 1) * HD] = dot(probs.astype(bf16), qkv_o[2 * heads + h]).astype(bf16)
    xt_o[...] = normal_o[...].T


def attention_back(cot, w_out, qkv, probs, grads):
    narrow = w_out.shape[0]
    heads = narrow // HD
    att = dot(cot, w_out[...], COLS).astype(bf16)
    for h in range(heads):
        a = att[:, h * HD : (h + 1) * HD]
        p = probs[h]
        dp = dot(a, qkv[2 * heads + h], COLS)
        along = jnp.sum(p * dp, axis=-1, keepdims=True)
        ds = (p * (dp - along) * SCALE).astype(bf16)
        for s, got in enumerate(
            (
                dot(ds, qkv[heads + h]),
                dot(ds, qkv[h], ROWS),
                dot(p.astype(bf16), a, ROWS),
            )
        ):
            at = s * narrow + h * HD
            grads[:, at : at + HD] = got.astype(bf16)


def input_back(where, grads, w, own_o, oth_o):
    narrow = w.shape[2]
    part = dot(grads[:, :narrow], w[0], COLS)
    part = part + dot(grads[:, narrow : 2 * narrow], w[1], COLS)
    part = (part + dot(grads[:, 2 * narrow :], w[2], COLS)).astype(bf16)
    for c in range(2):

        @pl.when(where[1] == c)
        def _():
            for half, core in ((own_o, c), (oth_o, 1 - c)):
                for y in range(2):
                    at = (2 * y + core) * narrow
                    half[:, y * narrow : (y + 1) * narrow] = part[:, at : at + narrow]


def first_body(where, t0, ty, tc, tcy, w_out, qkv, probs, w, cot_o, own_o, oth_o, grads):
    put_pieces(where, cot_o, (t0, ty, tc, tcy))
    attention_back(cot_o[...], w_out, qkv, probs, grads)
    input_back(where, grads, w, own_o, oth_o)


def term_of(g, normal, inv):
    width = g.shape[1]
    n = normal[...].astype(f32)
    mean = jnp.sum(g, axis=-1, keepdims=True) * (1.0 / width)
    along = jnp.sum(g * n, axis=-1, keepdims=True) * (1.0 / width)
    return (g - mean - n * along) * inv[:, :1]


def middle_body(where, own, oth, normal, inv, w_out, qkv, probs, w, term_o, own_o, oth_o, spot, grads):
    put_halves(where, spot, own, oth)
    term_o[...] = term_of(spot[...], normal, inv)
    attention_back(term_o[...].astype(bf16), w_out, qkv, probs, grads)
    input_back(where, grads, w, own_o, oth_o)


def last_body(where, own, oth, normal, inv, w_out, qkv, probs, cot, term, mine, imp_o, grads_o, tt_o, spot):
    put_halves(where, spot, own, oth)
    spot[...] = term_of(spot[...], normal, inv) + term[...]
    narrow = mine.shape[1]
    for g in range(4):

        @pl.when(where[0] == g)
        def _():
            imp_o[...] = mine[...] + spot[:, g * narrow : (g + 1) * narrow]

    total = (spot[...] + cot[...].astype(f32)).astype(bf16)
    tt_o[...] = total.T
    attention_back(total, w_out, qkv, probs, grads_o)


def value_rows_body(other, where, xt, tt, grads, att, out):
    narrow = att.shape[1]
    rows = out.shape[1]
    yh = 1 - where[3] if other else where[3]
    for x in range(out.shape[0]):
        at = pl.ds(pl.multiple_of(x * 2 * rows + yh * rows, 16), rows)
        out[x, :, :narrow] = dot(xt[at, :], grads[:, 2 * narrow :]).astype(bf16)
        out[x, :, narrow:] = dot(tt[at, :], att[...]).astype(bf16)


def query_rows_body(steps, where, xt, grads, *outs):
    rows, cols = outs[0].shape
    for step, out in zip(steps, outs):
        at = pl.ds(pl.multiple_of(lax.rem(where[2] + step, 4) * rows, 16), rows)
        out[...] = dot(xt[at, :], grads[:, :cols]).astype(bf16)


def shift(n, by):
    return [(i, (i + by) % n) for i in range(n)]


def add(*parts):
    return sum(p.astype(f32) for p in parts).astype(bf16)


def mp_sum(own, oth):
    chip = add(own, lax.ppermute(oth, "c", SWAP))
    whole = add(chip, lax.ppermute(chip, "yl", SWAP))
    return whole, lax.ppermute(whole, "c", SWAP)


def pieces_of(mine):
    y = lax.ppermute(mine, "yl", SWAP)
    return mine, y, lax.ppermute(mine, "c", SWAP), lax.ppermute(y, "c", SWAP)


def shards(z_star, cotangent, w_qkv, w_out):
    images, tokens, narrow = z_star.shape
    width = 4 * narrow
    heads = narrow // HD
    nx, ny, nz = [lax.axis_size(a) for a in DP]
    x, yh = lax.axis_index("x"), lax.axis_index("yh")
    where = jnp.stack([lax.axis_index(MP), lax.axis_index("c"), x, yh]).astype(jnp.int32)

    z = pieces_of(z_star[0])
    t = pieces_of(cotangent[0].astype(bf16))
    wide = like((tokens, width), bf16)
    half = like((tokens, 2 * narrow), bf16)
    proj = 2 * tokens * width * narrow
    small = 2 * tokens * tokens * HD * heads
    spot = pltpu.VMEM((tokens, width), f32)
    g_like = like((tokens, 3 * narrow), bf16)
    grads_at = pltpu.VMEM((tokens, 3 * narrow), bf16)
    normal, xt, inv, qkv, probs, att = call(
        forward_body,
        (
            wide,
            like((width, tokens), bf16),
            like((tokens, 128), f32),
            like((3 * heads, tokens, HD), bf16),
            like((heads, tokens, tokens), f32),
            like((tokens, narrow), bf16),
        ),
        (where, *z, w_qkv),
        [pltpu.VMEM((tokens, width), bf16)],
        flops=3 * proj + 2 * small,
        name="forward",
    )
    cot, own, oth = call(
        first_body,
        (wide, half, half),
        (where, *t, w_out, qkv, probs, w_qkv),
        [grads_at],
        flops=4 * proj + 4 * small,
        name="first",
    )
    own, oth = mp_sum(own, oth)
    term, own, oth = call(
        middle_body,
        (like((tokens, width), f32), half, half),
        (where, own, oth, normal, inv, w_out, qkv, probs, w_qkv),
        [spot, grads_at],
        flops=4 * proj + 4 * small,
        name="middle",
    )
    own, oth = mp_sum(own, oth)
    implicit, grads, tt = call(
        last_body,
        (like((tokens, narrow), f32), g_like, like((width, tokens), bf16)),
        (where, own, oth, normal, inv, w_out, qkv, probs, cot, term, cotangent[0]),
        [spot],
        flops=proj + 4 * small,
        name="last",
    )

    rows = width // (nx * ny)
    v_like = like((nx, rows, 2 * narrow), bf16)
    q_like = like((ny * rows, 2 * narrow), bf16)
    (v_send,) = call(
        functools.partial(value_rows_body, True),
        (v_like,),
        (where, xt, tt, grads, att),
        flops=proj,
        name="value_send",
    )
    v_got = lax.ppermute(v_send, "yh", SWAP)
    q_send = call(
        functools.partial(query_rows_body, (2, 1, 3)),
        (q_like,) * 3,
        (where, xt, grads),
        flops=2 * proj * 3 // 4,
        name="query_send",
    )
    q_got = [lax.ppermute(s, "x", shift(nx, by)) for s, by in zip(q_send, (2, 1, 3))]
    (v_keep,) = call(
        functools.partial(value_rows_body, False),
        (v_like,),
        (where, xt, tt, grads, att),
        flops=proj,
        name="value_keep",
    )
    (q_keep,) = call(
        functools.partial(query_rows_body, (0,)),
        (q_like,),
        (where, xt, grads),
        flops=2 * proj // 4,
        name="query_keep",
    )
    take = lambda a, j, n: lax.dynamic_index_in_dim(a, lax.rem(j, n), 0, keepdims=False)
    v = add(v_keep, v_got)
    v_got = [lax.ppermute(take(v, x + by, nx), "x", shift(nx, by)) for by in (2, 1, 3)]
    q = add(q_keep, *q_got).reshape(ny, rows, 2 * narrow)
    q_got = lax.ppermute(take(q, yh + 1, ny), "yh", SWAP)
    q = add(take(q, yh, ny), q_got)
    v = add(take(v, x, nx), *v_got)
    both = jnp.concatenate([q, v], axis=1).reshape(nz, rows // nz, width)
    got = lax.all_to_all(both, "z", 0, 0, tiled=True)
    factor = 1.0 / math.sqrt(images * nx * ny * nz * tokens)
    got = jnp.sum(got.astype(f32), axis=0) * factor
    grad_qkv = jnp.stack([got[:, s * narrow : (s + 1) * narrow] for s in range(3)])
    return implicit[None], grad_qkv, got[:, 3 * narrow :].T


def solution(mesh):
    split = Mesh(mesh.devices.reshape(4, 2, 8, 2, 2), AXES)
    return jax.shard_map(
        shards,
        mesh=split,
        in_specs=(P(DP, None, MP), P(DP, None, MP), P(None, None, MP), P(MP, None)),
        out_specs=(P(DP, None, MP), P(None, DP, MP), P(MP, DP)),
        check_vma=False,
    )
```

profile of v0, /device:TPU:1, one launch (start us, length us, event | category | flops | bytes accessed | tf_op | source)
XLA Modules:
  0.0 138.9 jit_solution(16889346875815262757)
XLA Ops:
  0.6 2.2 %collective-permute-start.3 = (bf16[257,320]{1,0:T(8,128)(2,1)}, bf16[257,320]{1,0:T(8,128)(2,1)S(1)}, u32[]{:S(2)}, u32[]{:S(2)}) collective-permute-start(bf16[257,320]{1,0:T(8,128)(2,1)} %bitcast.40), channel_id=1, source_target_pairs={{0,2},{2,0},{1,3},{3,1},{4,6},{6,4},{5,7},{7,5},{8,10},{10,8},{9,1... | collective-permute-start | bytes 493448 | tf_op jit(solution)/shard_map/ppermute | solution.py:201
  4.0 3.1 %collective-permute-start.4 = (bf16[257,320]{1,0:T(8,128)(2,1)}, bf16[257,320]{1,0:T(8,128)(2,1)}, u32[]{:S(2)}, u32[]{:S(2)}) collective-permute-start(bf16[257,320]{1,0:T(8,128)(2,1)} %bitcast.41), channel_id=1, source_target_pairs={{0,1},{1,0},{2,3},{3,2},{4,5},{5,4},{6,7},{7,6},{8,9},{9,8},{10,11... | collective-permute-start | bytes 493448 | tf_op jit(solution)/shard_map/ppermute | solution.py:202
  7.1 4.3 %collective-permute-start.5 = (bf16[257,320]{1,0:T(8,128)(2,1)S(1)}, bf16[257,320]{1,0:T(8,128)(2,1)}, u32[]{:S(2)}, u32[]{:S(2)}) collective-permute-start(bf16[257,320]{1,0:T(8,128)(2,1)S(1)} %collective-permute-done.3.zy), channel_id=1, source_target_pairs={{0,1},{1,0},{2,3},{3,2},{4,5},{5,4},{6,7},{7,6},{8,9},{9,8},{10,11... | collective-permute-start | bytes 493448 | tf_op jit(solution)/shard_map/ppermute | solution.py:202
  11.4 4.0 %copy.11.w = bf16[3,1280,320]{2,1,0:T(8,128)(2,1)S(1)} copy(bf16[3,1280,320]{1,2,0:T(8,128)(2,1)} %param.6) | data formatting | bytes 4915200 | tf_op args[2]
  18.1 4.4 %forward.1 = (bf16[257,1280]{1,0:T(8,128)(2,1)S(1)}, bf16[1280,257]{1,0:T(8,128)(2,1)S(1)}, f32[257,128]{1,0:T(8,128)S(1)}, bf16[12,257,80]{2,1,0:T(8,128)(2,1)S...) custom-call(s32[4]{0:T(128)S(1)} %pad_add_fusion.where, bf16[257,320]{1,0:T(8,128)(2,1)S(1)} %bitcast.42, ...), custom_call_target="tpu_custom_call" | custom-call | flops 716145920 | bytes 6277664 | tf_op jit(solution)/shard_map/forward/pallas_call | solution.py:34
  22.5 6.3 %first.1 = (bf16[257,1280]{1,0:T(8,128)(2,1)S(1)}, bf16[257,640]{1,0:T(8,128)(2,1)S(1)}, bf16[257,640]{1,0:T(8,128)(2,1)S(1)}) custom-call(s32[4]{0:T(128)S(1)} %pad_add_fusion.where, bf16[257,320]{1,0:T(8,128)(2,1)S(1)} %bitcast.38, bf16[257,320]{1,0:T(8,128)(2,1)} %collective-permute-done.ty, bf16[257,320]{1,0:T(8,128)(2,1)} %collective-permute-done.1.tc, ...), custom_call_target="tpu_custom_call" | custom-call | flops 1011223040 | bytes 6800800 | tf_op jit(solution)/shard_map/first/pallas_call | solution.py:34
  29.2 1.6 %collective-permute-done.6 = bf16[257,640]{1,0:T(8,128)(2,1)S(1)} collective-permute-done((bf16[257,640]{1,0:T(8,128)(2,1)S(1)}, bf16[257,640]{1,0:T(8,128)(2,1)S(1)}, u32[]{:S(2)}, u32[]{:S(2)}) %collective-permute-start.6) | collective-permute-done | bytes 328992 | tf_op jit(solution)/shard_map/ppermute | solution.py:195
  31.4 9.0 %collective-permute-done.7 = bf16[257,640]{1,0:T(8,128)(2,1)S(1)} collective-permute-done((bf16[257,640]{1,0:T(8,128)(2,1)S(1)}, bf16[257,640]{1,0:T(8,128)(2,1)S(1)}, u32[]{:S(2)}, u32[]{:S(2)}) %collective-permute-start.7) | collective-permute-done | bytes 328992 | tf_op jit(solution)/shard_map/ppermute | solution.py:196
  41.5 1.3 collective-permute-done.8.oth
  42.8 6.0 %middle.1 = (f32[257,1280]{1,0:T(8,128)S(1)}, bf16[257,640]{1,0:T(8,128)(2,1)S(1)}, bf16[257,640]{1,0:T(8,128)(2,1)S(1)}) custom-call(s32[4]{0:T(128)S(1)} %pad_add_fusion.where, bf16[257,640]{1,0:T(8,128)(2,1)S(1)} %add_convert_fusion.4.own, bf16[257,640]{1,0:T(8,128)(2,1)S(1)} %collective-permute-done.8.oth, ...), custom_call_target="tpu_custom_call" | custom-call | flops 1011223040 | bytes 8248224 | tf_op jit(solution)/shard_map/middle/pallas_call | solution.py:34
  49.2 1.3 collective-permute-done.9
  51.1 8.7 %collective-permute-done.10 = bf16[257,640]{1,0:T(8,128)(2,1)S(1)} collective-permute-done((bf16[257,640]{1,0:T(8,128)(2,1)S(1)}, bf16[257,640]{1,0:T(8,128)(2,1)S(1)}, u32[]{:S(2)}, u32[]{:S(2)}) %collective-permute-start.10) | collective-permute-done | bytes 328992 | tf_op jit(solution)/shard_map/ppermute | solution.py:196
  59.9 1.3 collective-permute-start.11
  61.2 1.2 collective-permute-done.11.oth
  62.5 4.9 %last.1 = (f32[257,320]{1,0:T(8,128)S(1)}, bf16[257,960]{1,0:T(8,128)(2,1)S(1)}, bf16[1280,257]{1,0:T(8,128)(2,1)S(1)}) custom-call(s32[4]{0:T(128)S(1)} %pad_add_fusion.where, bf16[257,640]{1,0:T(8,128)(2,1)S(1)} %add_convert_fusion.2.own, bf16[257,640]{1,0:T(8,128)(2,1)S(1)} %collective-permute-done.11.oth, ...), custom_call_target="tpu_custom_call" | custom-call | flops 379619840 | bytes 7599904 | tf_op jit(solution)/shard_map/last/pallas_call | solution.py:34
  67.3 1.4 %value_send.1 = bf16[4,160,640]{2,1,0:T(8,128)(2,1)S(1)} custom-call(s32[4]{0:T(128)S(1)} %pad_add_fusion.where, bf16[1280,257]{1,0:T(8,128)(2,1)S(1)} %get-tuple-element.32.xt, bf16[1280,257]{1,0:T(8,128)(2,1)S(1)} %get-tuple-element.37.tt, bf16[257,960]{1,0:T(8,128)(2,1)S(1)} %get-tuple-element.33.grads, bf16[257,320]{1,0:T(8,128)(2,1)S(1)} %get-tuple-element.38.att), custom_call_target="tpu_custom_call" | custom-call | flops 210534400 | bytes 2792976 | tf_op jit(solution)/shard_map/value_send/pallas_call | solution.py:34
  68.7 1.9 %collective-permute-start.16 = (bf16[4,160,640]{2,1,0:T(8,128)(2,1)S(1)}, bf16[4,160,640]{2,1,0:T(8,128)(2,1)}, u32[]{:S(2)}, u32[]{:S(2)}) collective-permute-start(bf16[4,160,640]{2,1,0:T(8,128)(2,1)S(1)} %value_send.1), channel_id=1, source_target_pairs={{0,32},{32,0},{1,33},{33,1},{2,34},{34,2},{3,35},{35,3},{4,36},{36... | collective-permute-start | bytes 2457608 | tf_op jit(solution)/shard_map/ppermute | solution.py:274
  70.7 2.2 %query_send.1 = (bf16[320,640]{1,0:T(8,128)(2,1)}, bf16[320,640]{1,0:T(8,128)(2,1)}, bf16[320,640]{1,0:T(8,128)(2,1)}) custom-call(s32[4]{0:T(128)S(1)} %pad_add_fusion.where, bf16[1280,257]{1,0:T(8,128)(2,1)S(1)} %get-tuple-element.32.xt, bf16[257,960]{1,0:T(8,128)(2,1)S(1)} %get-tuple-element.33.grads), custom_call_target="tpu_custom_call" | custom-call | flops 315801600 | bytes 2380176 | tf_op jit(solution)/shard_map/query_send/pallas_call | solution.py:34
  72.8 2.7 %collective-permute-start.12 = (bf16[320,640]{1,0:T(8,128)(2,1)}, bf16[320,640]{1,0:T(8,128)(2,1)}, u32[]{:S(2)}, u32[]{:S(2)}) collective-permute-start(bf16[320,640]{1,0:T(8,128)(2,1)} %get-tuple-element.34), channel_id=1, source_target_pairs={{0,128},{64,192},{128,0},{192,64},{1,129},{65,193},{129,1},{193,65... | collective-permute-start | bytes 1228808 | tf_op jit(solution)/shard_map/ppermute | solution.py:282
  75.9 2.4 %collective-permute-start.14 = (bf16[320,640]{1,0:T(8,128)(2,1)}, bf16[320,640]{1,0:T(8,128)(2,1)}, u32[]{:S(2)}, u32[]{:S(2)}) collective-permute-start(bf16[320,640]{1,0:T(8,128)(2,1)} %get-tuple-element.36), channel_id=1, source_target_pairs={{0,192},{64,0},{128,64},{192,128},{1,193},{65,1},{129,65},{193,129... | collective-permute-start | bytes 1228808 | tf_op jit(solution)/shard_map/ppermute | solution.py:282
  80.4 1.4 %value_keep.1 = bf16[4,160,640]{2,1,0:T(8,128)(2,1)S(1)} custom-call(s32[4]{0:T(128)S(1)} %pad_add_fusion.where, bf16[1280,257]{1,0:T(8,128)(2,1)S(1)} %copy-done.1, bf16[1280,257]{1,0:T(8,128)(2,1)S(1)} %get-tuple-element.37.tt, bf16[257,960]{1,0:T(8,128)(2,1)S(1)} %get-tuple-element.33.grads, bf16[257,320]{1,0:T(8,128)(2,1)S(1)} %get-tuple-element.38.att), custom_call_target="tpu_custom_call" | custom-call | flops 210534400 | bytes 2792976 | tf_op jit(solution)/shard_map/value_keep/pallas_call | solution.py:34
  81.8 3.4 %collective-permute-done.12 = bf16[320,640]{1,0:T(8,128)(2,1)} collective-permute-done((bf16[320,640]{1,0:T(8,128)(2,1)}, bf16[320,640]{1,0:T(8,128)(2,1)}, u32[]{:S(2)}, u32[]{:S(2)}) %collective-permute-start.12) | collective-permute-done | bytes 409632 | tf_op jit(solution)/shard_map/ppermute | solution.py:282
  85.2 9.6 %collective-permute-done.13 = bf16[320,640]{1,0:T(8,128)(2,1)} collective-permute-done((bf16[320,640]{1,0:T(8,128)(2,1)}, bf16[320,640]{1,0:T(8,128)(2,1)}, u32[]{:S(2)}, u32[]{:S(2)}) %collective-permute-start.13) | collective-permute-done | bytes 409632 | tf_op jit(solution)/shard_map/ppermute | solution.py:282
  94.8 1.5 %add_convert_fusion.1 = bf16[320,640]{1,0:T(8,128)(2,1)S(1)} fusion(bf16[320,640]{1,0:T(8,128)(2,1)} %collective-permute-done.14, bf16[320,640]{1,0:T(8,128)(2,1)} %collective-permute-done.13, bf16[320,640]{1,0:T(8,128)(2,1)} %collective-permute-done.12, bf16[320,640]{1,0:T(8,128)(2,1)S(1)} %query_keep.1), kind=kLoop, calls=%fused_computation.2 | loop fusion | flops 1638400 | bytes 2048000 | tf_op jit(solution)/shard_map/convert_element_type | solution.py:191
  96.3 1.2 collective-permute-start.15
  97.6 1.4 add_convert_fusion
  99.0 1.3 collective-permute-start.17
  101.1 1.9 %collective-permute-start.19 = (bf16[160,640]{1,0:T(8,128)(2,1)S(1)}, bf16[160,640]{1,0:T(8,128)(2,1)S(1)}, u32[]{:S(2)}, u32[]{:S(2)}) collective-permute-start(bf16[160,640]{1,0:T(8,128)(2,1)S(1)} %get-tuple-element.46), channel_id=1, source_target_pairs={{0,192},{64,0},{128,64},{192,128},{1,193},{65,1},{129,65},{193,129... | collective-permute-start | bytes 614408 | tf_op jit(solution)/shard_map/ppermute | solution.py:299
  104.0 2.5 %collective-permute-done.17 = bf16[160,640]{1,0:T(8,128)(2,1)S(1)} collective-permute-done((bf16[160,640]{1,0:T(8,128)(2,1)S(1)}, bf16[160,640]{1,0:T(8,128)(2,1)S(1)}, u32[]{:S(2)}, u32[]{:S(2)}) %collective-permute-start.17) | collective-permute-done | bytes 204832 | tf_op jit(solution)/shard_map/ppermute | solution.py:299
  106.5 5.5 %collective-permute-done.18 = bf16[160,640]{1,0:T(8,128)(2,1)S(1)} collective-permute-done((bf16[160,640]{1,0:T(8,128)(2,1)S(1)}, bf16[160,640]{1,0:T(8,128)(2,1)S(1)}, u32[]{:S(2)}, u32[]{:S(2)}) %collective-permute-start.18) | collective-permute-done | bytes 204832 | tf_op jit(solution)/shard_map/ppermute | solution.py:299
  113.0 7.1 %all-to-all-start = ((bf16[8,20,1280]{2,1,0:T(8,128)(2,1)}), bf16[8,20,1280]{2,1,0:T(8,128)(2,1)S(1)}, u32[]{:S(2)}, u32[]{:S(2)}) async-start(bf16[8,20,1280]{2,1,0:T(8,128)(2,1)} %reshape.17), calls=%async_computation | async-start | bytes 983040 | tf_op jit(solution)/shard_map/all_to_all | solution.py:305
  121.3 16.1 %all-to-all-done = bf16[8,20,1280]{2,1,0:T(8,128)(2,1)S(1)} async-done(((bf16[8,20,1280]{2,1,0:T(8,128)(2,1)}), bf16[8,20,1280]{2,1,0:T(8,128)(2,1)S(1)}, u32[]{:S(2)}, u32[]{:S(2)}) %all-to-all-start) | async-done | bytes 409632 | tf_op jit(solution)/shard_map/all_to_all | solution.py:305
  (53 shorter events, 14.8 us)
Async XLA Ops:
  0.6 6.4 %collective-permute-start.3 = (bf16[257,320]{1,0:T(8,128)(2,1)}, bf16[257,320]{1,0:T(8,128)(2,1)S(1)}, u32[]{:S(2)}, u32[]{:S(2)}) collective-permute-start(bf16[257,320]{1,0:T(8,128)(2,1)} %bitcast.40), channel_id=1, source_target_pairs={{0,2},{2,0},{1,3},{3,1},{4,6},{6,4},{5,7},{7,5},{8,10},{10,8},{9,1... | collective-permute-start | bytes 493448 | tf_op jit(solution)/shard_map/ppermute | solution.py:201
  3.9 11.6 %collective-permute-start = (bf16[257,320]{1,0:T(8,128)(2,1)S(1)}, bf16[257,320]{1,0:T(8,128)(2,1)}, u32[]{:S(2)}, u32[]{:S(2)}) collective-permute-start(bf16[257,320]{1,0:T(8,128)(2,1)S(1)} %bitcast.36), channel_id=1, source_target_pairs={{0,2},{2,0},{1,3},{3,1},{4,6},{6,4},{5,7},{7,5},{8,10},{10,8},{9,1... | collective-permute-start | bytes 493448 | tf_op jit(solution)/shard_map/ppermute | solution.py:201
  4.0 12.2 %collective-permute-start.4 = (bf16[257,320]{1,0:T(8,128)(2,1)}, bf16[257,320]{1,0:T(8,128)(2,1)}, u32[]{:S(2)}, u32[]{:S(2)}) collective-permute-start(bf16[257,320]{1,0:T(8,128)(2,1)} %bitcast.41), channel_id=1, source_target_pairs={{0,1},{1,0},{2,3},{3,2},{4,5},{5,4},{6,7},{7,6},{8,9},{9,8},{10,11... | collective-permute-start | bytes 493448 | tf_op jit(solution)/shard_map/ppermute | solution.py:202
  7.1 8.4 %copy-start.4 = (bf16[257,320]{1,0:T(8,128)(2,1)}, bf16[257,320]{1,0:T(8,128)(2,1)S(1)}, u32[]{:S(2)}) copy-start(bf16[257,320]{1,0:T(8,128)(2,1)S(1)} %collective-permute-done.3.zy) | copy-start | bytes 493444
  7.1 9.1 %collective-permute-start.5 = (bf16[257,320]{1,0:T(8,128)(2,1)S(1)}, bf16[257,320]{1,0:T(8,128)(2,1)}, u32[]{:S(2)}, u32[]{:S(2)}) collective-permute-start(bf16[257,320]{1,0:T(8,128)(2,1)S(1)} %collective-permute-done.3.zy), channel_id=1, source_target_pairs={{0,1},{1,0},{2,3},{3,2},{4,5},{5,4},{6,7},{7,6},{8,9},{9,8},{10,11... | collective-permute-start | bytes 493448 | tf_op jit(solution)/shard_map/ppermute | solution.py:202
  11.4 11.1 %collective-permute-start.1 = (bf16[257,320]{1,0:T(8,128)(2,1)S(1)}, bf16[257,320]{1,0:T(8,128)(2,1)}, u32[]{:S(2)}, u32[]{:S(2)}) collective-permute-start(bf16[257,320]{1,0:T(8,128)(2,1)S(1)} %bitcast.37), channel_id=1, source_target_pairs={{0,1},{1,0},{2,3},{3,2},{4,5},{5,4},{6,7},{7,6},{8,9},{9,8},{10,11... | collective-permute-start | bytes 493448 | tf_op jit(solution)/shard_map/ppermute | solution.py:202
  15.5 7.0 %collective-permute-start.2 = (bf16[257,320]{1,0:T(8,128)(2,1)}, bf16[257,320]{1,0:T(8,128)(2,1)S(1)}, u32[]{:S(2)}, u32[]{:S(2)}) collective-permute-start(bf16[257,320]{1,0:T(8,128)(2,1)} %collective-permute-done.ty), channel_id=1, source_target_pairs={{0,1},{1,0},{2,3},{3,2},{4,5},{5,4},{6,7},{7,6},{8,9},{9,8},{10,11... | collective-permute-start | bytes 493448 | tf_op jit(solution)/shard_map/ppermute | solution.py:202
  16.1 6.4 %copy-start.2 = (bf16[320,1280]{1,0:T(8,128)(2,1)S(1)}, bf16[320,1280]{1,0:T(8,128)(2,1)}, u32[]{:S(2)}) copy-start(bf16[320,1280]{1,0:T(8,128)(2,1)} %w_out.5) | copy-start | bytes 2457604
  16.2 1.0 copy-start.3
  17.2 0.9 copy-start.5
  22.5 48.2 %copy-start = (bf16[1280,257]{1,0:T(8,128)(2,1)}, bf16[1280,257]{1,0:T(8,128)(2,1)S(1)}, u32[]{:S(2)}) copy-start(bf16[1280,257]{1,0:T(8,128)(2,1)S(1)} %get-tuple-element.32.xt) | copy-start | bytes 1973764
  28.9 1.9 %collective-permute-start.6 = (bf16[257,640]{1,0:T(8,128)(2,1)S(1)}, bf16[257,640]{1,0:T(8,128)(2,1)S(1)}, u32[]{:S(2)}, u32[]{:S(2)}) collective-permute-start(bf16[257,640]{1,0:T(8,128)(2,1)S(1)} %get-tuple-element.24), channel_id=1, source_target_pairs={{0,1},{1,0},{2,3},{3,2},{4,5},{5,4},{6,7},{7,6},{8,9},{9,8},{10,11... | collective-permute-start | bytes 986888 | tf_op jit(solution)/shard_map/ppermute | solution.py:195
  30.9 9.4 %collective-permute-start.7 = (bf16[257,640]{1,0:T(8,128)(2,1)S(1)}, bf16[257,640]{1,0:T(8,128)(2,1)S(1)}, u32[]{:S(2)}, u32[]{:S(2)}) collective-permute-start(bf16[257,640]{1,0:T(8,128)(2,1)S(1)} %add_convert_fusion.5), channel_id=1, source_target_pairs={{0,2},{2,0},{1,3},{3,1},{4,6},{6,4},{5,7},{7,5},{8,10},{10,8},{9,1... | collective-permute-start | bytes 986888 | tf_op jit(solution)/shard_map/ppermute | solution.py:196
  40.4 2.4 %collective-permute-start.8 = (bf16[257,640]{1,0:T(8,128)(2,1)S(1)}, bf16[257,640]{1,0:T(8,128)(2,1)S(1)}, u32[]{:S(2)}, u32[]{:S(2)}) collective-permute-start(bf16[257,640]{1,0:T(8,128)(2,1)S(1)} %add_convert_fusion.4.own), channel_id=1, source_target_pairs={{0,1},{1,0},{2,3},{3,2},{4,5},{5,4},{6,7},{7,6},{8,9},{9,8},{10,11... | collective-permute-start | bytes 986888 | tf_op jit(solution)/shard_map/ppermute | solution.py:197
  48.7 12.4 %copy-start.6 = (f32[1,257,320]{2,0,1:T(1,128)S(1)}, f32[1,257,320]{2,0,1:T(1,128)}, u32[]{:S(2)}) copy-start(f32[1,257,320]{2,0,1:T(1,128)} %param.5) | copy-start | bytes 986884
  48.8 1.7 %collective-permute-start.9 = (bf16[257,640]{1,0:T(8,128)(2,1)S(1)}, bf16[257,640]{1,0:T(8,128)(2,1)S(1)}, u32[]{:S(2)}, u32[]{:S(2)}) collective-permute-start(bf16[257,640]{1,0:T(8,128)(2,1)S(1)} %get-tuple-element.28), channel_id=1, source_target_pairs={{0,1},{1,0},{2,3},{3,2},{4,5},{5,4},{6,7},{7,6},{8,9},{9,8},{10,11... | collective-permute-start | bytes 986888 | tf_op jit(solution)/shard_map/ppermute | solution.py:195
  50.6 9.2 %collective-permute-start.10 = (bf16[257,640]{1,0:T(8,128)(2,1)S(1)}, bf16[257,640]{1,0:T(8,128)(2,1)S(1)}, u32[]{:S(2)}, u32[]{:S(2)}) collective-permute-start(bf16[257,640]{1,0:T(8,128)(2,1)S(1)} %add_convert_fusion.3), channel_id=1, source_target_pairs={{0,2},{2,0},{1,3},{3,1},{4,6},{6,4},{5,7},{7,5},{8,10},{10,8},{9,1... | collective-permute-start | bytes 986888 | tf_op jit(solution)/shard_map/ppermute | solution.py:196
  59.9 2.6 %collective-permute-start.11 = (bf16[257,640]{1,0:T(8,128)(2,1)S(1)}, bf16[257,640]{1,0:T(8,128)(2,1)S(1)}, u32[]{:S(2)}, u32[]{:S(2)}) collective-permute-start(bf16[257,640]{1,0:T(8,128)(2,1)S(1)} %add_convert_fusion.2.own), channel_id=1, source_target_pairs={{0,1},{1,0},{2,3},{3,2},{4,5},{5,4},{6,7},{7,6},{8,9},{9,8},{10,11... | collective-permute-start | bytes 986888 | tf_op jit(solution)/shard_map/ppermute | solution.py:197
  68.7 28.8 %collective-permute-start.16 = (bf16[4,160,640]{2,1,0:T(8,128)(2,1)S(1)}, bf16[4,160,640]{2,1,0:T(8,128)(2,1)}, u32[]{:S(2)}, u32[]{:S(2)}) collective-permute-start(bf16[4,160,640]{2,1,0:T(8,128)(2,1)S(1)} %value_send.1), channel_id=1, source_target_pairs={{0,32},{32,0},{1,33},{33,1},{2,34},{34,2},{3,35},{35,3},{4,36},{36... | collective-permute-start | bytes 2457608 | tf_op jit(solution)/shard_map/ppermute | solution.py:274
  72.8 12.4 %collective-permute-start.12 = (bf16[320,640]{1,0:T(8,128)(2,1)}, bf16[320,640]{1,0:T(8,128)(2,1)}, u32[]{:S(2)}, u32[]{:S(2)}) collective-permute-start(bf16[320,640]{1,0:T(8,128)(2,1)} %get-tuple-element.34), channel_id=1, source_target_pairs={{0,128},{64,192},{128,0},{192,64},{1,129},{65,193},{129,1},{193,65... | collective-permute-start | bytes 1228808 | tf_op jit(solution)/shard_map/ppermute | solution.py:282
  75.6 19.3 %collective-permute-start.13 = (bf16[320,640]{1,0:T(8,128)(2,1)}, bf16[320,640]{1,0:T(8,128)(2,1)}, u32[]{:S(2)}, u32[]{:S(2)}) collective-permute-start(bf16[320,640]{1,0:T(8,128)(2,1)} %get-tuple-element.35), channel_id=1, source_target_pairs={{0,64},{64,128},{128,192},{192,0},{1,65},{65,129},{129,193},{193,1... | collective-permute-start | bytes 1228808 | tf_op jit(solution)/shard_map/ppermute | solution.py:282
  75.9 18.9 %collective-permute-start.14 = (bf16[320,640]{1,0:T(8,128)(2,1)}, bf16[320,640]{1,0:T(8,128)(2,1)}, u32[]{:S(2)}, u32[]{:S(2)}) collective-permute-start(bf16[320,640]{1,0:T(8,128)(2,1)} %get-tuple-element.36), channel_id=1, source_target_pairs={{0,192},{64,0},{128,64},{192,128},{1,193},{65,1},{129,65},{193,129... | collective-permute-start | bytes 1228808 | tf_op jit(solution)/shard_map/ppermute | solution.py:282
  78.3 1.2 copy-start.1
  96.3 7.6 %collective-permute-start.15 = (bf16[160,640]{1,0:T(8,128)(2,1)S(1)}, bf16[160,640]{1,0:T(8,128)(2,1)S(1)}, u32[]{:S(2)}, u32[]{:S(2)}) collective-permute-start(bf16[160,640]{1,0:T(8,128)(2,1)S(1)} %dynamic-slice_bitcast_fusion.3), channel_id=1, source_target_pairs={{0,32},{32,0},{1,33},{33,1},{2,34},{34,2},{3,35},{35,3},{4,36},{36... | collective-permute-start | bytes 614408 | tf_op jit(solution)/shard_map/ppermute | solution.py:301
  99.0 7.5 %collective-permute-start.17 = (bf16[160,640]{1,0:T(8,128)(2,1)S(1)}, bf16[160,640]{1,0:T(8,128)(2,1)S(1)}, u32[]{:S(2)}, u32[]{:S(2)}) collective-permute-start(bf16[160,640]{1,0:T(8,128)(2,1)S(1)} %get-tuple-element.45), channel_id=1, source_target_pairs={{0,128},{64,192},{128,0},{192,64},{1,129},{65,193},{129,1},{193,65... | collective-permute-start | bytes 614408 | tf_op jit(solution)/shard_map/ppermute | solution.py:299
  100.3 11.6 %collective-permute-start.18 = (bf16[160,640]{1,0:T(8,128)(2,1)S(1)}, bf16[160,640]{1,0:T(8,128)(2,1)S(1)}, u32[]{:S(2)}, u32[]{:S(2)}) collective-permute-start(bf16[160,640]{1,0:T(8,128)(2,1)S(1)} %get-tuple-element.47), channel_id=1, source_target_pairs={{0,64},{64,128},{128,192},{192,0},{1,65},{65,129},{129,193},{193,1... | collective-permute-start | bytes 614408 | tf_op jit(solution)/shard_map/ppermute | solution.py:299
  101.1 10.9 %collective-permute-start.19 = (bf16[160,640]{1,0:T(8,128)(2,1)S(1)}, bf16[160,640]{1,0:T(8,128)(2,1)S(1)}, u32[]{:S(2)}, u32[]{:S(2)}) collective-permute-start(bf16[160,640]{1,0:T(8,128)(2,1)S(1)} %get-tuple-element.46), channel_id=1, source_target_pairs={{0,192},{64,0},{128,64},{192,128},{1,193},{65,1},{129,65},{193,129... | collective-permute-start | bytes 614408 | tf_op jit(solution)/shard_map/ppermute | solution.py:299
  113.0 24.4 %all-to-all-start = ((bf16[8,20,1280]{2,1,0:T(8,128)(2,1)}), bf16[8,20,1280]{2,1,0:T(8,128)(2,1)S(1)}, u32[]{:S(2)}, u32[]{:S(2)}) async-start(bf16[8,20,1280]{2,1,0:T(8,128)(2,1)} %reshape.17), calls=%async_computation | async-start | bytes 983040 | tf_op jit(solution)/shard_map/all_to_all | solution.py:305
where the time goes:
time: 139 us
  waiting for transfers between devices  61.1 us (44%)
  starting transfers between devices  34.1 us (25%)
  Pallas kernels  27.5 us (20%)
  local copies, waits for them, and re-layouts  11.1 us (8%)
  other arithmetic  4.22 us (3%)
    pallas_call x8, Pallas kernels, call(): pl.pallas_call(body, out_shape=outs, in_specs=[smem] + [vmem] * (len(ins)...  27.5 us
    ppermute x2, waiting for transfers between devices, mp_sum(): whole = add(chip, lax.ppermute(chip, 'yl', SWAP))  17.7 us
    all_to_all x1, waiting for transfers between devices, shards(): got = lax.all_to_all(both, 'z', 0, 0, tiled=True)  16.1 us
    ppermute x3, waiting for transfers between devices, shards(): lax.ppermute(s, 'x', shift(nx, by))  13 us
    unnamed x18, local copies, waits for them, and re-layouts  9.38 us
    ppermute x4, starting transfers between devices, pieces_of(): return (mine, y, lax.ppermute(mine, 'c', SWAP), lax.ppermute(y, 'c', SWAP))  8.02 us
    ppermute x3, waiting for transfers between devices, shards(): lax.ppermute(take(v, x + by, nx), 'x', shift(nx, by))  7.97 us
    all_to_all x1, starting transfers between devices, shards(): got = lax.all_to_all(both, 'z', 0, 0, tiled=True)  7.13 us
  transfers between devices with their start and end apart: 21, of which 12 were waited for; matrix products, arithmetic and copies ran while one was open for 7% of the time, Pallas kernels for 6%

commit v1 on v0

--- a/solution.py
+++ b/solution.py
@@ -9,6 +9,7 @@
 from jax.sharding import Mesh
 from jax.sharding import PartitionSpec as P
 
+
 HD = 80
 AXES = ("x", "yh", "z", "yl", "c")
 DP = ("x", "yh", "z")
@@ -27,7 +28,7 @@
     return lax.dot_general(a, b, dims, preferred_element_type=f32)
 
 
-def call(body, outs, ins, scratch=(), flops=0, name=None):
+def call(body, outs, ins, scratch=(), flops=0):
     vmem = pl.BlockSpec(memory_space=pltpu.VMEM)
     smem = pl.BlockSpec(memory_space=pltpu.SMEM)
     size = sum(math.prod(o.shape) * o.dtype.itemsize for o in list(outs) + list(ins))
@@ -39,7 +40,6 @@
         scratch_shapes=list(scratch),
         compiler_params=pltpu.CompilerParams(vmem_limit_bytes=28 * 2**20),
         cost_estimate=pl.CostEstimate(flops=flops, bytes_accessed=size, transcendentals=0),
-        name=name,
     )(*ins)
 
 
@@ -73,7 +73,7 @@
 def forward_body(where, z0, zy, zc, zcy, w, normal_o, xt_o, inv_o, qkv_o, probs_o, att_o, zs):
     put_pieces(where, zs, (z0, zy, zc, zcy))
     width = zs.shape[1]
-    narrow = w.shape[2]
+    narrow = w.shape[1]
     values = zs[...].astype(f32)
     centred = values - jnp.sum(values, axis=-1, keepdims=True) * (1.0 / width)
     inv = lax.rsqrt(jnp.sum(centred * centred, axis=-1, keepdims=True) * (1.0 / width) + epsilon)
@@ -81,7 +81,7 @@
     normal_o[...] = (centred * inv).astype(bf16)
     heads = narrow // HD
     for s in range(3):
-        got = dot(normal_o[...], w[s]).astype(bf16)
+        got = dot(normal_o[...], w[s], COLS).astype(bf16)
         for h in range(heads):
             qkv_o[s * heads + h] = got[:, h * HD : (h + 1) * HD]
     for h in range(heads):
@@ -116,10 +116,10 @@
 
 
 def input_back(where, grads, w, own_o, oth_o):
-    narrow = w.shape[2]
-    part = dot(grads[:, :narrow], w[0], COLS)
-    part = part + dot(grads[:, narrow : 2 * narrow], w[1], COLS)
-    part = (part + dot(grads[:, 2 * narrow :], w[2], COLS)).astype(bf16)
+    narrow = w.shape[1]
+    part = dot(grads[:, :narrow], w[0])
+    part = part + dot(grads[:, narrow : 2 * narrow], w[1])
+    part = (part + dot(grads[:, 2 * narrow :], w[2])).astype(bf16)
     for c in range(2):
 
         @pl.when(where[1] == c)
@@ -151,7 +151,7 @@
     input_back(where, grads, w, own_o, oth_o)
 
 
-def last_body(where, own, oth, normal, inv, w_out, qkv, probs, cot, term, mine, imp_o, grads_o, tt_o, spot):
+def total_body(where, own, oth, normal, inv, cot, term, mine, att, imp_o, total_o, rows_o, spot):
     put_halves(where, spot, own, oth)
     spot[...] = term_of(spot[...], normal, inv) + term[...]
     narrow = mine.shape[1]
@@ -162,18 +162,26 @@
             imp_o[...] = mine[...] + spot[:, g * narrow : (g + 1) * narrow]
 
     total = (spot[...] + cot[...].astype(f32)).astype(bf16)
-    tt_o[...] = total.T
-    attention_back(total, w_out, qkv, probs, grads_o)
-
-
-def value_rows_body(other, where, xt, tt, grads, att, out):
-    narrow = att.shape[1]
+    total_o[...] = total
+    got = dot(total, att[...], ROWS)
+    nz, _, _ = rows_o.shape
+    each = total.shape[1] // (nz * 8)
+    for d in range(8):
+        for z in range(nz):
+            at = (d * nz + z) * each
+            rows_o[z, d * each : (d + 1) * each, :] = got[at : at + each, :].astype(bf16)
+
+
+def last_body(where, total, w_out, qkv, probs, grads_o):
+    attention_back(total[...], w_out, qkv, probs, grads_o)
+
+
+def value_rows_body(other, first, where, xt, grads, out):
     rows = out.shape[1]
     yh = 1 - where[3] if other else where[3]
     for x in range(out.shape[0]):
         at = pl.ds(pl.multiple_of(x * 2 * rows + yh * rows, 16), rows)
-        out[x, :, :narrow] = dot(xt[at, :], grads[:, 2 * narrow :]).astype(bf16)
-        out[x, :, narrow:] = dot(tt[at, :], att[...]).astype(bf16)
+        out[x] = dot(xt[at, :], grads[:, first:]).astype(bf16)
 
 
 def query_rows_body(steps, where, xt, grads, *outs):
@@ -210,6 +218,7 @@
     x, yh = lax.axis_index("x"), lax.axis_index("yh")
     where = jnp.stack([lax.axis_index(MP), lax.axis_index("c"), x, yh]).astype(jnp.int32)
 
+    w_t = jnp.swapaxes(w_qkv, 1, 2)
     z = pieces_of(z_star[0])
     t = pieces_of(cotangent[0].astype(bf16))
     wide = like((tokens, width), bf16)
@@ -229,88 +238,89 @@
             like((heads, tokens, tokens), f32),
             like((tokens, narrow), bf16),
         ),
-        (where, *z, w_qkv),
+        (where, *z, w_t),
         [pltpu.VMEM((tokens, width), bf16)],
         flops=3 * proj + 2 * small,
-        name="forward",
     )
     cot, own, oth = call(
         first_body,
         (wide, half, half),
-        (where, *t, w_out, qkv, probs, w_qkv),
+        (where, *t, w_out, qkv, probs, w_t),
         [grads_at],
         flops=4 * proj + 4 * small,
-        name="first",
     )
     own, oth = mp_sum(own, oth)
     term, own, oth = call(
         middle_body,
         (like((tokens, width), f32), half, half),
-        (where, own, oth, normal, inv, w_out, qkv, probs, w_qkv),
+        (where, own, oth, normal, inv, w_out, qkv, probs, w_t),
         [spot, grads_at],
         flops=4 * proj + 4 * small,
-        name="middle",
     )
     own, oth = mp_sum(own, oth)
-    implicit, grads, tt = call(
-        last_body,
-        (like((tokens, narrow), f32), g_like, like((width, tokens), bf16)),
-        (where, own, oth, normal, inv, w_out, qkv, probs, cot, term, cotangent[0]),
+    rows = width // (nx * ny)
+    implicit, total, o_rows = call(
+        total_body,
+        (like((tokens, narrow), f32), wide, like((nz, rows, narrow), bf16)),
+        (where, own, oth, normal, inv, cot, term, cotangent[0], att),
         [spot],
-        flops=proj + 4 * small,
-        name="last",
-    )
-
-    rows = width // (nx * ny)
-    v_like = like((nx, rows, 2 * narrow), bf16)
-    q_like = like((ny * rows, 2 * narrow), bf16)
+        flops=proj,
+    )
+    o_got = lax.all_to_all(o_rows, "z", 0, 0, tiled=True)
+    (grads,) = call(last_body, (g_like,), (where, total, w_out, qkv, probs), flops=proj + 4 * small)
+
+    first = 512
+    v_like = like((nx, rows, 3 * narrow - first), bf16)
+    q_like = like((ny * rows, first), bf16)
+    v_flops = 2 * tokens * (width // 2) * (3 * narrow - first)
+    q_flops = 2 * tokens * (width // 4) * first
     (v_send,) = call(
-        functools.partial(value_rows_body, True),
+        functools.partial(value_rows_body, True, first),
         (v_like,),
-        (where, xt, tt, grads, att),
-        flops=proj,
-        name="value_send",
+        (where, xt, grads),
+        flops=v_flops,
     )
     v_got = lax.ppermute(v_send, "yh", SWAP)
     q_send = call(
         functools.partial(query_rows_body, (2, 1, 3)),
         (q_like,) * 3,
         (where, xt, grads),
-        flops=2 * proj * 3 // 4,
-        name="query_send",
+        flops=3 * q_flops,
     )
     q_got = [lax.ppermute(s, "x", shift(nx, by)) for s, by in zip(q_send, (2, 1, 3))]
     (v_keep,) = call(
-        functools.partial(value_rows_body, False),
+        functools.partial(value_rows_body, False, first),
         (v_like,),
-        (where, xt, tt, grads, att),
-        flops=proj,
-        name="value_keep",
+        (where, xt, grads),
+        flops=v_flops,
     )
     (q_keep,) = call(
-        functools.partial(query_rows_body, (0,)),
-        (q_like,),
-        (where, xt, grads),
-        flops=2 * proj // 4,
-        name="query_keep",
+        functools.partial(query_rows_body, (0,)), (q_like,), (where, xt, grads), flops=q_flops
     )
     take = lambda a, j, n: lax.dynamic_index_in_dim(a, lax.rem(j, n), 0, keepdims=False)
+    v_got, q_got, o_got = lax.optimization_barrier((v_got, q_got, o_got))
     v = add(v_keep, v_got)
     v_got = [lax.ppermute(take(v, x + by, nx), "x", shift(nx, by)) for by in (2, 1, 3)]
-    q = add(q_keep, *q_got).reshape(ny, rows, 2 * narrow)
+    q = add(q_keep, *q_got).reshape(ny, rows, first)
     q_got = lax.ppermute(take(q, yh + 1, ny), "yh", SWAP)
+    o = jnp.sum(o_got.astype(f32), axis=0).astype(bf16).reshape(nx * ny, rows // nz, narrow)
+    o = lax.all_to_all(o, ("x", "yh"), 0, 0, tiled=True)
+    q_got, v_got, o = lax.optimization_barrier((q_got, v_got, o))
     q = add(take(q, yh, ny), q_got)
     v = add(take(v, x, nx), *v_got)
-    both = jnp.concatenate([q, v], axis=1).reshape(nz, rows // nz, width)
+    both = jnp.concatenate([q, v], axis=1).reshape(nz, rows // nz, 3 * narrow)
     got = lax.all_to_all(both, "z", 0, 0, tiled=True)
     factor = 1.0 / math.sqrt(images * nx * ny * nz * tokens)
     got = jnp.sum(got.astype(f32), axis=0) * factor
+    o = jnp.sum(o.astype(f32), axis=0) * factor
     grad_qkv = jnp.stack([got[:, s * narrow : (s + 1) * narrow] for s in range(3)])
-    return implicit[None], grad_qkv, got[:, 3 * narrow :].T
+    return implicit[None], grad_qkv, o.T
 
 
 def solution(mesh):
     split = Mesh(mesh.devices.reshape(4, 2, 8, 2, 2), AXES)
+
+
     return jax.shard_map(
         shards,
         mesh=split,

time: 139 us -> 154 us (1.11); the launches traced: 139 us -> 151 us
  starting transfers between devices: 34.1 us -> 49.6 us
  waiting for transfers between devices: 61.1 us -> 48.8 us
  local copies, waits for them, and re-layouts: 11.1 us -> 19.2 us
  other arithmetic: 4.22 us -> 5.95 us
    all_to_all x0 -> x2, starting transfers between devices: none -> 12.3 us  [the longest x1 8.29 us: shards(): o_got = lax.all_to_all(o_rows, 'z', 0, 0, tiled=True)]
    unnamed x18 -> x47, local copies, waits for them, and re-layouts: 9.38 us -> 17.5 us
    ppermute x3, waiting for transfers between devices: 7.97 us -> 0.01 us  [shards(): lax.ppermute(take(v, x + by, nx), 'x', shift(nx, by))]
    all_to_all x0 -> x2, waiting for transfers between devices: none -> 6.86 us  [the longest x1 6.85 us: shards(): o = lax.all_to_all(o, ('x', 'yh'), 0, 0, tiled=True)]
    all_to_all x1, waiting for transfers between devices: 16.1 us -> 9.44 us  [shards(): got = lax.all_to_all(both, 'z', 0, 0, tiled=True)]
    ppermute x3, waiting for transfers between devices: 13 us -> 11.1 us  [shards(): lax.ppermute(s, 'x', shift(nx, by))]
    ppermute x2, waiting for transfers between devices: 17.7 us -> 15.9 us  [mp_sum(): whole = add(chip, lax.ppermute(chip, 'yl', SWAP))]
    ppermute x2, starting transfers between devices: 0.95 us -> 2.71 us  [mp_sum(): whole = add(chip, lax.ppermute(chip, 'yl', SWAP))]
  transfers between devices with their start and end apart: 21 -> 23, of which waited for: 12 -> 10; matrix products, arithmetic and copies ran while one was open for 7% -> 4% of each run, Pallas kernels for 6% -> 8%
where the time goes in v1:
time: 154 us; the launch traced here: 151 us
  starting transfers between devices  49.6 us (32%)
  waiting for transfers between devices  48.8 us (32%)
  Pallas kernels  26.2 us (17%)
  local copies, waits for them, and re-layouts  19.2 us (12%)
  other arithmetic  5.95 us (4%)
    pallas_call x9, Pallas kernels, call(): pl.pallas_call(body, out_shape=outs, in_specs=[smem] + [vmem] * (len(ins)...  26.2 us
    unnamed x47, local copies, waits for them, and re-layouts  17.5 us
    ppermute x2, waiting for transfers between devices, mp_sum(): whole = add(chip, lax.ppermute(chip, 'yl', SWAP))  15.9 us
    ppermute x3, waiting for transfers between devices, shards(): lax.ppermute(s, 'x', shift(nx, by))  11.1 us
    all_to_all x1, waiting for transfers between devices, shards(): got = lax.all_to_all(both, 'z', 0, 0, tiled=True)  9.44 us
    ppermute x4, starting transfers between devices, pieces_of(): return (mine, y, lax.ppermute(mine, 'c', SWAP), lax.ppermute(y, 'c', SWAP))  8.92 us
    all_to_all x1, starting transfers between devices, shards(): o_got = lax.all_to_all(o_rows, 'z', 0, 0, tiled=True)  8.29 us
    all_to_all x1, waiting for transfers between devices, shards(): o = lax.all_to_all(o, ('x', 'yh'), 0, 0, tiled=True)  6.85 us
  transfers between devices with their start and end apart: 23, of which 10 were waited for; matrix products, arithmetic and copies ran while one was open for 4% of the time, Pallas kernels for 8%

profile of v1, /device:TPU:1, one launch (start us, length us, event | category | flops | bytes accessed | tf_op | source)
XLA Modules:
  0.0 150.7 jit_solution(4600497619983534645)
XLA Ops:
  0.6 2.2 %collective-permute-start.3 = (bf16[257,320]{1,0:T(8,128)(2,1)}, bf16[257,320]{1,0:T(8,128)(2,1)S(1)}, u32[]{:S(2)}, u32[]{:S(2)}) collective-permute-start(bf16[257,320]{1,0:T(8,128)(2,1)} %bitcast.44), channel_id=1, source_target_pairs={{0,2},{2,0},{1,3},{3,1},{4,6},{6,4},{5,7},{7,5},{8,10},{10,8},{9,1... | collective-permute-start | bytes 493448 | tf_op jit(solution)/shard_map/ppermute | solution.py:209
  4.0 3.1 %collective-permute-start.4 = (bf16[257,320]{1,0:T(8,128)(2,1)}, bf16[257,320]{1,0:T(8,128)(2,1)S(1)}, u32[]{:S(2)}, u32[]{:S(2)}) collective-permute-start(bf16[257,320]{1,0:T(8,128)(2,1)} %bitcast.45), channel_id=1, source_target_pairs={{0,1},{1,0},{2,3},{3,2},{4,5},{5,4},{6,7},{7,6},{8,9},{9,8},{10,11... | collective-permute-start | bytes 493448 | tf_op jit(solution)/shard_map/ppermute | solution.py:210
  7.1 4.3 %collective-permute-start.5 = (bf16[257,320]{1,0:T(8,128)(2,1)S(1)}, bf16[257,320]{1,0:T(8,128)(2,1)S(1)}, u32[]{:S(2)}, u32[]{:S(2)}) collective-permute-start(bf16[257,320]{1,0:T(8,128)(2,1)S(1)} %collective-permute-done.3.zy), channel_id=1, source_target_pairs={{0,1},{1,0},{2,3},{3,2},{4,5},{5,4},{6,7},{7,6},{8,9},{9,8},{10,11... | collective-permute-start | bytes 493448 | tf_op jit(solution)/shard_map/ppermute | solution.py:210
  12.1 1.5 collective-permute-start.2
  15.0 1.7 %copy-done = bf16[3,1280,320]{1,2,0:T(8,128)(2,1)S(1)} copy-done((bf16[3,1280,320]{1,2,0:T(8,128)(2,1)S(1)}, bf16[3,1280,320]{1,2,0:T(8,128)(2,1)}, u32[]{:S(2)}) %copy-start) | copy-done | bytes 2457624
  20.4 3.8 %shard_map.67 = (bf16[257,1280]{1,0:T(8,128)(2,1)S(1)}, bf16[1280,257]{1,0:T(8,128)(2,1)S(1)}, f32[257,128]{1,0:T(8,128)S(1)}, bf16[12,257,80]{2,1,0:T(8,128)(2,...) custom-call(s32[4]{0:T(128)S(1)} %pad_add_fusion.where, bf16[257,320]{1,0:T(8,128)(2,1)S(1)} %bitcast.46, ...), custom_call_target="tpu_custom_call" | custom-call | flops 716145920 | bytes 6277664 | tf_op jit(solution)/shard_map/pallas_call | solution.py:35
  24.3 1.4 copy-done.2
  25.7 5.9 %shard_map.68 = (bf16[257,1280]{1,0:T(8,128)(2,1)S(1)}, bf16[257,640]{1,0:T(8,128)(2,1)S(1)}, bf16[257,640]{1,0:T(8,128)(2,1)S(1)}) custom-call(s32[4]{0:T(128)S(1)} %pad_add_fusion.where, bf16[257,320]{1,0:T(8,128)(2,1)S(1)} %bitcast.42, bf16[257,320]{1,0:T(8,128)(2,1)S(1)} %collective-permute-done.ty, bf16[257,320]{1,0:T(8,128)(2,1)} %collective-permute-done.1.tc, ...), custom_call_target="tpu_custom_call" | custom-call | flops 1011223040 | bytes 6800800 | tf_op jit(solution)/shard_map/pallas_call | solution.py:35
  31.9 1.6 %collective-permute-done.6 = bf16[257,640]{1,0:T(8,128)(2,1)S(1)} collective-permute-done((bf16[257,640]{1,0:T(8,128)(2,1)S(1)}, bf16[257,640]{1,0:T(8,128)(2,1)S(1)}, u32[]{:S(2)}, u32[]{:S(2)}) %collective-permute-start.6) | collective-permute-done | bytes 328992 | tf_op jit(solution)/shard_map/ppermute | solution.py:203
  33.6 1.4 collective-permute-start.7
  35.0 8.1 %collective-permute-done.7 = bf16[257,640]{1,0:T(8,128)(2,1)S(1)} collective-permute-done((bf16[257,640]{1,0:T(8,128)(2,1)S(1)}, bf16[257,640]{1,0:T(8,128)(2,1)S(1)}, u32[]{:S(2)}, u32[]{:S(2)}) %collective-permute-start.7) | collective-permute-done | bytes 328992 | tf_op jit(solution)/shard_map/ppermute | solution.py:204
  45.5 5.9 %shard_map.69 = (f32[257,1280]{1,0:T(8,128)S(1)}, bf16[257,640]{1,0:T(8,128)(2,1)S(1)}, bf16[257,640]{1,0:T(8,128)(2,1)S(1)}) custom-call(s32[4]{0:T(128)S(1)} %pad_add_fusion.where, bf16[257,640]{1,0:T(8,128)(2,1)S(1)} %add_convert_fusion.3.own, bf16[257,640]{1,0:T(8,128)(2,1)S(1)} %collective-permute-done.8.oth, ...), custom_call_target="tpu_custom_call" | custom-call | flops 1011223040 | bytes 8248224 | tf_op jit(solution)/shard_map/pallas_call | solution.py:35
  53.3 1.4 collective-permute-start.10
  54.7 7.9 %collective-permute-done.10 = bf16[257,640]{1,0:T(8,128)(2,1)S(1)} collective-permute-done((bf16[257,640]{1,0:T(8,128)(2,1)S(1)}, bf16[257,640]{1,0:T(8,128)(2,1)S(1)}, u32[]{:S(2)}, u32[]{:S(2)}) %collective-permute-start.10) | collective-permute-done | bytes 328992 | tf_op jit(solution)/shard_map/ppermute | solution.py:204
  62.6 1.3 collective-permute-start.11
  65.2 2.4 %shard_map.70 = (f32[257,320]{1,0:T(8,128)S(1)}, bf16[257,1280]{1,0:T(8,128)(2,1)S(1)}, bf16[8,160,320]{2,1,0:T(8,128)(2,1)S(1)}) custom-call(s32[4]{0:T(128)S(1)} %pad_add_fusion.where, bf16[257,640]{1,0:T(8,128)(2,1)S(1)} %add_convert_fusion.1.own, bf16[257,640]{1,0:T(8,128)(2,1)S(1)} %collective-permute-done.11.oth, ...), custom_call_target="tpu_custom_call" | custom-call | flops 210534400 | bytes 5720720 | tf_op jit(solution)/shard_map/pallas_call | solution.py:35
  70.6 8.3 %all-to-all-start = ((bf16[8,160,320]{2,1,0:T(8,128)(2,1)}), bf16[8,160,320]{2,1,0:T(8,128)(2,1)}, u32[]{:S(2)}, u32[]{:S(2)}) async-start(bf16[8,160,320]{2,1,0:T(8,128)(2,1)} %copy-done.7), calls=%async_computation | async-start | bytes 1966080 | tf_op jit(solution)/shard_map/all_to_all | solution.py:269
  82.3 3.5 %shard_map.71.grads = bf16[257,960]{1,0:T(8,128)(2,1)S(1)} custom-call(s32[4]{0:T(128)S(1)} %copy-done.20, bf16[257,1280]{1,0:T(8,128)(2,1)S(1)} %copy-done.9, bf16[320,1280]{1,0:T(8,128)(2,1)S(1)} %copy-done.4, bf16[12,257,80]{2,1,0:T(8,128)(2,1)S(1)} %copy-done.6, f32[4,257,257]{2,1,0:T(8,128)S(1)} %get-tuple-element.32.probs), custom_call_target="tpu_custom_call" | custom-call | flops 379619840 | bytes 3520800 | tf_op jit(solution)/shard_map/pallas_call | solution.py:35
  86.9 3.0 %collective-permute-start.12 = (bf16[4,160,448]{2,1,0:T(8,128)(2,1)S(1)}, bf16[4,160,448]{2,1,0:T(8,128)(2,1)}, u32[]{:S(2)}, u32[]{:S(2)}) collective-permute-start(bf16[4,160,448]{2,1,0:T(8,128)(2,1)S(1)} %shard_map.73), channel_id=1, source_target_pairs={{0,32},{32,0},{1,33},{33,1},{2,34},{34,2},{3,35},{35,3},{4,36},{36... | collective-permute-start | bytes 1720328 | tf_op jit(solution)/shard_map/ppermute | solution.py:283
  89.9 1.8 %shard_map.74 = (bf16[320,512]{1,0:T(8,128)(2,1)}, bf16[320,512]{1,0:T(8,128)(2,1)}, bf16[320,512]{1,0:T(8,128)(2,1)S(1)}) custom-call(s32[4]{0:T(128)S(1)} %copy-done.20, bf16[1280,257]{1,0:T(8,128)(2,1)S(1)} %get-tuple-element.43.xt, bf16[257,960]{1,0:T(8,128)(2,1)S(1)} %shard_map.71.grads), custom_call_target="tpu_custom_call" | custom-call | flops 252641280 | bytes 2134416 | tf_op jit(solution)/shard_map/pallas_call | solution.py:35
  91.6 2.7 %collective-permute-start.13 = (bf16[320,512]{1,0:T(8,128)(2,1)}, bf16[320,512]{1,0:T(8,128)(2,1)}, u32[]{:S(2)}, u32[]{:S(2)}) collective-permute-start(bf16[320,512]{1,0:T(8,128)(2,1)} %get-tuple-element.45), channel_id=1, source_target_pairs={{0,128},{64,192},{128,0},{192,64},{1,129},{65,193},{129,1},{193,65... | collective-permute-start | bytes 983048 | tf_op jit(solution)/shard_map/ppermute | solution.py:290
  94.7 2.4 %collective-permute-start.15 = (bf16[320,512]{1,0:T(8,128)(2,1)S(1)}, bf16[320,512]{1,0:T(8,128)(2,1)}, u32[]{:S(2)}, u32[]{:S(2)}) collective-permute-start(bf16[320,512]{1,0:T(8,128)(2,1)S(1)} %get-tuple-element.47), channel_id=1, source_target_pairs={{0,192},{64,0},{128,64},{192,128},{1,193},{65,1},{129,65},{193,129... | collective-permute-start | bytes 983048 | tf_op jit(solution)/shard_map/ppermute | solution.py:290
  99.0 3.0 %collective-permute-done.13 = bf16[320,512]{1,0:T(8,128)(2,1)} collective-permute-done((bf16[320,512]{1,0:T(8,128)(2,1)}, bf16[320,512]{1,0:T(8,128)(2,1)}, u32[]{:S(2)}, u32[]{:S(2)}) %collective-permute-start.13) | collective-permute-done | bytes 327712 | tf_op jit(solution)/shard_map/ppermute | solution.py:290
  101.9 8.2 %collective-permute-done.14 = bf16[320,512]{1,0:T(8,128)(2,1)} collective-permute-done((bf16[320,512]{1,0:T(8,128)(2,1)}, bf16[320,512]{1,0:T(8,128)(2,1)}, u32[]{:S(2)}, u32[]{:S(2)}) %collective-permute-start.14) | collective-permute-done | bytes 327712 | tf_op jit(solution)/shard_map/ppermute | solution.py:290
  110.1 1.3 add_convert_fusion.5
  113.0 2.4 %collective-permute-start.17 = (bf16[160,448]{1,0:T(8,128)(2,1)S(1)}, bf16[160,448]{1,0:T(8,128)(2,1)S(1)}, u32[]{:S(2)}, u32[]{:S(2)}) collective-permute-start(bf16[160,448]{1,0:T(8,128)(2,1)S(1)} %get-tuple-element.67), channel_id=1, source_target_pairs={{0,128},{64,192},{128,0},{192,64},{1,129},{65,193},{129,1},{193,65... | collective-permute-start | bytes 430088 | tf_op jit(solution)/shard_map/ppermute | solution.py:303
  116.1 1.9 %collective-permute-start.19 = (bf16[160,448]{1,0:T(8,128)(2,1)S(1)}, bf16[160,448]{1,0:T(8,128)(2,1)S(1)}, u32[]{:S(2)}, u32[]{:S(2)}) collective-permute-start(bf16[160,448]{1,0:T(8,128)(2,1)S(1)} %get-tuple-element.65), channel_id=1, source_target_pairs={{0,192},{64,0},{128,64},{192,128},{1,193},{65,1},{129,65},{193,129... | collective-permute-start | bytes 430088 | tf_op jit(solution)/shard_map/ppermute | solution.py:303
  118.0 1.4 reduce_sum.30
  120.1 4.0 %all-to-all-start.1 = ((bf16[8,20,320]{2,1,0:T(8,128)(2,1)}), bf16[8,20,320]{2,1,0:T(8,128)(2,1)S(1)}, u32[]{:S(2)}, u32[]{:S(2)}) async-start(bf16[8,20,320]{2,1,0:T(8,128)(2,1)} %reshape.20), calls=%async_computation.1 | async-start | bytes 294912 | tf_op jit(solution)/shard_map/all_to_all | solution.py:307
  124.1 6.9 %all-to-all-done.1 = bf16[8,20,320]{2,1,0:T(8,128)(2,1)S(1)} async-done(((bf16[8,20,320]{2,1,0:T(8,128)(2,1)}), bf16[8,20,320]{2,1,0:T(8,128)(2,1)S(1)}, u32[]{:S(2)}, u32[]{:S(2)}) %all-to-all-start.1) | async-done | bytes 102432 | tf_op jit(solution)/shard_map/all_to_all | solution.py:307
  132.0 6.6 %all-to-all-start.2 = ((bf16[8,20,960]{2,1,0:T(8,128)(2,1)}), bf16[8,20,960]{2,1,0:T(8,128)(2,1)S(1)}, u32[]{:S(2)}, u32[]{:S(2)}) async-start(bf16[8,20,960]{2,1,0:T(8,128)(2,1)} %reshape.21), calls=%async_computation.2 | async-start | bytes 786432 | tf_op jit(solution)/shard_map/all_to_all | solution.py:312
  140.5 9.4 %all-to-all-done.2 = bf16[8,20,960]{2,1,0:T(8,128)(2,1)S(1)} async-done(((bf16[8,20,960]{2,1,0:T(8,128)(2,1)}), bf16[8,20,960]{2,1,0:T(8,128)(2,1)S(1)}, u32[]{:S(2)}, u32[]{:S(2)}) %all-to-all-start.2) | async-done | bytes 307232 | tf_op jit(solution)/shard_map/all_to_all | solution.py:312
  (91 shorter events, 29.3 us)
Async XLA Ops:
  0.6 6.4 %collective-permute-start.3 = (bf16[257,320]{1,0:T(8,128)(2,1)}, bf16[257,320]{1,0:T(8,128)(2,1)S(1)}, u32[]{:S(2)}, u32[]{:S(2)}) collective-permute-start(bf16[257,320]{1,0:T(8,128)(2,1)} %bitcast.44), channel_id=1, source_target_pairs={{0,2},{2,0},{1,3},{3,1},{4,6},{6,4},{5,7},{7,5},{8,10},{10,8},{9,1... | collective-permute-start | bytes 493448 | tf_op jit(solution)/shard_map/ppermute | solution.py:209
  3.9 8.2 %collective-permute-start = (bf16[257,320]{1,0:T(8,128)(2,1)S(1)}, bf16[257,320]{1,0:T(8,128)(2,1)S(1)}, u32[]{:S(2)}, u32[]{:S(2)}) collective-permute-start(bf16[257,320]{1,0:T(8,128)(2,1)S(1)} %bitcast.40), channel_id=1, source_target_pairs={{0,2},{2,0},{1,3},{3,1},{4,6},{6,4},{5,7},{7,5},{8,10},{10,8},{9,1... | collective-permute-start | bytes 493448 | tf_op jit(solution)/shard_map/ppermute | solution.py:209
  4.0 9.7 %collective-permute-start.4 = (bf16[257,320]{1,0:T(8,128)(2,1)}, bf16[257,320]{1,0:T(8,128)(2,1)S(1)}, u32[]{:S(2)}, u32[]{:S(2)}) collective-permute-start(bf16[257,320]{1,0:T(8,128)(2,1)} %bitcast.45), channel_id=1, source_target_pairs={{0,1},{1,0},{2,3},{3,2},{4,5},{5,4},{6,7},{7,6},{8,9},{9,8},{10,11... | collective-permute-start | bytes 493448 | tf_op jit(solution)/shard_map/ppermute | solution.py:210
  7.1 7.3 %collective-permute-start.5 = (bf16[257,320]{1,0:T(8,128)(2,1)S(1)}, bf16[257,320]{1,0:T(8,128)(2,1)S(1)}, u32[]{:S(2)}, u32[]{:S(2)}) collective-permute-start(bf16[257,320]{1,0:T(8,128)(2,1)S(1)} %collective-permute-done.3.zy), channel_id=1, source_target_pairs={{0,1},{1,0},{2,3},{3,2},{4,5},{5,4},{6,7},{7,6},{8,9},{9,8},{10,11... | collective-permute-start | bytes 493448 | tf_op jit(solution)/shard_map/ppermute | solution.py:210
  12.1 12.2 %collective-permute-start.1 = (bf16[257,320]{1,0:T(8,128)(2,1)S(1)}, bf16[257,320]{1,0:T(8,128)(2,1)}, u32[]{:S(2)}, u32[]{:S(2)}) collective-permute-start(bf16[257,320]{1,0:T(8,128)(2,1)S(1)} %bitcast.41), channel_id=1, source_target_pairs={{0,1},{1,0},{2,3},{3,2},{4,5},{5,4},{6,7},{7,6},{8,9},{9,8},{10,11... | collective-permute-start | bytes 493448 | tf_op jit(solution)/shard_map/ppermute | solution.py:210
  12.1 12.2 %collective-permute-start.2 = (bf16[257,320]{1,0:T(8,128)(2,1)S(1)}, bf16[257,320]{1,0:T(8,128)(2,1)S(1)}, u32[]{:S(2)}, u32[]{:S(2)}) collective-permute-start(bf16[257,320]{1,0:T(8,128)(2,1)S(1)} %collective-permute-done.ty), channel_id=1, source_target_pairs={{0,1},{1,0},{2,3},{3,2},{4,5},{5,4},{6,7},{7,6},{8,9},{9,8},{10,11... | collective-permute-start | bytes 493448 | tf_op jit(solution)/shard_map/ppermute | solution.py:210
  15.0 1.7 %copy-start = (bf16[3,1280,320]{1,2,0:T(8,128)(2,1)S(1)}, bf16[3,1280,320]{1,2,0:T(8,128)(2,1)}, u32[]{:S(2)}) copy-start(bf16[3,1280,320]{1,2,0:T(8,128)(2,1)} %param.6) | copy-start | bytes 7372804
  20.4 3.9 %copy-start.1 = (bf16[3,1280,320]{1,2,0:T(8,128)(2,1)S(1)}, bf16[3,1280,320]{1,2,0:T(8,128)(2,1)}, u32[]{:S(2)}) copy-start(bf16[3,1280,320]{1,2,0:T(8,128)(2,1)} %param.6) | copy-start | bytes 7372804
  24.3 21.3 %copy-start.5 = (bf16[12,257,80]{2,1,0:T(8,128)(2,1)}, bf16[12,257,80]{2,1,0:T(8,128)(2,1)S(1)}, u32[]{:S(2)}) copy-start(bf16[12,257,80]{2,1,0:T(8,128)(2,1)S(1)} %get-tuple-element.31.qkv) | copy-start | bytes 1480324
  24.3 1.4 copy-start.2
  31.6 13.9 %copy-start.3 = (bf16[320,1280]{1,0:T(8,128)(2,1)S(1)}, bf16[320,1280]{1,0:T(8,128)(2,1)}, u32[]{:S(2)}) copy-start(bf16[320,1280]{1,0:T(8,128)(2,1)} %w_out.5) | copy-start | bytes 2457604
  31.6 1.9 %collective-permute-start.6 = (bf16[257,640]{1,0:T(8,128)(2,1)S(1)}, bf16[257,640]{1,0:T(8,128)(2,1)S(1)}, u32[]{:S(2)}, u32[]{:S(2)}) collective-permute-start(bf16[257,640]{1,0:T(8,128)(2,1)S(1)} %get-tuple-element.34), channel_id=1, source_target_pairs={{0,1},{1,0},{2,3},{3,2},{4,5},{5,4},{6,7},{7,6},{8,9},{9,8},{10,11... | collective-permute-start | bytes 986888 | tf_op jit(solution)/shard_map/ppermute | solution.py:203
  33.6 9.4 %collective-permute-start.7 = (bf16[257,640]{1,0:T(8,128)(2,1)S(1)}, bf16[257,640]{1,0:T(8,128)(2,1)S(1)}, u32[]{:S(2)}, u32[]{:S(2)}) collective-permute-start(bf16[257,640]{1,0:T(8,128)(2,1)S(1)} %add_convert_fusion.4), channel_id=1, source_target_pairs={{0,2},{2,0},{1,3},{3,1},{4,6},{6,4},{5,7},{7,5},{8,10},{10,8},{9,1... | collective-permute-start | bytes 986888 | tf_op jit(solution)/shard_map/ppermute | solution.py:204
  43.2 2.4 %collective-permute-start.8 = (bf16[257,640]{1,0:T(8,128)(2,1)S(1)}, bf16[257,640]{1,0:T(8,128)(2,1)S(1)}, u32[]{:S(2)}, u32[]{:S(2)}) collective-permute-start(bf16[257,640]{1,0:T(8,128)(2,1)S(1)} %add_convert_fusion.3.own), channel_id=1, source_target_pairs={{0,1},{1,0},{2,3},{3,2},{4,5},{5,4},{6,7},{7,6},{8,9},{9,8},{10,11... | collective-permute-start | bytes 986888 | tf_op jit(solution)/shard_map/ppermute | solution.py:205
  51.5 12.5 %copy-start.21 = (f32[1,257,320]{2,0,1:T(1,128)S(1)}, f32[1,257,320]{2,0,1:T(1,128)}, u32[]{:S(2)}) copy-start(f32[1,257,320]{2,0,1:T(1,128)} %param.5) | copy-start | bytes 986884
  51.5 1.7 %collective-permute-start.9 = (bf16[257,640]{1,0:T(8,128)(2,1)S(1)}, bf16[257,640]{1,0:T(8,128)(2,1)S(1)}, u32[]{:S(2)}, u32[]{:S(2)}) collective-permute-start(bf16[257,640]{1,0:T(8,128)(2,1)S(1)} %get-tuple-element.38), channel_id=1, source_target_pairs={{0,1},{1,0},{2,3},{3,2},{4,5},{5,4},{6,7},{7,6},{8,9},{9,8},{10,11... | collective-permute-start | bytes 986888 | tf_op jit(solution)/shard_map/ppermute | solution.py:203
  53.3 9.2 %collective-permute-start.10 = (bf16[257,640]{1,0:T(8,128)(2,1)S(1)}, bf16[257,640]{1,0:T(8,128)(2,1)S(1)}, u32[]{:S(2)}, u32[]{:S(2)}) collective-permute-start(bf16[257,640]{1,0:T(8,128)(2,1)S(1)} %add_convert_fusion.2), channel_id=1, source_target_pairs={{0,2},{2,0},{1,3},{3,1},{4,6},{6,4},{5,7},{7,5},{8,10},{10,8},{9,1... | collective-permute-start | bytes 986888 | tf_op jit(solution)/shard_map/ppermute | solution.py:204
  62.6 2.6 %collective-permute-start.11 = (bf16[257,640]{1,0:T(8,128)(2,1)S(1)}, bf16[257,640]{1,0:T(8,128)(2,1)S(1)}, u32[]{:S(2)}, u32[]{:S(2)}) collective-permute-start(bf16[257,640]{1,0:T(8,128)(2,1)S(1)} %add_convert_fusion.1.own), channel_id=1, source_target_pairs={{0,1},{1,0},{2,3},{3,2},{4,5},{5,4},{6,7},{7,6},{8,9},{9,8},{10,11... | collective-permute-start | bytes 986888 | tf_op jit(solution)/shard_map/ppermute | solution.py:205
  70.6 8.3 %copy-start.20 = (s32[4]{0:T(128)S(1)}, s32[4]{0:T(128)}, u32[]{:S(2)}) copy-start(s32[4]{0:T(128)} %copy-done.19) | copy-start | bytes 52
  70.6 39.5 %all-to-all-start = ((bf16[8,160,320]{2,1,0:T(8,128)(2,1)}), bf16[8,160,320]{2,1,0:T(8,128)(2,1)}, u32[]{:S(2)}, u32[]{:S(2)}) async-start(bf16[8,160,320]{2,1,0:T(8,128)(2,1)} %copy-done.7), calls=%async_computation | async-start | bytes 1966080 | tf_op jit(solution)/shard_map/all_to_all | solution.py:269
  78.9 1.1 copy-start.4
  86.9 23.3 %collective-permute-start.12 = (bf16[4,160,448]{2,1,0:T(8,128)(2,1)S(1)}, bf16[4,160,448]{2,1,0:T(8,128)(2,1)}, u32[]{:S(2)}, u32[]{:S(2)}) collective-permute-start(bf16[4,160,448]{2,1,0:T(8,128)(2,1)S(1)} %shard_map.73), channel_id=1, source_target_pairs={{0,32},{32,0},{1,33},{33,1},{2,34},{34,2},{3,35},{35,3},{4,36},{36... | collective-permute-start | bytes 1720328 | tf_op jit(solution)/shard_map/ppermute | solution.py:283
  91.6 10.3 %collective-permute-start.13 = (bf16[320,512]{1,0:T(8,128)(2,1)}, bf16[320,512]{1,0:T(8,128)(2,1)}, u32[]{:S(2)}, u32[]{:S(2)}) collective-permute-start(bf16[320,512]{1,0:T(8,128)(2,1)} %get-tuple-element.45), channel_id=1, source_target_pairs={{0,128},{64,192},{128,0},{192,64},{1,129},{65,193},{129,1},{193,65... | collective-permute-start | bytes 983048 | tf_op jit(solution)/shard_map/ppermute | solution.py:290
  94.4 15.7 %collective-permute-start.14 = (bf16[320,512]{1,0:T(8,128)(2,1)}, bf16[320,512]{1,0:T(8,128)(2,1)}, u32[]{:S(2)}, u32[]{:S(2)}) collective-permute-start(bf16[320,512]{1,0:T(8,128)(2,1)} %get-tuple-element.46), channel_id=1, source_target_pairs={{0,64},{64,128},{128,192},{192,0},{1,65},{65,129},{129,193},{193,1... | collective-permute-start | bytes 983048 | tf_op jit(solution)/shard_map/ppermute | solution.py:290
  94.7 15.4 %collective-permute-start.15 = (bf16[320,512]{1,0:T(8,128)(2,1)S(1)}, bf16[320,512]{1,0:T(8,128)(2,1)}, u32[]{:S(2)}, u32[]{:S(2)}) collective-permute-start(bf16[320,512]{1,0:T(8,128)(2,1)S(1)} %get-tuple-element.47), channel_id=1, source_target_pairs={{0,192},{64,0},{128,64},{192,128},{1,193},{65,1},{129,65},{193,129... | collective-permute-start | bytes 983048 | tf_op jit(solution)/shard_map/ppermute | solution.py:290
  111.5 19.5 %collective-permute-start.16 = (bf16[160,512]{1,0:T(8,128)(2,1)S(1)}, bf16[160,512]{1,0:T(8,128)(2,1)S(1)}, u32[]{:S(2)}, u32[]{:S(2)}) collective-permute-start(bf16[160,512]{1,0:T(8,128)(2,1)S(1)} %dynamic-slice_bitcast_fusion.3), channel_id=1, source_target_pairs={{0,32},{32,0},{1,33},{33,1},{2,34},{34,2},{3,35},{35,3},{4,36},{36... | collective-permute-start | bytes 491528 | tf_op jit(solution)/shard_map/ppermute | solution.py:305
  113.0 18.0 %collective-permute-start.17 = (bf16[160,448]{1,0:T(8,128)(2,1)S(1)}, bf16[160,448]{1,0:T(8,128)(2,1)S(1)}, u32[]{:S(2)}, u32[]{:S(2)}) collective-permute-start(bf16[160,448]{1,0:T(8,128)(2,1)S(1)} %get-tuple-element.67), channel_id=1, source_target_pairs={{0,128},{64,192},{128,0},{192,64},{1,129},{65,193},{129,1},{193,65... | collective-permute-start | bytes 430088 | tf_op jit(solution)/shard_map/ppermute | solution.py:303
  115.3 15.6 %collective-permute-start.18 = (bf16[160,448]{1,0:T(8,128)(2,1)S(1)}, bf16[160,448]{1,0:T(8,128)(2,1)S(1)}, u32[]{:S(2)}, u32[]{:S(2)}) collective-permute-start(bf16[160,448]{1,0:T(8,128)(2,1)S(1)} %get-tuple-element.66), channel_id=1, source_target_pairs={{0,64},{64,128},{128,192},{192,0},{1,65},{65,129},{129,193},{193,1... | collective-permute-start | bytes 430088 | tf_op jit(solution)/shard_map/ppermute | solution.py:303
  116.1 14.8 %collective-permute-start.19 = (bf16[160,448]{1,0:T(8,128)(2,1)S(1)}, bf16[160,448]{1,0:T(8,128)(2,1)S(1)}, u32[]{:S(2)}, u32[]{:S(2)}) collective-permute-start(bf16[160,448]{1,0:T(8,128)(2,1)S(1)} %get-tuple-element.65), channel_id=1, source_target_pairs={{0,192},{64,0},{128,64},{192,128},{1,193},{65,1},{129,65},{193,129... | collective-permute-start | bytes 430088 | tf_op jit(solution)/shard_map/ppermute | solution.py:303
  120.1 10.8 %all-to-all-start.1 = ((bf16[8,20,320]{2,1,0:T(8,128)(2,1)}), bf16[8,20,320]{2,1,0:T(8,128)(2,1)S(1)}, u32[]{:S(2)}, u32[]{:S(2)}) async-start(bf16[8,20,320]{2,1,0:T(8,128)(2,1)} %reshape.20), calls=%async_computation.1 | async-start | bytes 294912 | tf_op jit(solution)/shard_map/all_to_all | solution.py:307
  131.0 7.7 %copy-start.11 = (f32[257,320]{1,0:T(8,128)S(1)}, f32[257,320]{1,0:T(8,128)}, u32[]{:S(2)}) copy-start(f32[257,320]{1,0:T(8,128)} %copy-done.10) | copy-start | bytes 986884
  132.0 17.9 %all-to-all-start.2 = ((bf16[8,20,960]{2,1,0:T(8,128)(2,1)}), bf16[8,20,960]{2,1,0:T(8,128)(2,1)S(1)}, u32[]{:S(2)}, u32[]{:S(2)}) async-start(bf16[8,20,960]{2,1,0:T(8,128)(2,1)} %reshape.21), calls=%async_computation.2 | async-start | bytes 786432 | tf_op jit(solution)/shard_map/all_to_all | solution.py:312
  (13 other events, 11.1 us)

commit v2 on v0

v2 whole, which is shorter than its diff:
```python
import functools
import math

import jax
import jax.numpy as jnp
from jax import lax
from jax.experimental import pallas as pl
from jax.experimental.pallas import tpu as pltpu
from jax.sharding import Mesh
from jax.sharding import PartitionSpec as P


HD = 80
AXES = ("x", "yh", "z", "yl", "c")
DP = ("x", "yh", "z")
MP = ("yl", "c")
SWAP = [(0, 1), (1, 0)]
MINE, OTHER = 0, 1

epsilon = 1e-06
f32 = jnp.float32
bf16 = jnp.bfloat16
SCALE = HD ** (-0.5)
ROWS = (((0,), (0,)), ((), ()))
COLS = (((1,), (1,)), ((), ()))


def dot(a, b, dims=(((1,), (0,)), ((), ()))):
    return lax.dot_general(a, b, dims, preferred_element_type=f32)


def call(body, outs, ins, scratch=(), flops=0):
    vmem = pl.BlockSpec(memory_space=pltpu.VMEM)
    smem = pl.BlockSpec(memory_space=pltpu.SMEM)
    size = sum(math.prod(o.shape) * o.dtype.itemsize for o in list(outs) + list(ins))
    return pl.pallas_call(
        body,
        out_shape=outs,
        in_specs=[smem] + [vmem] * (len(ins) - 1),
        out_specs=[vmem] * len(outs),
        scratch_shapes=list(scratch),
        compiler_params=pltpu.CompilerParams(vmem_limit_bytes=20 * 2**20),
        cost_estimate=pl.CostEstimate(flops=flops, bytes_accessed=size, transcendentals=0),
    )(*ins)


def like(shape, dtype):
    return jax.ShapeDtypeStruct(shape, dtype)


def prepare_body(where, cot, w, w_out, cot_o, w_o, w_out_o):
    narrow = w_out.shape[0]
    cot_o[...] = cot[...].astype(bf16)
    for c in range(2):

        @pl.when(where[1] == c)
        def _():
            for k, core in enumerate((c, 1 - c)):
                for y in range(2):
                    src = (2 * y + core) * narrow
                    at = (2 * k + y) * narrow
                    w_out_o[:, at : at + narrow] = w_out[:, src : src + narrow]
                    for s in range(3):
                        w_o[s * narrow : (s + 1) * narrow, at : at + narrow] = w[s, :, src : src + narrow]


def put_pieces(where, spot, mine, y, core, both):
    narrow = mine.shape[1]
    for yl in range(2):

        @pl.when(where[0] == yl)
        def _():
            for k, (near, far) in enumerate(((mine, y), (core, both))):
                for at, piece in ((2 * k + yl, near), (2 * k + 1 - yl, far)):
                    spot[:, at * narrow : (at + 1) * narrow] = piece[...]


def forward_body(where, z0, zy, zc, zcy, w, normal_o, xt_o, inv_o, qkv_o, probs_o, att_o, zs):
    put_pieces(where, zs, z0, zy, zc, zcy)
    width = zs.shape[1]
    narrow = width // 4
    values = zs[...].astype(f32)
    centred = values - jnp.sum(values, axis=-1, keepdims=True) * (1.0 / width)
    inv = lax.rsqrt(jnp.sum(centred * centred, axis=-1, keepdims=True) * (1.0 / width) + epsilon)
    inv_o[...] = jnp.broadcast_to(inv, inv_o.shape)
    normal_o[...] = (centred * inv).astype(bf16)
    heads = narrow // HD
    for s in range(3):
        got = dot(normal_o[...], w[s * narrow : (s + 1) * narrow, :], COLS).astype(bf16)
        for h in range(heads):
            qkv_o[s * heads + h] = got[:, h * HD : (h + 1) * HD]
    for h in range(heads):
        scores = dot(qkv_o[h], qkv_o[heads + h], COLS) * SCALE
        top = jnp.max(scores, axis=-1, keepdims=True)
        e = jnp.exp(scores - top)
        probs = e / jnp.sum(e, axis=-1, keepdims=True)
        probs_o[h] = probs
        att_o[:, h * HD : (h + 1) * HD] = dot(probs.astype(bf16), qkv_o[2 * heads + h]).astype(bf16)
    xt_o[...] = normal_o[...].T


def attention_back(cot, w_out, qkv, probs, grads):
    narrow = w_out.shape[0]
    heads = narrow // HD
    att = dot(cot, w_out[...], COLS).astype(bf16)
    for h in range(heads):
        a = att[:, h * HD : (h + 1) * HD]
        p = probs[h]
        dp = dot(a, qkv[2 * heads + h], COLS)
        along = jnp.sum(p * dp, axis=-1, keepdims=True)
        ds = (p * (dp - along) * SCALE).astype(bf16)
        for s, got in enumerate(
            (
                dot(ds, qkv[heads + h]),
                dot(ds, qkv[h], ROWS),
                dot(p.astype(bf16), a, ROWS),
            )
        ):
            at = s * narrow + h * HD
            grads[:, at : at + HD] = got.astype(bf16)


def input_back(half, grads, w):
    wide = w.shape[1] // 2
    return dot(grads[...], w[:, half * wide : (half + 1) * wide]).astype(bf16)


def first_body(where, t0, ty, tc, tcy, w_out, qkv, probs, w, cot_o, grads_o, oth_o):
    put_pieces(where, cot_o, t0, ty, tc, tcy)
    attention_back(cot_o[...], w_out, qkv, probs, grads_o)
    oth_o[...] = input_back(OTHER, grads_o, w)


def own_body(where, grads, w, own_o):
    own_o[...] = input_back(MINE, grads, w)


def put_term(spot, chip, far, chip_c, far_c, normal, inv):
    half = chip.shape[1]
    spot[:, :half] = chip[...].astype(f32) + far[...].astype(f32)
    spot[:, half:] = chip_c[...].astype(f32) + far_c[...].astype(f32)
    g = spot[...]
    width = g.shape[1]
    n = normal[...].astype(f32)
    mean = jnp.sum(g, axis=-1, keepdims=True) * (1.0 / width)
    along = jnp.sum(g * n, axis=-1, keepdims=True) * (1.0 / width)
    return (g - mean - n * along) * inv[:, :1]


def middle_body(where, chip, far, chip_c, far_c, normal, inv, w_out, qkv, probs, w, term_o, grads_o, oth_o):
    term_o[...] = put_term(term_o, chip, far, chip_c, far_c, normal, inv)
    attention_back(term_o[...].astype(bf16), w_out, qkv, probs, grads_o)
    oth_o[...] = input_back(OTHER, grads_o, w)


def last_body(where, chip, far, chip_c, far_c, normal, inv, w_out, qkv, probs, cot, term, mine, imp_o, grads_o, total_o, spot):
    spot[...] = put_term(spot, chip, far, chip_c, far_c, normal, inv) + term[...]
    narrow = mine.shape[1]
    for yl in range(2):

        @pl.when(where[0] == yl)
        def _():
            imp_o[...] = mine[...] + spot[:, yl * narrow : (yl + 1) * narrow]

    total = (spot[...] + cot[...].astype(f32)).astype(bf16)
    total_o[...] = total
    attention_back(total, w_out, qkv, probs, grads_o)


def spot_of(where, x, narrow):
    other = lax.rem(x + where[1], 2)
    return (2 * other + lax.div(x, 2)) * narrow


def gather_rows(where, src, dst, picks, narrow):
    rows = narrow // 2
    for i, (dx, dy) in enumerate(picks):
        at = spot_of(where, lax.bitwise_xor(where[2], dx), narrow)
        at = at + lax.bitwise_xor(where[3], dy) * rows
        dst[i * rows : (i + 1) * rows, :] = src[pl.ds(pl.multiple_of(at, 16), rows), :]


def rows_body(picks, first, where, xt, grads, out, xs):
    gather_rows(where, xt, xs, picks, grads.shape[1] // 3)
    out[...] = dot(xs[...], grads[:, first : first + out.shape[1]]).astype(bf16)


def turn_body(where, total, tt_o):
    tt_o[...] = total[...].T


def tail_rows_body(picks, where, xt, tt, grads, att, out, xs):
    narrow = att.shape[1]
    left = out.shape[1] - narrow
    gather_rows(where, xt, xs, picks, narrow)
    one = dot(xs[...], grads[:, grads.shape[1] - left :])
    gather_rows(where, tt, xs, picks, narrow)
    two = dot(xs[...], att[...])
    out[:, :left] = one.astype(bf16)
    out[:, left:] = two.astype(bf16)


def pack_body(where, k1, g1, k2, g2, k3, g3, out, spot):
    at = 0
    for k, g in ((k1, g1), (k2, g2), (k3, g3)):
        spot[:, at : at + k.shape[1]] = k[...].astype(f32) + g[...].astype(f32)
        at += k.shape[1]
    nz, _, lanes = out.shape
    each = spot.shape[0] // nz
    for z in range(nz):
        for b in range(spot.shape[1] // lanes):
            piece = spot[z * each : (z + 1) * each, b * lanes : (b + 1) * lanes]
            out[z, b * each : (b + 1) * each, :] = piece.astype(bf16)


def unpack_body(factor, where, got, qkv_o, out_o, spot):
    total = got[0].astype(f32)
    for z in range(1, got.shape[0]):
        total = total + got[z].astype(f32)
    total = total * factor
    each, width = spot.shape
    lanes = got.shape[2]
    for b in range(width // lanes):
        spot[:, b * lanes : (b + 1) * lanes] = total[b * each : (b + 1) * each, :]
    narrow = out_o.shape[1]
    for k in range(3):
        qkv_o[k] = spot[:, k * narrow : (k + 1) * narrow]
    out_o[...] = spot[:, 3 * narrow :]


def add(*parts):
    return sum(p.astype(f32) for p in parts).astype(bf16)


def mp_sum(oth, own):
    chip = add(own(), lax.ppermute(oth, "c", SWAP))
    far = lax.ppermute(chip, "yl", SWAP)
    return chip, far, lax.ppermute(chip, "c", SWAP), lax.ppermute(far, "c", SWAP)


def shards(z_star, cotangent, w_qkv, w_out):
    images, tokens, narrow = z_star.shape
    width = 4 * narrow
    heads = narrow // HD
    nx, ny, nz = [lax.axis_size(a) for a in DP]
    x, yh = lax.axis_index("x"), lax.axis_index("yh")
    where = jnp.stack([lax.axis_index("yl"), lax.axis_index("c"), x, yh]).astype(jnp.int32)

    wide = like((tokens, width), bf16)
    wide_f = like((tokens, width), f32)
    half = like((tokens, 2 * narrow), bf16)
    g_like = like((tokens, 3 * narrow), bf16)
    proj = 2 * tokens * width * narrow
    small = 2 * tokens * tokens * HD * heads

    z0 = z_star[0]
    zy = lax.ppermute(z0, "yl", SWAP)
    zc = lax.ppermute(z0, "c", SWAP)
    t0, w, wo = call(
        prepare_body,
        (like((tokens, narrow), bf16), like((3 * narrow, width), bf16), like((narrow, width), bf16)),
        (where, cotangent[0], jnp.swapaxes(w_qkv, 1, 2), w_out),
        flops=proj,
    )
    tc = lax.ppermute(t0, "c", SWAP)
    zy, t0 = lax.optimization_barrier((zy, t0))
    zcy = lax.ppermute(zy, "c", SWAP)
    ty = lax.ppermute(t0, "yl", SWAP)
    tcy = lax.ppermute(ty, "c", SWAP)
    normal, xt, inv, qkv, probs, att = call(
        forward_body,
        (
            wide,
            like((width, tokens), bf16),
            like((tokens, 128), f32),
            like((3 * heads, tokens, HD), bf16),
            like((heads, tokens, tokens), f32),
            like((tokens, narrow), bf16),
        ),
        (where, z0, zy, zc, zcy, w),
        [pltpu.VMEM((tokens, width), bf16)],
        flops=3 * proj + 2 * small,
    )

    def own_of(grads):
        return call(own_body, (half,), (where, grads, w), flops=3 * proj // 2)[0]

    cot, grads, oth = call(
        first_body,
        (wide, g_like, half),
        (where, t0, ty, tc, tcy, wo, qkv, probs, w),
        flops=3 * proj + 4 * small,
    )
    sums = mp_sum(oth, lambda: own_of(grads))
    term, grads, oth = call(
        middle_body,
        (wide_f, g_like, half),
        (where, *sums, normal, inv, wo, qkv, probs, w),
        flops=3 * proj + 4 * small,
    )
    sums = mp_sum(oth, lambda: own_of(grads))
    implicit, grads, total = call(
        last_body,
        (like((tokens, narrow), f32), g_like, wide),
        (where, *sums, normal, inv, wo, qkv, probs, cot, term, cotangent[0]),
        [pltpu.VMEM((tokens, width), f32)],
        flops=proj + 4 * small,
    )

    rows = width // (nx * ny)
    each = rows // nz
    tall = [pltpu.VMEM((4 * rows, tokens), bf16)]

    def block(picks, first, cols):
        return call(
            functools.partial(rows_body, picks, first),
            (like((4 * rows, cols), bf16),),
            (where, xt, grads),
            tall,
            flops=2 * tokens * 4 * rows * cols,
        )[0]

    def tail_block(picks, cols):
        return call(
            functools.partial(tail_rows_body, picks),
            (like((4 * rows, cols), bf16),),
            (where, xt, tt, grads, att),
            tall,
            flops=2 * tokens * 4 * rows * cols,
        )[0]

    def swap_x(value, by):
        return lax.ppermute(value, "x", [(i, i ^ by) for i in range(nx)])

    def swap_yh(value):
        return lax.ppermute(value, "yh", SWAP)

    def at(value, start, count):
        return value[start * rows : (start + count) * rows]

    one, two, three = 384, 512, 384
    s2 = block(((3, 0), (2, 0), (3, 1), (2, 1)), one, two)
    g2 = swap_x(s2, 3)
    s1 = block(((1, 0), (1, 1), (2, 0), (2, 1)), 0, one)
    g1 = swap_x(s1, 1)
    (tt,) = call(turn_body, (like((width, tokens), bf16),), (where, total), flops=proj)
    s3 = tail_block(((0, 1), (3, 1), (1, 1), (2, 1)), three)
    g3 = swap_yh(s3)
    k2 = block(((0, 0), (1, 0), (0, 1), (1, 1)), one, two)
    k1 = block(((0, 0), (0, 1), (3, 0), (3, 1)), 0, one)
    k3 = tail_block(((0, 0), (3, 0), (1, 0), (2, 0)), three)

    h2 = swap_yh(add(at(k2, 2, 2), at(g2, 2, 2)))
    h1 = swap_x(add(at(k1, 2, 2), at(g1, 2, 2)), 3)
    h3 = swap_x(add(at(k3, 2, 2), at(g3, 2, 2)), 1)

    def last_half(k, g, h, swap):
        send = add(at(k, 1, 1), at(g, 1, 1), at(h, 1, 1))
        got = swap(send)
        return add(at(k, 0, 1), at(g, 0, 1), at(h, 0, 1)), got

    e2 = last_half(k2, g2, h2, lambda v: swap_x(v, 1))
    e1 = last_half(k1, g1, h1, swap_yh)
    e3 = last_half(k3, g3, h3, lambda v: swap_x(v, 3))
    dense = each * width // 128
    (packed,) = call(
        pack_body,
        (like((nz, dense, 128), bf16),),
        (where, *e1, *e2, *e3),
        [pltpu.VMEM((rows, width), f32)],
        flops=rows * width,
    )
    got = lax.all_to_all(packed, "z", 0, 0, tiled=True)
    factor = 1.0 / math.sqrt(images * nx * ny * nz * tokens)
    grad_qkv, grad_o = call(
        functools.partial(unpack_body, factor),
        (like((3, each, narrow), f32), like((each, narrow), f32)),
        (where, got),
        [pltpu.VMEM((each, width), f32)],
        flops=rows * width,
    )
    return implicit[None], grad_qkv, grad_o.T


def solution(mesh):
    split = Mesh(mesh.devices.reshape(4, 2, 8, 2, 2), AXES)

    return jax.shard_map(
        shards,
        mesh=split,
        in_specs=(P(DP, None, MP), P(DP, None, MP), P(None, None, MP), P(MP, None)),
        out_specs=(P(DP, None, MP), P(None, DP, MP), P(MP, DP)),
        check_vma=False,
    )
```

time: 139 us -> 122 us (0.88)
  the two profiles are of different devices: /device:TPU:1 before, /device:TPU:16 now
where the time goes in v2:
time: 122 us
  waiting for transfers between devices  57.8 us (47%)
  Pallas kernels  31.4 us (26%)
  starting transfers between devices  26.3 us (22%)
  local copies, waits for them, and re-layouts  5.02 us (4%)
    pallas_call x16, Pallas kernels, call(): pl.pallas_call(body, out_shape=outs, in_specs=[smem] + [vmem] * (len(ins)...  31.4 us
    ppermute x2, waiting for transfers between devices, mp_sum(): far = lax.ppermute(chip, 'yl', SWAP)  18 us
    ppermute x6, waiting for transfers between devices, swap_x(): return lax.ppermute(value, 'x', [(i, i ^ by) for i in range(nx)])  14.8 us
    all_to_all x1, waiting for transfers between devices, shards(): got = lax.all_to_all(packed, 'z', 0, 0, tiled=True)  10.9 us
    ppermute x6, starting transfers between devices, swap_x(): return lax.ppermute(value, 'x', [(i, i ^ by) for i in range(nx)])  9.19 us
    all_to_all x1, starting transfers between devices, shards(): got = lax.all_to_all(packed, 'z', 0, 0, tiled=True)  8.49 us
    ppermute x3, waiting for transfers between devices, swap_yh(): return lax.ppermute(value, 'yh', SWAP)  5.55 us
    unnamed x8, local copies, waits for them, and re-layouts  5.02 us
  transfers between devices with their start and end apart: 24, of which 14 were waited for; matrix products, arithmetic and copies ran while one was open for 2% of the time, Pallas kernels for 11%

profile of v2, /device:TPU:16, one launch (start us, length us, event | category | flops | bytes accessed | tf_op | source)
XLA Modules:
  0.0 122.2 jit_solution(13263314770743139470)
XLA Ops:
  0.6 1.4 %collective-permute-start = (bf16[257,320]{1,0:T(8,128)(2,1)}, bf16[257,320]{1,0:T(8,128)(2,1)S(1)}, u32[]{:S(2)}, u32[]{:S(2)}) collective-permute-start(bf16[257,320]{1,0:T(8,128)(2,1)} %bitcast.15), channel_id=1, source_target_pairs={{0,2},{2,0},{1,3},{3,1},{4,6},{6,4},{5,7},{7,5},{8,10},{10,8},{9,1... | collective-permute-start | bytes 493448 | tf_op jit(solution)/shard_map/ppermute | solution.py:257
  3.1 1.7 %copy-done = bf16[3,1280,320]{1,2,0:T(8,128)(2,1)S(1)} copy-done((bf16[3,1280,320]{1,2,0:T(8,128)(2,1)S(1)}, bf16[3,1280,320]{1,2,0:T(8,128)(2,1)}, u32[]{:S(2)}) %copy-start) | copy-done | bytes 2457624
  4.8 1.1 copy-done.1
  6.0 1.4 %shard_map.67 = (bf16[257,320]{1,0:T(8,128)(2,1)S(1)}, bf16[960,1280]{1,0:T(8,128)(2,1)S(1)}, bf16[320,1280]{1,0:T(8,128)(2,1)S(1)}) custom-call(s32[4]{0:T(128)S(1)} %pad_add_fusion.where, f32[257,320]{1,0:T(8,128)S(1)} %bitcast.11, bf16[3,320,1280]{2,1,0:T(8,128)(2,1)S(1)} %bitcast.13, bf16[320,1280]{1,0:T(8,128)(2,1)S(1)} %copy-done.1), custom_call_target="tpu_custom_call" | custom-call | flops 210534400 | bytes 7047056 | tf_op jit(solution)/shard_map/pallas_call | solution.py:36
  7.7 1.3 %collective-permute-start.1 = (bf16[257,320]{1,0:T(8,128)(2,1)S(1)}, bf16[257,320]{1,0:T(8,128)(2,1)S(1)}, u32[]{:S(2)}, u32[]{:S(2)}) collective-permute-start(bf16[257,320]{1,0:T(8,128)(2,1)S(1)} %get-tuple-element.26.t0), channel_id=1, source_target_pairs={{0,2},{2,0},{1,3},{3,1},{4,6},{6,4},{5,7},{7,5},{8,10},{10,8},{9,1... | collective-permute-start | bytes 493448 | tf_op jit(solution)/shard_map/ppermute | solution.py:268
  9.5 4.4 %collective-permute-done.1.ty = bf16[257,320]{1,0:T(8,128)(2,1)S(1)} collective-permute-done((bf16[257,320]{1,0:T(8,128)(2,1)S(1)}, bf16[257,320]{1,0:T(8,128)(2,1)S(1)}, u32[]{:S(2)}, u32[]{:S(2)}) %collective-permute-start.1) | collective-permute-done | bytes 164512 | tf_op jit(solution)/shard_map/ppermute | solution.py:268
  13.9 3.8 %shard_map.68 = (bf16[257,1280]{1,0:T(8,128)(2,1)S(1)}, bf16[1280,257]{1,0:T(8,128)(2,1)S(1)}, f32[257,128]{1,0:T(8,128)S(1)}, bf16[12,257,80]{2,1,0:T(8,128)(2,...) custom-call(s32[4]{0:T(128)S(1)} %pad_add_fusion.where, bf16[257,320]{1,0:T(8,128)(2,1)S(1)} %bitcast.17, ...), custom_call_target="tpu_custom_call" | custom-call | flops 716145920 | bytes 6277664 | tf_op jit(solution)/shard_map/pallas_call | solution.py:36
  17.8 4.5 %shard_map.69 = (bf16[257,1280]{1,0:T(8,128)(2,1)S(1)}, bf16[257,960]{1,0:T(8,128)(2,1)S(1)}, bf16[257,640]{1,0:T(8,128)(2,1)S(1)}) custom-call(s32[4]{0:T(128)S(1)} %pad_add_fusion.where, bf16[257,320]{1,0:T(8,128)(2,1)S(1)} %get-tuple-element.26.t0, bf16[257,320]{1,0:T(8,128)(2,1)S(1)} %collective-permute-done.1.ty, ...), custom_call_target="tpu_custom_call" | custom-call | flops 800688640 | bytes 6965280 | tf_op jit(solution)/shard_map/pallas_call | solution.py:36
  23.1 1.1 shard_map.70
  25.6 9.1 %collective-permute-done.7.far = bf16[257,640]{1,0:T(8,128)(2,1)S(1)} collective-permute-done((bf16[257,640]{1,0:T(8,128)(2,1)S(1)}, bf16[257,640]{1,0:T(8,128)(2,1)S(1)}, u32[]{:S(2)}, u32[]{:S(2)}) %collective-permute-start.7) | collective-permute-done | bytes 328992 | tf_op jit(solution)/shard_map/ppermute | solution.py:237
  34.7 1.6 %collective-permute-done.9.far_c = bf16[257,640]{1,0:T(8,128)(2,1)S(1)} collective-permute-done((bf16[257,640]{1,0:T(8,128)(2,1)S(1)}, bf16[257,640]{1,0:T(8,128)(2,1)S(1)}, u32[]{:S(2)}, u32[]{:S(2)}) %collective-permute-start.9) | collective-permute-done | bytes 328992 | tf_op jit(solution)/shard_map/ppermute | solution.py:238
  36.4 4.7 %shard_map.71 = (f32[257,1280]{1,0:T(8,128)S(1)}, bf16[257,960]{1,0:T(8,128)(2,1)S(1)}, bf16[257,640]{1,0:T(8,128)(2,1)S(1)}) custom-call(s32[4]{0:T(128)S(1)} %pad_add_fusion.where, bf16[257,640]{1,0:T(8,128)(2,1)S(1)} %add_convert_fusion.1.chip, bf16[257,640]{1,0:T(8,128)(2,1)S(1)} %collective-permute-done.7.far, ...), custom_call_target="tpu_custom_call" | custom-call | flops 800688640 | bytes 9070624 | tf_op jit(solution)/shard_map/pallas_call | solution.py:36
  41.3 1.1 shard_map.72
  44.0 8.9 %collective-permute-done.11.far = bf16[257,640]{1,0:T(8,128)(2,1)S(1)} collective-permute-done((bf16[257,640]{1,0:T(8,128)(2,1)S(1)}, bf16[257,640]{1,0:T(8,128)(2,1)S(1)}, u32[]{:S(2)}, u32[]{:S(2)}) %collective-permute-start.11) | collective-permute-done | bytes 328992 | tf_op jit(solution)/shard_map/ppermute | solution.py:237
  53.0 1.6 %collective-permute-done.13.far_c = bf16[257,640]{1,0:T(8,128)(2,1)S(1)} collective-permute-done((bf16[257,640]{1,0:T(8,128)(2,1)S(1)}, bf16[257,640]{1,0:T(8,128)(2,1)S(1)}, u32[]{:S(2)}, u32[]{:S(2)}) %collective-permute-start.13) | collective-permute-done | bytes 328992 | tf_op jit(solution)/shard_map/ppermute | solution.py:238
  54.6 4.4 %shard_map.73 = (f32[257,320]{1,0:T(8,128)S(1)}, bf16[257,960]{1,0:T(8,128)(2,1)S(1)}, bf16[257,1280]{1,0:T(8,128)(2,1)S(1)}) custom-call(s32[4]{0:T(128)S(1)} %pad_add_fusion.where, bf16[257,640]{1,0:T(8,128)(2,1)S(1)} %add_convert_fusion.chip, bf16[257,640]{1,0:T(8,128)(2,1)S(1)} %collective-permute-done.11.far, ...), custom_call_target="tpu_custom_call" | custom-call | flops 379619840 | bytes 8257824 | tf_op jit(solution)/shard_map/pallas_call | solution.py:36
  60.0 1.8 %collective-permute-start.14 = (bf16[640,384]{1,0:T(8,128)(2,1)S(1)}, bf16[640,384]{1,0:T(8,128)(2,1)S(1)}, u32[]{:S(2)}, u32[]{:S(2)}) collective-permute-start(bf16[640,384]{1,0:T(8,128)(2,1)S(1)} %shard_map.75), channel_id=1, source_target_pairs={{0,64},{64,0},{128,192},{192,128},{1,65},{65,1},{129,193},{193,129... | collective-permute-start | bytes 1474568 | tf_op jit(solution)/shard_map/ppermute | solution.py:333
  62.9 2.2 %collective-permute-start.17 = (bf16[640,512]{1,0:T(8,128)(2,1)S(1)}, bf16[640,512]{1,0:T(8,128)(2,1)S(1)}, u32[]{:S(2)}, u32[]{:S(2)}) collective-permute-start(bf16[640,512]{1,0:T(8,128)(2,1)S(1)} %shard_map.77), channel_id=1, source_target_pairs={{0,192},{64,128},{128,64},{192,0},{1,193},{65,129},{129,65},{193,1... | collective-permute-start | bytes 1966088 | tf_op jit(solution)/shard_map/ppermute | solution.py:333
  65.9 1.3 %shard_map.80 = bf16[640,384]{1,0:T(8,128)(2,1)S(1)} custom-call(s32[4]{0:T(128)S(1)} %pad_add_fusion.where, bf16[1280,257]{1,0:T(8,128)(2,1)S(1)} %get-tuple-element.41.xt, bf16[1280,257]{1,0:T(8,128)(2,1)S(1)} %shard_map.78.tt, bf16[257,960]{1,0:T(8,128)(2,1)S(1)} %get-tuple-element.42.grads, bf16[257,320]{1,0:T(8,128)(2,1)S(1)} %get-tuple-element.44.att), custom_call_target="tpu_custom_call" | custom-call | flops 126320640 | bytes 2465296 | tf_op jit(solution)/shard_map/pallas_call | solution.py:36
  68.9 1.3 %shard_map.79 = bf16[640,384]{1,0:T(8,128)(2,1)S(1)} custom-call(s32[4]{0:T(128)S(1)} %pad_add_fusion.where, bf16[1280,257]{1,0:T(8,128)(2,1)S(1)} %get-tuple-element.41.xt, bf16[1280,257]{1,0:T(8,128)(2,1)S(1)} %shard_map.78.tt, bf16[257,960]{1,0:T(8,128)(2,1)S(1)} %get-tuple-element.42.grads, bf16[257,320]{1,0:T(8,128)(2,1)S(1)} %get-tuple-element.44.att), custom_call_target="tpu_custom_call" | custom-call | flops 126320640 | bytes 2465296 | tf_op jit(solution)/shard_map/pallas_call | solution.py:36
  71.3 2.3 %collective-permute-done.14 = bf16[640,384]{1,0:T(8,128)(2,1)S(1)} collective-permute-done((bf16[640,384]{1,0:T(8,128)(2,1)S(1)}, bf16[640,384]{1,0:T(8,128)(2,1)S(1)}, u32[]{:S(2)}, u32[]{:S(2)}) %collective-permute-start.14) | collective-permute-done | bytes 491552 | tf_op jit(solution)/shard_map/ppermute | solution.py:333
  73.7 2.8 %collective-permute-start.15 = (bf16[320,384]{1,0:T(8,128)(2,1)S(1)}, bf16[320,384]{1,0:T(8,128)(2,1)S(1)}, u32[]{:S(2)}, u32[]{:S(2)}) collective-permute-start(bf16[320,384]{1,0:T(8,128)(2,1)S(1)} %add_convert_fusion.4), channel_id=1, source_target_pairs={{0,192},{64,128},{128,64},{192,0},{1,193},{65,129},{129,65},{193,1... | collective-permute-start | bytes 737288 | tf_op jit(solution)/shard_map/ppermute | solution.py:333
  76.5 5.3 %collective-permute-done.17 = bf16[640,512]{1,0:T(8,128)(2,1)S(1)} collective-permute-done((bf16[640,512]{1,0:T(8,128)(2,1)S(1)}, bf16[640,512]{1,0:T(8,128)(2,1)S(1)}, u32[]{:S(2)}, u32[]{:S(2)}) %collective-permute-start.17) | collective-permute-done | bytes 655392 | tf_op jit(solution)/shard_map/ppermute | solution.py:333
  82.8 3.2 %collective-permute-done.15 = bf16[320,384]{1,0:T(8,128)(2,1)S(1)} collective-permute-done((bf16[320,384]{1,0:T(8,128)(2,1)S(1)}, bf16[320,384]{1,0:T(8,128)(2,1)S(1)}, u32[]{:S(2)}, u32[]{:S(2)}) %collective-permute-start.15) | collective-permute-done | bytes 245792 | tf_op jit(solution)/shard_map/ppermute | solution.py:333
  86.8 5.5 %collective-permute-done.18 = bf16[320,512]{1,0:T(8,128)(2,1)S(1)} collective-permute-done((bf16[320,512]{1,0:T(8,128)(2,1)S(1)}, bf16[320,512]{1,0:T(8,128)(2,1)S(1)}, u32[]{:S(2)}, u32[]{:S(2)}) %collective-permute-start.18) | collective-permute-done | bytes 327712 | tf_op jit(solution)/shard_map/ppermute | solution.py:336
  92.6 2.2 %collective-permute-start.22 = (bf16[160,384]{1,0:T(8,128)(2,1)S(1)}, bf16[160,384]{1,0:T(8,128)(2,1)S(1)}, u32[]{:S(2)}, u32[]{:S(2)}) collective-permute-start(bf16[160,384]{1,0:T(8,128)(2,1)S(1)} %get-tuple-element.52), channel_id=1, source_target_pairs={{0,192},{64,128},{128,64},{192,0},{1,193},{65,129},{129,65},{193,1... | collective-permute-start | bytes 368648 | tf_op jit(solution)/shard_map/ppermute | solution.py:333
  94.8 4.0 %collective-permute-done.22.g3 = bf16[160,384]{1,0:T(8,128)(2,1)S(1)} collective-permute-done((bf16[160,384]{1,0:T(8,128)(2,1)S(1)}, bf16[160,384]{1,0:T(8,128)(2,1)S(1)}, u32[]{:S(2)}, u32[]{:S(2)}) %collective-permute-start.22) | collective-permute-done | bytes 122912 | tf_op jit(solution)/shard_map/ppermute | solution.py:333
  98.8 1.5 %shard_map.81 = bf16[8,200,128]{2,1,0:T(8,128)(2,1)} custom-call(s32[4]{0:T(128)S(1)} %pad_add_fusion.where, bf16[160,384]{1,0:T(8,128)(2,1)S(1)} %get-tuple-element.55.k1, bf16[160,384]{1,0:T(8,128)(2,1)S(1)} %collective-permute-done.16.g1, bf16[160,512]{1,0:T(8,128)(2,1)S(1)} %get-tuple-element.51.k2, bf16[160,512]{1,0:T(8,128)(2,1)S(1)} %collective-permute-done.19.g2, ...), custom_call_target="tpu_custom_call" | custom-call | flops 204800 | bytes 1228816 | tf_op jit(solution)/shard_map/pallas_call | solution.py:36
  100.3 8.5 %all-to-all-start = ((bf16[8,200,128]{2,1,0:T(8,128)(2,1)}), bf16[8,200,128]{2,1,0:T(8,128)(2,1)S(1)}, u32[]{:S(2)}, u32[]{:S(2)}) async-start(bf16[8,200,128]{2,1,0:T(8,128)(2,1)} %shard_map.81), calls=%async_computation | async-start | bytes 819200 | tf_op jit(solution)/shard_map/all_to_all | solution.py:373
  108.8 1.2 copy.7
  109.9 10.9 %all-to-all-done.got = bf16[8,200,128]{2,1,0:T(8,128)(2,1)S(1)} async-done(((bf16[8,200,128]{2,1,0:T(8,128)(2,1)}), bf16[8,200,128]{2,1,0:T(8,128)(2,1)S(1)}, u32[]{:S(2)}, u32[]{:S(2)}) %all-to-all-start) | async-done | bytes 409632 | tf_op jit(solution)/shard_map/all_to_all | solution.py:373
  120.9 1.3 %shard_map.82 = (f32[3,20,320]{2,1,0:T(8,128)}, f32[20,320]{1,0:T(8,128)}) custom-call(s32[4]{0:T(128)S(1)} %pad_add_fusion.where, bf16[8,200,128]{2,1,0:T(8,128)(2,1)S(1)} %all-to-all-done.got), custom_call_target="tpu_custom_call" | custom-call | flops 204800 | bytes 512016 | tf_op jit(solution)/shard_map/pallas_call | solution.py:36
  (49 shorter events, 13.8 us)
Async XLA Ops:
  0.6 8.4 %copy-start.2 = (bf16[1,257,320]{2,1,0:T(8,128)(2,1)S(1)}, bf16[1,257,320]{2,1,0:T(8,128)(2,1)}, u32[]{:S(2)}) copy-start(bf16[1,257,320]{2,1,0:T(8,128)(2,1)} %param.4) | copy-start | bytes 493444
  0.6 7.1 %collective-permute-start = (bf16[257,320]{1,0:T(8,128)(2,1)}, bf16[257,320]{1,0:T(8,128)(2,1)S(1)}, u32[]{:S(2)}, u32[]{:S(2)}) collective-permute-start(bf16[257,320]{1,0:T(8,128)(2,1)} %bitcast.15), channel_id=1, source_target_pairs={{0,2},{2,0},{1,3},{3,1},{4,6},{6,4},{5,7},{7,5},{8,10},{10,8},{9,1... | collective-permute-start | bytes 493448 | tf_op jit(solution)/shard_map/ppermute | solution.py:257
  3.1 1.7 %copy-start = (bf16[3,1280,320]{1,2,0:T(8,128)(2,1)S(1)}, bf16[3,1280,320]{1,2,0:T(8,128)(2,1)}, u32[]{:S(2)}) copy-start(bf16[3,1280,320]{1,2,0:T(8,128)(2,1)} %param.6) | copy-start | bytes 7372804
  4.8 1.1 copy-start.1
  7.7 6.2 %collective-permute-start.1 = (bf16[257,320]{1,0:T(8,128)(2,1)S(1)}, bf16[257,320]{1,0:T(8,128)(2,1)S(1)}, u32[]{:S(2)}, u32[]{:S(2)}) collective-permute-start(bf16[257,320]{1,0:T(8,128)(2,1)S(1)} %get-tuple-element.26.t0), channel_id=1, source_target_pairs={{0,2},{2,0},{1,3},{3,1},{4,6},{6,4},{5,7},{7,5},{8,10},{10,8},{9,1... | collective-permute-start | bytes 493448 | tf_op jit(solution)/shard_map/ppermute | solution.py:268
  9.0 4.9 %collective-permute-start.4 = (bf16[257,320]{1,0:T(8,128)(2,1)S(1)}, bf16[257,320]{1,0:T(8,128)(2,1)S(1)}, u32[]{:S(2)}, u32[]{:S(2)}) collective-permute-start(bf16[257,320]{1,0:T(8,128)(2,1)S(1)} %bitcast.16), channel_id=1, source_target_pairs={{0,1},{1,0},{2,3},{3,2},{4,5},{5,4},{6,7},{7,6},{8,9},{9,8},{10,11... | collective-permute-start | bytes 493448 | tf_op jit(solution)/shard_map/ppermute | solution.py:258
  9.0 4.9 %collective-permute-start.5 = (bf16[257,320]{1,0:T(8,128)(2,1)S(1)}, bf16[257,320]{1,0:T(8,128)(2,1)S(1)}, u32[]{:S(2)}, u32[]{:S(2)}) collective-permute-start(bf16[257,320]{1,0:T(8,128)(2,1)S(1)} %collective-permute-done.zy), channel_id=1, source_target_pairs={{0,1},{1,0},{2,3},{3,2},{4,5},{5,4},{6,7},{7,6},{8,9},{9,8},{10,11... | collective-permute-start | bytes 493448 | tf_op jit(solution)/shard_map/ppermute | solution.py:267
  9.5 8.2 %collective-permute-start.2 = (bf16[257,320]{1,0:T(8,128)(2,1)S(1)}, bf16[257,320]{1,0:T(8,128)(2,1)S(1)}, u32[]{:S(2)}, u32[]{:S(2)}) collective-permute-start(bf16[257,320]{1,0:T(8,128)(2,1)S(1)} %get-tuple-element.26.t0), channel_id=1, source_target_pairs={{0,1},{1,0},{2,3},{3,2},{4,5},{5,4},{6,7},{7,6},{8,9},{9,8},{10,11... | collective-permute-start | bytes 493448 | tf_op jit(solution)/shard_map/ppermute | solution.py:265
  13.9 3.8 %collective-permute-start.3 = (bf16[257,320]{1,0:T(8,128)(2,1)S(1)}, bf16[257,320]{1,0:T(8,128)(2,1)S(1)}, u32[]{:S(2)}, u32[]{:S(2)}) collective-permute-start(bf16[257,320]{1,0:T(8,128)(2,1)S(1)} %collective-permute-done.1.ty), channel_id=1, source_target_pairs={{0,1},{1,0},{2,3},{3,2},{4,5},{5,4},{6,7},{7,6},{8,9},{9,8},{10,11... | collective-permute-start | bytes 493448 | tf_op jit(solution)/shard_map/ppermute | solution.py:269
  22.3 2.0 %collective-permute-start.6 = (bf16[257,640]{1,0:T(8,128)(2,1)S(1)}, bf16[257,640]{1,0:T(8,128)(2,1)S(1)}, u32[]{:S(2)}, u32[]{:S(2)}) collective-permute-start(bf16[257,640]{1,0:T(8,128)(2,1)S(1)} %get-tuple-element.33), channel_id=1, source_target_pairs={{0,1},{1,0},{2,3},{3,2},{4,5},{5,4},{6,7},{7,6},{8,9},{9,8},{10,11... | collective-permute-start | bytes 986888 | tf_op jit(solution)/shard_map/ppermute | solution.py:236
  24.4 10.3 %collective-permute-start.7 = (bf16[257,640]{1,0:T(8,128)(2,1)S(1)}, bf16[257,640]{1,0:T(8,128)(2,1)S(1)}, u32[]{:S(2)}, u32[]{:S(2)}) collective-permute-start(bf16[257,640]{1,0:T(8,128)(2,1)S(1)} %add_convert_fusion.1.chip), channel_id=1, source_target_pairs={{0,2},{2,0},{1,3},{3,1},{4,6},{6,4},{5,7},{7,5},{8,10},{10,8},{9,1... | collective-permute-start | bytes 986888 | tf_op jit(solution)/shard_map/ppermute | solution.py:237
  25.5 9.2 %collective-permute-start.8 = (bf16[257,640]{1,0:T(8,128)(2,1)S(1)}, bf16[257,640]{1,0:T(8,128)(2,1)S(1)}, u32[]{:S(2)}, u32[]{:S(2)}) collective-permute-start(bf16[257,640]{1,0:T(8,128)(2,1)S(1)} %add_convert_fusion.1.chip), channel_id=1, source_target_pairs={{0,1},{1,0},{2,3},{3,2},{4,5},{5,4},{6,7},{7,6},{8,9},{9,8},{10,11... | collective-permute-start | bytes 986888 | tf_op jit(solution)/shard_map/ppermute | solution.py:238
  34.7 1.6 %collective-permute-start.9 = (bf16[257,640]{1,0:T(8,128)(2,1)S(1)}, bf16[257,640]{1,0:T(8,128)(2,1)S(1)}, u32[]{:S(2)}, u32[]{:S(2)}) collective-permute-start(bf16[257,640]{1,0:T(8,128)(2,1)S(1)} %collective-permute-done.7.far), channel_id=1, source_target_pairs={{0,1},{1,0},{2,3},{3,2},{4,5},{5,4},{6,7},{7,6},{8,9},{9,8},{10,11... | collective-permute-start | bytes 986888 | tf_op jit(solution)/shard_map/ppermute | solution.py:238
  41.1 1.7 %collective-permute-start.10 = (bf16[257,640]{1,0:T(8,128)(2,1)S(1)}, bf16[257,640]{1,0:T(8,128)(2,1)S(1)}, u32[]{:S(2)}, u32[]{:S(2)}) collective-permute-start(bf16[257,640]{1,0:T(8,128)(2,1)S(1)} %get-tuple-element.37), channel_id=1, source_target_pairs={{0,1},{1,0},{2,3},{3,2},{4,5},{5,4},{6,7},{7,6},{8,9},{9,8},{10,11... | collective-permute-start | bytes 986888 | tf_op jit(solution)/shard_map/ppermute | solution.py:236
  42.9 10.1 %collective-permute-start.11 = (bf16[257,640]{1,0:T(8,128)(2,1)S(1)}, bf16[257,640]{1,0:T(8,128)(2,1)S(1)}, u32[]{:S(2)}, u32[]{:S(2)}) collective-permute-start(bf16[257,640]{1,0:T(8,128)(2,1)S(1)} %add_convert_fusion.chip), channel_id=1, source_target_pairs={{0,2},{2,0},{1,3},{3,1},{4,6},{6,4},{5,7},{7,5},{8,10},{10,8},{9,1... | collective-permute-start | bytes 986888 | tf_op jit(solution)/shard_map/ppermute | solution.py:237
  44.0 9.0 %collective-permute-start.12 = (bf16[257,640]{1,0:T(8,128)(2,1)S(1)}, bf16[257,640]{1,0:T(8,128)(2,1)S(1)}, u32[]{:S(2)}, u32[]{:S(2)}) collective-permute-start(bf16[257,640]{1,0:T(8,128)(2,1)S(1)} %add_convert_fusion.chip), channel_id=1, source_target_pairs={{0,1},{1,0},{2,3},{3,2},{4,5},{5,4},{6,7},{7,6},{8,9},{9,8},{10,11... | collective-permute-start | bytes 986888 | tf_op jit(solution)/shard_map/ppermute | solution.py:238
  53.0 1.6 %collective-permute-start.13 = (bf16[257,640]{1,0:T(8,128)(2,1)S(1)}, bf16[257,640]{1,0:T(8,128)(2,1)S(1)}, u32[]{:S(2)}, u32[]{:S(2)}) collective-permute-start(bf16[257,640]{1,0:T(8,128)(2,1)S(1)} %collective-permute-done.11.far), channel_id=1, source_target_pairs={{0,1},{1,0},{2,3},{3,2},{4,5},{5,4},{6,7},{7,6},{8,9},{9,8},{10,11... | collective-permute-start | bytes 986888 | tf_op jit(solution)/shard_map/ppermute | solution.py:238
  60.0 13.6 %collective-permute-start.14 = (bf16[640,384]{1,0:T(8,128)(2,1)S(1)}, bf16[640,384]{1,0:T(8,128)(2,1)S(1)}, u32[]{:S(2)}, u32[]{:S(2)}) collective-permute-start(bf16[640,384]{1,0:T(8,128)(2,1)S(1)} %shard_map.75), channel_id=1, source_target_pairs={{0,64},{64,0},{128,192},{192,128},{1,65},{65,1},{129,193},{193,129... | collective-permute-start | bytes 1474568 | tf_op jit(solution)/shard_map/ppermute | solution.py:333
  62.9 18.9 %collective-permute-start.17 = (bf16[640,512]{1,0:T(8,128)(2,1)S(1)}, bf16[640,512]{1,0:T(8,128)(2,1)S(1)}, u32[]{:S(2)}, u32[]{:S(2)}) collective-permute-start(bf16[640,512]{1,0:T(8,128)(2,1)S(1)} %shard_map.77), channel_id=1, source_target_pairs={{0,192},{64,128},{128,64},{192,0},{1,193},{65,129},{129,65},{193,1... | collective-permute-start | bytes 1966088 | tf_op jit(solution)/shard_map/ppermute | solution.py:333
  67.2 15.4 %collective-permute-start.20 = (bf16[640,384]{1,0:T(8,128)(2,1)S(1)}, bf16[640,384]{1,0:T(8,128)(2,1)S(1)}, u32[]{:S(2)}, u32[]{:S(2)}) collective-permute-start(bf16[640,384]{1,0:T(8,128)(2,1)S(1)} %shard_map.80), channel_id=1, source_target_pairs={{0,32},{32,0},{1,33},{33,1},{2,34},{34,2},{3,35},{35,3},{4,36},{36... | collective-permute-start | bytes 1474568 | tf_op jit(solution)/shard_map/ppermute | solution.py:336
  73.7 12.3 %collective-permute-start.15 = (bf16[320,384]{1,0:T(8,128)(2,1)S(1)}, bf16[320,384]{1,0:T(8,128)(2,1)S(1)}, u32[]{:S(2)}, u32[]{:S(2)}) collective-permute-start(bf16[320,384]{1,0:T(8,128)(2,1)S(1)} %add_convert_fusion.4), channel_id=1, source_target_pairs={{0,192},{64,128},{128,64},{192,0},{1,193},{65,129},{129,65},{193,1... | collective-permute-start | bytes 737288 | tf_op jit(solution)/shard_map/ppermute | solution.py:333
  81.9 10.4 %collective-permute-start.18 = (bf16[320,512]{1,0:T(8,128)(2,1)S(1)}, bf16[320,512]{1,0:T(8,128)(2,1)S(1)}, u32[]{:S(2)}, u32[]{:S(2)}) collective-permute-start(bf16[320,512]{1,0:T(8,128)(2,1)S(1)} %add_convert_fusion.2), channel_id=1, source_target_pairs={{0,32},{32,0},{1,33},{33,1},{2,34},{34,2},{3,35},{35,3},{4,36},{36... | collective-permute-start | bytes 983048 | tf_op jit(solution)/shard_map/ppermute | solution.py:336
  82.7 9.9 %collective-permute-start.21 = (bf16[320,384]{1,0:T(8,128)(2,1)S(1)}, bf16[320,384]{1,0:T(8,128)(2,1)S(1)}, u32[]{:S(2)}, u32[]{:S(2)}) collective-permute-start(bf16[320,384]{1,0:T(8,128)(2,1)S(1)} %add_convert_fusion.3), channel_id=1, source_target_pairs={{0,64},{64,0},{128,192},{192,128},{1,65},{65,1},{129,193},{193,129... | collective-permute-start | bytes 737288 | tf_op jit(solution)/shard_map/ppermute | solution.py:333
  86.0 8.8 %collective-permute-start.16 = (bf16[160,384]{1,0:T(8,128)(2,1)S(1)}, bf16[160,384]{1,0:T(8,128)(2,1)S(1)}, u32[]{:S(2)}, u32[]{:S(2)}) collective-permute-start(bf16[160,384]{1,0:T(8,128)(2,1)S(1)} %get-tuple-element.54), channel_id=1, source_target_pairs={{0,32},{32,0},{1,33},{33,1},{2,34},{34,2},{3,35},{35,3},{4,36},{36... | collective-permute-start | bytes 368648 | tf_op jit(solution)/shard_map/ppermute | solution.py:336
  92.4 6.4 %collective-permute-start.19 = (bf16[160,512]{1,0:T(8,128)(2,1)S(1)}, bf16[160,512]{1,0:T(8,128)(2,1)S(1)}, u32[]{:S(2)}, u32[]{:S(2)}) collective-permute-start(bf16[160,512]{1,0:T(8,128)(2,1)S(1)} %get-tuple-element.50), channel_id=1, source_target_pairs={{0,64},{64,0},{128,192},{192,128},{1,65},{65,1},{129,193},{193,129... | collective-permute-start | bytes 491528 | tf_op jit(solution)/shard_map/ppermute | solution.py:333
  92.6 6.2 %collective-permute-start.22 = (bf16[160,384]{1,0:T(8,128)(2,1)S(1)}, bf16[160,384]{1,0:T(8,128)(2,1)S(1)}, u32[]{:S(2)}, u32[]{:S(2)}) collective-permute-start(bf16[160,384]{1,0:T(8,128)(2,1)S(1)} %get-tuple-element.52), channel_id=1, source_target_pairs={{0,192},{64,128},{128,64},{192,0},{1,193},{65,129},{129,65},{193,1... | collective-permute-start | bytes 368648 | tf_op jit(solution)/shard_map/ppermute | solution.py:333
  100.3 20.5 %all-to-all-start = ((bf16[8,200,128]{2,1,0:T(8,128)(2,1)}), bf16[8,200,128]{2,1,0:T(8,128)(2,1)S(1)}, u32[]{:S(2)}, u32[]{:S(2)}) async-start(bf16[8,200,128]{2,1,0:T(8,128)(2,1)} %shard_map.81), calls=%async_computation | async-start | bytes 819200 | tf_op jit(solution)/shard_map/all_to_all | solution.py:373

commit v3 on v2

--- a/solution.py
+++ b/solution.py
@@ -31,12 +31,11 @@
 
 def call(body, outs, ins, scratch=(), flops=0):
     vmem = pl.BlockSpec(memory_space=pltpu.VMEM)
-    smem = pl.BlockSpec(memory_space=pltpu.SMEM)
     size = sum(math.prod(o.shape) * o.dtype.itemsize for o in list(outs) + list(ins))
     return pl.pallas_call(
         body,
         out_shape=outs,
-        in_specs=[smem] + [vmem] * (len(ins) - 1),
+        in_specs=[vmem] * len(ins),
         out_specs=[vmem] * len(outs),
         scratch_shapes=list(scratch),
         compiler_params=pltpu.CompilerParams(vmem_limit_bytes=20 * 2**20),
@@ -48,35 +47,42 @@
     return jax.ShapeDtypeStruct(shape, dtype)
 
 
-def prepare_body(where, cot, w, w_out, cot_o, w_o, w_out_o):
-    narrow = w_out.shape[0]
-    cot_o[...] = cot[...].astype(bf16)
+def reordered(dst, rows, src, narrow):
     for c in range(2):
 
-        @pl.when(where[1] == c)
+        @pl.when(lax.axis_index("c") == c)
         def _():
             for k, core in enumerate((c, 1 - c)):
                 for y in range(2):
-                    src = (2 * y + core) * narrow
-                    at = (2 * k + y) * narrow
-                    w_out_o[:, at : at + narrow] = w_out[:, src : src + narrow]
-                    for s in range(3):
-                        w_o[s * narrow : (s + 1) * narrow, at : at + narrow] = w[s, :, src : src + narrow]
-
-
-def put_pieces(where, spot, mine, y, core, both):
+                    old = (2 * y + core) * narrow
+                    new = (2 * k + y) * narrow
+                    dst[rows, new : new + narrow] = src[:, old : old + narrow]
+
+
+def prepare_body(cot, w, cot_o, w_o):
+    narrow = cot.shape[1]
+    cot_o[...] = cot[...].astype(bf16)
+    for s in range(3):
+        reordered(w_o, slice(s * narrow, (s + 1) * narrow), w.at[s], narrow)
+
+
+def prepare_out_body(w_out, w_out_o):
+    reordered(w_out_o, slice(None), w_out, w_out.shape[0])
+
+
+def put_pieces(spot, mine, y, core, both):
     narrow = mine.shape[1]
     for yl in range(2):
 
-        @pl.when(where[0] == yl)
+        @pl.when(lax.axis_index("yl") == yl)
         def _():
             for k, (near, far) in enumerate(((mine, y), (core, both))):
                 for at, piece in ((2 * k + yl, near), (2 * k + 1 - yl, far)):
                     spot[:, at * narrow : (at + 1) * narrow] = piece[...]
 
 
-def forward_body(where, z0, zy, zc, zcy, w, normal_o, xt_o, inv_o, qkv_o, probs_o, att_o, zs):
-    put_pieces(where, zs, z0, zy, zc, zcy)
+def forward_body(z0, zy, zc, zcy, w, normal_o, xt_o, inv_o, qkv_o, probs_o, att_o, zs):
+    put_pieces(zs, z0, zy, zc, zcy)
     width = zs.shape[1]
     narrow = width // 4
     values = zs[...].astype(f32)
@@ -89,35 +95,34 @@
         got = dot(normal_o[...], w[s * narrow : (s + 1) * narrow, :], COLS).astype(bf16)
         for h in range(heads):
             qkv_o[s * heads + h] = got[:, h * HD : (h + 1) * HD]
+    xt_o[...] = normal_o[...].T
+    scores = [dot(qkv_o[h], qkv_o[heads + h], COLS) * SCALE for h in range(heads)]
     for h in range(heads):
-        scores = dot(qkv_o[h], qkv_o[heads + h], COLS) * SCALE
-        top = jnp.max(scores, axis=-1, keepdims=True)
-        e = jnp.exp(scores - top)
-        probs = e / jnp.sum(e, axis=-1, keepdims=True)
-        probs_o[h] = probs
-        att_o[:, h * HD : (h + 1) * HD] = dot(probs.astype(bf16), qkv_o[2 * heads + h]).astype(bf16)
-    xt_o[...] = normal_o[...].T
+        e = jnp.exp(scores[h] - jnp.max(scores[h], axis=-1, keepdims=True))
+        probs_o[h] = e / jnp.sum(e, axis=-1, keepdims=True)
+    for h in range(heads):
+        att_o[:, h * HD : (h + 1) * HD] = dot(probs_o[h].astype(bf16), qkv_o[2 * heads + h]).astype(bf16)
 
 
 def attention_back(cot, w_out, qkv, probs, grads):
     narrow = w_out.shape[0]
     heads = narrow // HD
     att = dot(cot, w_out[...], COLS).astype(bf16)
+    each = [att[:, h * HD : (h + 1) * HD] for h in range(heads)]
+
+    def put(s, h, got):
+        at = s * narrow + h * HD
+        grads[:, at : at + HD] = got.astype(bf16)
+
+    dps = [dot(each[h], qkv[2 * heads + h], COLS) for h in range(heads)]
     for h in range(heads):
-        a = att[:, h * HD : (h + 1) * HD]
+        put(2, h, dot(probs[h].astype(bf16), each[h], ROWS))
+    for h in range(heads):
         p = probs[h]
-        dp = dot(a, qkv[2 * heads + h], COLS)
-        along = jnp.sum(p * dp, axis=-1, keepdims=True)
-        ds = (p * (dp - along) * SCALE).astype(bf16)
-        for s, got in enumerate(
-            (
-                dot(ds, qkv[heads + h]),
-                dot(ds, qkv[h], ROWS),
-                dot(p.astype(bf16), a, ROWS),
-            )
-        ):
-            at = s * narrow + h * HD
-            grads[:, at : at + HD] = got.astype(bf16)
+        along = jnp.sum(p * dps[h], axis=-1, keepdims=True)
+        ds = (p * (dps[h] - along) * SCALE).astype(bf16)
+        put(0, h, dot(ds, qkv[heads + h]))
+        put(1, h, dot(ds, qkv[h], ROWS))
 
 
 def input_back(half, grads, w):
@@ -125,13 +130,13 @@
     return dot(grads[...], w[:, half * wide : (half + 1) * wide]).astype(bf16)
 
 
-def first_body(where, t0, ty, tc, tcy, w_out, qkv, probs, w, cot_o, grads_o, oth_o):
-    put_pieces(where, cot_o, t0, ty, tc, tcy)
+def first_body(t0, ty, tc, tcy, w_out, qkv, probs, w, cot_o, grads_o, oth_o):
+    put_pieces(cot_o, t0, ty, tc, tcy)
     attention_back(cot_o[...], w_out, qkv, probs, grads_o)
     oth_o[...] = input_back(OTHER, grads_o, w)
 
 
-def own_body(where, grads, w, own_o):
+def own_body(grads, w, own_o):
     own_o[...] = input_back(MINE, grads, w)
 
 
@@ -147,18 +152,18 @@
     return (g - mean - n * along) * inv[:, :1]
 
 
-def middle_body(where, chip, far, chip_c, far_c, normal, inv, w_out, qkv, probs, w, term_o, grads_o, oth_o):
+def middle_body(chip, far, chip_c, far_c, normal, inv, w_out, qkv, probs, w, term_o, grads_o, oth_o):
     term_o[...] = put_term(term_o, chip, far, chip_c, far_c, normal, inv)
     attention_back(term_o[...].astype(bf16), w_out, qkv, probs, grads_o)
     oth_o[...] = input_back(OTHER, grads_o, w)
 
 
-def last_body(where, chip, far, chip_c, far_c, normal, inv, w_out, qkv, probs, cot, term, mine, imp_o, grads_o, total_o, spot):
+def last_body(chip, far, chip_c, far_c, normal, inv, w_out, qkv, probs, cot, term, mine, imp_o, grads_o, total_o, spot):
     spot[...] = put_term(spot, chip, far, chip_c, far_c, normal, inv) + term[...]
     narrow = mine.shape[1]
     for yl in range(2):
 
-        @pl.when(where[0] == yl)
+        @pl.when(lax.axis_index("yl") == yl)
         def _():
             imp_o[...] = mine[...] + spot[:, yl * narrow : (yl + 1) * narrow]
 
@@ -167,40 +172,40 @@
     attention_back(total, w_out, qkv, probs, grads_o)
 
 
-def spot_of(where, x, narrow):
-    other = lax.rem(x + where[1], 2)
+def spot_of(x, narrow):
+    other = lax.rem(x + lax.axis_index("c"), 2)
     return (2 * other + lax.div(x, 2)) * narrow
 
 
-def gather_rows(where, src, dst, picks, narrow):
+def gather_rows(src, dst, picks, narrow):
     rows = narrow // 2
     for i, (dx, dy) in enumerate(picks):
-        at = spot_of(where, lax.bitwise_xor(where[2], dx), narrow)
-        at = at + lax.bitwise_xor(where[3], dy) * rows
+        at = spot_of(lax.bitwise_xor(lax.axis_index("x"), dx), narrow)
+        at = at + lax.bitwise_xor(lax.axis_index("yh"), dy) * rows
         dst[i * rows : (i + 1) * rows, :] = src[pl.ds(pl.multiple_of(at, 16), rows), :]
 
 
-def rows_body(picks, first, where, xt, grads, out, xs):
-    gather_rows(where, xt, xs, picks, grads.shape[1] // 3)
+def rows_body(picks, first, xt, grads, out, xs):
+    gather_rows(xt, xs, picks, grads.shape[1] // 3)
     out[...] = dot(xs[...], grads[:, first : first + out.shape[1]]).astype(bf16)
 
 
-def turn_body(where, total, tt_o):
+def turn_body(total, tt_o):
     tt_o[...] = total[...].T
 
 
-def tail_rows_body(picks, where, xt, tt, grads, att, out, xs):
+def tail_rows_body(picks, xt, tt, grads, att, out, xs):
     narrow = att.shape[1]
     left = out.shape[1] - narrow
-    gather_rows(where, xt, xs, picks, narrow)
+    gather_rows(xt, xs, picks, narrow)
     one = dot(xs[...], grads[:, grads.shape[1] - left :])
-    gather_rows(where, tt, xs, picks, narrow)
+    gather_rows(tt, xs, picks, narrow)
     two = dot(xs[...], att[...])
     out[:, :left] = one.astype(bf16)
     out[:, left:] = two.astype(bf16)
 
 
-def pack_body(where, k1, g1, k2, g2, k3, g3, out, spot):
+def pack_body(k1, g1, k2, g2, k3, g3, out, spot):
     at = 0
     for k, g in ((k1, g1), (k2, g2), (k3, g3)):
         spot[:, at : at + k.shape[1]] = k[...].astype(f32) + g[...].astype(f32)
@@ -213,7 +218,7 @@
             out[z, b * each : (b + 1) * each, :] = piece.astype(bf16)
 
 
-def unpack_body(factor, where, got, qkv_o, out_o, spot):
+def unpack_body(factor, got, qkv_o, out_o, spot):
     total = got[0].astype(f32)
     for z in range(1, got.shape[0]):
         total = total + got[z].astype(f32)
@@ -243,8 +248,6 @@
     width = 4 * narrow
     heads = narrow // HD
     nx, ny, nz = [lax.axis_size(a) for a in DP]
-    x, yh = lax.axis_index("x"), lax.axis_index("yh")
-    where = jnp.stack([lax.axis_index("yl"), lax.axis_index("c"), x, yh]).astype(jnp.int32)
 
     wide = like((tokens, width), bf16)
     wide_f = like((tokens, width), f32)
@@ -256,14 +259,14 @@
     z0 = z_star[0]
     zy = lax.ppermute(z0, "yl", SWAP)
     zc = lax.ppermute(z0, "c", SWAP)
-    t0, w, wo = call(
+    t0, w = call(
         prepare_body,
-        (like((tokens, narrow), bf16), like((3 * narrow, width), bf16), like((narrow, width), bf16)),
-        (where, cotangent[0], jnp.swapaxes(w_qkv, 1, 2), w_out),
+        (like((tokens, narrow), bf16), like((3 * narrow, width), bf16)),
+        (cotangent[0], jnp.swapaxes(w_qkv, 1, 2)),
         flops=proj,
     )
+    (wo,) = call(prepare_out_body, (like((narrow, width), bf16),), (w_out,), flops=proj)
     tc = lax.ppermute(t0, "c", SWAP)
-    zy, t0 = lax.optimization_barrier((zy, t0))
     zcy = lax.ppermute(zy, "c", SWAP)
     ty = lax.ppermute(t0, "yl", SWAP)
     tcy = lax.ppermute(ty, "c", SWAP)
@@ -277,32 +280,32 @@
             like((heads, tokens, tokens), f32),
             like((tokens, narrow), bf16),
         ),
-        (where, z0, zy, zc, zcy, w),
+        (z0, zy, zc, zcy, w),
         [pltpu.VMEM((tokens, width), bf16)],
         flops=3 * proj + 2 * small,
     )
 
     def own_of(grads):
-        return call(own_body, (half,), (where, grads, w), flops=3 * proj // 2)[0]
+        return call(own_body, (half,), (grads, w), flops=3 * proj // 2)[0]
 
     cot, grads, oth = call(
         first_body,
         (wide, g_like, half),
-        (where, t0, ty, tc, tcy, wo, qkv, probs, w),
+        (t0, ty, tc, tcy, wo, qkv, probs, w),
         flops=3 * proj + 4 * small,
     )
     sums = mp_sum(oth, lambda: own_of(grads))
     term, grads, oth = call(
         middle_body,
         (wide_f, g_like, half),
-        (where, *sums, normal, inv, wo, qkv, probs, w),
+        (*sums, normal, inv, wo, qkv, probs, w),
         flops=3 * proj + 4 * small,
     )
     sums = mp_sum(oth, lambda: own_of(grads))
     implicit, grads, total = call(
         last_body,
         (like((tokens, narrow), f32), g_like, wide),
-        (where, *sums, normal, inv, wo, qkv, probs, cot, term, cotangent[0]),
+        (*sums, normal, inv, wo, qkv, probs, cot, term, cotangent[0]),
         [pltpu.VMEM((tokens, width), f32)],
         flops=proj + 4 * small,
     )
@@ -315,7 +318,7 @@
         return call(
             functools.partial(rows_body, picks, first),
             (like((4 * rows, cols), bf16),),
-            (where, xt, grads),
+            (xt, grads),
             tall,
             flops=2 * tokens * 4 * rows * cols,
         )[0]
@@ -324,7 +327,7 @@
         return call(
             functools.partial(tail_rows_body, picks),
             (like((4 * rows, cols), bf16),),
-            (where, xt, tt, grads, att),
+            (xt, tt, grads, att),
             tall,
             flops=2 * tokens * 4 * rows * cols,
         )[0]
@@ -343,7 +346,7 @@
     g2 = swap_x(s2, 3)
     s1 = block(((1, 0), (1, 1), (2, 0), (2, 1)), 0, one)
     g1 = swap_x(s1, 1)
-    (tt,) = call(turn_body, (like((width, tokens), bf16),), (where, total), flops=proj)
+    (tt,) = call(turn_body, (like((width, tokens), bf16),), (total,), flops=proj)
     s3 = tail_block(((0, 1), (3, 1), (1, 1), (2, 1)), three)
     g3 = swap_yh(s3)
     k2 = block(((0, 0), (1, 0), (0, 1), (1, 1)), one, two)
@@ -366,7 +369,7 @@
     (packed,) = call(
         pack_body,
         (like((nz, dense, 128), bf16),),
-        (where, *e1, *e2, *e3),
+        (*e1, *e2, *e3),
         [pltpu.VMEM((rows, width), f32)],
         flops=rows * width,
     )
@@ -375,7 +378,7 @@
     grad_qkv, grad_o = call(
         functools.partial(unpack_body, factor),
         (like((3, each, narrow), f32), like((each, narrow), f32)),
-        (where, got),
+        (got,),
         [pltpu.VMEM((each, width), f32)],
         flops=rows * width,
     )

time: 122 us -> 113 us (0.926)
  the two profiles are of different devices: /device:TPU:16 before, /device:TPU:8 now
where the time goes in v3:
time: 113 us
  waiting for transfers between devices  56.8 us (50%)
  starting transfers between devices  30.6 us (27%)
  Pallas kernels  20 us (18%)
  local copies, waits for them, and re-layouts  3.87 us (3%)
    pallas_call x17, Pallas kernels, call(): pl.pallas_call(body, out_shape=outs, in_specs=[vmem] * len(ins), out_spec...  20 us
    ppermute x2, waiting for transfers between devices, mp_sum(): far = lax.ppermute(chip, 'yl', SWAP)  18.1 us
    ppermute x6, waiting for transfers between devices, swap_x(): return lax.ppermute(value, 'x', [(i, i ^ by) for i in range(nx)])  14 us
    all_to_all x1, waiting for transfers between devices, shards(): got = lax.all_to_all(packed, 'z', 0, 0, tiled=True)  10.9 us
    ppermute x6, starting transfers between devices, swap_x(): return lax.ppermute(value, 'x', [(i, i ^ by) for i in range(nx)])  8.75 us
    all_to_all x1, starting transfers between devices, shards(): got = lax.all_to_all(packed, 'z', 0, 0, tiled=True)  8.46 us
    ppermute x3, starting transfers between devices, swap_yh(): return lax.ppermute(value, 'yh', SWAP)  7.37 us
    unnamed x8, local copies, waits for them, and re-layouts  3.87 us
  transfers between devices with their start and end apart: 24, of which 14 were waited for; matrix products, arithmetic and copies ran while one was open for 2% of the time, Pallas kernels for 7%

profile of v3, /device:TPU:8, one launch (start us, length us, event | category | flops | bytes accessed | tf_op | source)
XLA Modules:
  0.0 112.9 jit_solution(15510701692007683995)
XLA Ops:
  0.6 2.2 %collective-permute-start.3 = (bf16[257,320]{1,0:T(8,128)(2,1)}, bf16[257,320]{1,0:T(8,128)(2,1)S(1)}, u32[]{:S(2)}, u32[]{:S(2)}) collective-permute-start(bf16[257,320]{1,0:T(8,128)(2,1)} %bitcast.11), channel_id=1, source_target_pairs={{0,2},{2,0},{1,3},{3,1},{4,6},{6,4},{5,7},{7,5},{8,10},{10,8},{9,1... | collective-permute-start | bytes 493448 | tf_op jit(solution)/shard_map/ppermute | solution.py:260
  2.9 1.0 copy.10
  3.9 1.7 %copy-done = bf16[3,1280,320]{1,2,0:T(8,128)(2,1)S(1)} copy-done((bf16[3,1280,320]{1,2,0:T(8,128)(2,1)S(1)}, bf16[3,1280,320]{1,2,0:T(8,128)(2,1)}, u32[]{:S(2)}) %copy-start) | copy-done | bytes 2457624
  6.6 2.1 %collective-permute-done.3.zy = bf16[257,320]{1,0:T(8,128)(2,1)S(1)} collective-permute-done((bf16[257,320]{1,0:T(8,128)(2,1)}, bf16[257,320]{1,0:T(8,128)(2,1)S(1)}, u32[]{:S(2)}, u32[]{:S(2)}) %collective-permute-start.3) | collective-permute-done | bytes 164512 | tf_op jit(solution)/shard_map/ppermute | solution.py:260
  9.2 3.0 %collective-permute-done.ty = bf16[257,320]{1,0:T(8,128)(2,1)S(1)} collective-permute-done((bf16[257,320]{1,0:T(8,128)(2,1)S(1)}, bf16[257,320]{1,0:T(8,128)(2,1)S(1)}, u32[]{:S(2)}, u32[]{:S(2)}) %collective-permute-start) | collective-permute-done | bytes 164512 | tf_op jit(solution)/shard_map/ppermute | solution.py:271
  12.4 2.9 %shard_map.69 = (bf16[257,1280]{1,0:T(8,128)(2,1)S(1)}, bf16[1280,257]{1,0:T(8,128)(2,1)S(1)}, f32[257,128]{1,0:T(8,128)S(1)}, bf16[12,257,80]{2,1,0:T(8,128)(2,...) custom-call(bf16[257,320]{1,0:T(8,128)(2,1)S(1)} %bitcast.13, ...), custom_call_target="tpu_custom_call" | custom-call | flops 716145920 | bytes 6277648 | tf_op jit(solution)/shard_map/pallas_call | solution.py:35
  15.4 2.9 %shard_map.70 = (bf16[257,1280]{1,0:T(8,128)(2,1)S(1)}, bf16[257,960]{1,0:T(8,128)(2,1)S(1)}, bf16[257,640]{1,0:T(8,128)(2,1)S(1)}) custom-call(bf16[257,320]{1,0:T(8,128)(2,1)S(1)} %get-tuple-element.22.t0, bf16[257,320]{1,0:T(8,128)(2,1)S(1)} %collective-permute-done.ty, bf16[257,320]{1,0:T(8,128)(2,1)S(1)} %collective-permute-done.1.tc, ...), custom_call_target="tpu_custom_call" | custom-call | flops 800688640 | bytes 6965264 | tf_op jit(solution)/shard_map/pallas_call | solution.py:35
  20.2 1.1 collective-permute-start.7
  21.4 9.1 %collective-permute-done.7.far = bf16[257,640]{1,0:T(8,128)(2,1)S(1)} collective-permute-done((bf16[257,640]{1,0:T(8,128)(2,1)S(1)}, bf16[257,640]{1,0:T(8,128)(2,1)S(1)}, u32[]{:S(2)}, u32[]{:S(2)}) %collective-permute-start.7) | collective-permute-done | bytes 328992 | tf_op jit(solution)/shard_map/ppermute | solution.py:242
  30.5 1.6 %collective-permute-done.9.far_c = bf16[257,640]{1,0:T(8,128)(2,1)S(1)} collective-permute-done((bf16[257,640]{1,0:T(8,128)(2,1)S(1)}, bf16[257,640]{1,0:T(8,128)(2,1)S(1)}, u32[]{:S(2)}, u32[]{:S(2)}) %collective-permute-start.9) | collective-permute-done | bytes 328992 | tf_op jit(solution)/shard_map/ppermute | solution.py:243
  32.2 3.4 %shard_map.72 = (f32[257,1280]{1,0:T(8,128)S(1)}, bf16[257,960]{1,0:T(8,128)(2,1)S(1)}, bf16[257,640]{1,0:T(8,128)(2,1)S(1)}) custom-call(bf16[257,640]{1,0:T(8,128)(2,1)S(1)} %add_convert_fusion.1.chip, bf16[257,640]{1,0:T(8,128)(2,1)S(1)} %collective-permute-done.7.far, bf16[257,640]{1,0:T(8,128)(2,1)S(1)} %collective-permute-done.8.chip_c, ...), custom_call_target="tpu_custom_call" | custom-call | flops 800688640 | bytes 9070608 | tf_op jit(solution)/shard_map/pallas_call | solution.py:35
  36.4 0.9 collective-permute-done.10
  37.4 1.1 collective-permute-start.11
  38.5 9.0 %collective-permute-done.11.far = bf16[257,640]{1,0:T(8,128)(2,1)S(1)} collective-permute-done((bf16[257,640]{1,0:T(8,128)(2,1)S(1)}, bf16[257,640]{1,0:T(8,128)(2,1)S(1)}, u32[]{:S(2)}, u32[]{:S(2)}) %collective-permute-start.11) | collective-permute-done | bytes 328992 | tf_op jit(solution)/shard_map/ppermute | solution.py:242
  47.5 1.6 %collective-permute-done.13.far_c = bf16[257,640]{1,0:T(8,128)(2,1)S(1)} collective-permute-done((bf16[257,640]{1,0:T(8,128)(2,1)S(1)}, bf16[257,640]{1,0:T(8,128)(2,1)S(1)}, u32[]{:S(2)}, u32[]{:S(2)}) %collective-permute-start.13) | collective-permute-done | bytes 328992 | tf_op jit(solution)/shard_map/ppermute | solution.py:243
  49.1 3.1 %shard_map.74 = (f32[257,320]{1,0:T(8,128)S(1)}, bf16[257,960]{1,0:T(8,128)(2,1)S(1)}, bf16[257,1280]{1,0:T(8,128)(2,1)S(1)}) custom-call(bf16[257,640]{1,0:T(8,128)(2,1)S(1)} %add_convert_fusion.chip, bf16[257,640]{1,0:T(8,128)(2,1)S(1)} %collective-permute-done.11.far, bf16[257,640]{1,0:T(8,128)(2,1)S(1)} %collective-permute-done.12.chip_c, ...), custom_call_target="tpu_custom_call" | custom-call | flops 379619840 | bytes 8257808 | tf_op jit(solution)/shard_map/pallas_call | solution.py:35
  52.7 1.5 %collective-permute-start.14 = (bf16[640,384]{1,0:T(8,128)(2,1)S(1)}, bf16[640,384]{1,0:T(8,128)(2,1)S(1)}, u32[]{:S(2)}, u32[]{:S(2)}) collective-permute-start(bf16[640,384]{1,0:T(8,128)(2,1)S(1)} %shard_map.76), channel_id=1, source_target_pairs={{0,64},{64,0},{128,192},{192,128},{1,65},{65,1},{129,193},{193,129... | collective-permute-start | bytes 1474568 | tf_op jit(solution)/shard_map/ppermute | solution.py:336
  54.7 2.2 %collective-permute-start.17 = (bf16[640,512]{1,0:T(8,128)(2,1)S(1)}, bf16[640,512]{1,0:T(8,128)(2,1)S(1)}, u32[]{:S(2)}, u32[]{:S(2)}) collective-permute-start(bf16[640,512]{1,0:T(8,128)(2,1)S(1)} %shard_map.78), channel_id=1, source_target_pairs={{0,192},{64,128},{128,64},{192,0},{1,193},{65,129},{129,65},{193,1... | collective-permute-start | bytes 1966088 | tf_op jit(solution)/shard_map/ppermute | solution.py:336
  58.0 2.6 %collective-permute-start.20 = (bf16[640,384]{1,0:T(8,128)(2,1)S(1)}, bf16[640,384]{1,0:T(8,128)(2,1)S(1)}, u32[]{:S(2)}, u32[]{:S(2)}) collective-permute-start(bf16[640,384]{1,0:T(8,128)(2,1)S(1)} %shard_map.81), channel_id=1, source_target_pairs={{0,32},{32,0},{1,33},{33,1},{2,34},{34,2},{3,35},{35,3},{4,36},{36... | collective-permute-start | bytes 1474568 | tf_op jit(solution)/shard_map/ppermute | solution.py:339
  62.3 3.8 %collective-permute-done.14 = bf16[640,384]{1,0:T(8,128)(2,1)S(1)} collective-permute-done((bf16[640,384]{1,0:T(8,128)(2,1)S(1)}, bf16[640,384]{1,0:T(8,128)(2,1)S(1)}, u32[]{:S(2)}, u32[]{:S(2)}) %collective-permute-start.14) | collective-permute-done | bytes 491552 | tf_op jit(solution)/shard_map/ppermute | solution.py:336
  66.2 2.7 %collective-permute-start.15 = (bf16[320,384]{1,0:T(8,128)(2,1)S(1)}, bf16[320,384]{1,0:T(8,128)(2,1)S(1)}, u32[]{:S(2)}, u32[]{:S(2)}) collective-permute-start(bf16[320,384]{1,0:T(8,128)(2,1)S(1)} %add_convert_fusion.4), channel_id=1, source_target_pairs={{0,192},{64,128},{128,64},{192,0},{1,193},{65,129},{129,65},{193,1... | collective-permute-start | bytes 737288 | tf_op jit(solution)/shard_map/ppermute | solution.py:336
  68.9 4.7 %collective-permute-done.17 = bf16[640,512]{1,0:T(8,128)(2,1)S(1)} collective-permute-done((bf16[640,512]{1,0:T(8,128)(2,1)S(1)}, bf16[640,512]{1,0:T(8,128)(2,1)S(1)}, u32[]{:S(2)}, u32[]{:S(2)}) %collective-permute-start.17) | collective-permute-done | bytes 655392 | tf_op jit(solution)/shard_map/ppermute | solution.py:336
  73.7 2.4 %collective-permute-start.18 = (bf16[320,512]{1,0:T(8,128)(2,1)S(1)}, bf16[320,512]{1,0:T(8,128)(2,1)S(1)}, u32[]{:S(2)}, u32[]{:S(2)}) collective-permute-start(bf16[320,512]{1,0:T(8,128)(2,1)S(1)} %add_convert_fusion.2), channel_id=1, source_target_pairs={{0,32},{32,0},{1,33},{33,1},{2,34},{34,2},{3,35},{35,3},{4,36},{36... | collective-permute-start | bytes 983048 | tf_op jit(solution)/shard_map/ppermute | solution.py:339
  76.2 1.5 %collective-permute-done.15 = bf16[320,384]{1,0:T(8,128)(2,1)S(1)} collective-permute-done((bf16[320,384]{1,0:T(8,128)(2,1)S(1)}, bf16[320,384]{1,0:T(8,128)(2,1)S(1)}, u32[]{:S(2)}, u32[]{:S(2)}) %collective-permute-start.15) | collective-permute-done | bytes 245792 | tf_op jit(solution)/shard_map/ppermute | solution.py:336
  77.9 2.4 %collective-permute-start.16 = (bf16[160,384]{1,0:T(8,128)(2,1)S(1)}, bf16[160,384]{1,0:T(8,128)(2,1)S(1)}, u32[]{:S(2)}, u32[]{:S(2)}) collective-permute-start(bf16[160,384]{1,0:T(8,128)(2,1)S(1)} %get-tuple-element.48), channel_id=1, source_target_pairs={{0,32},{32,0},{1,33},{33,1},{2,34},{34,2},{3,35},{35,3},{4,36},{36... | collective-permute-start | bytes 368648 | tf_op jit(solution)/shard_map/ppermute | solution.py:339
  80.2 3.9 %collective-permute-done.18 = bf16[320,512]{1,0:T(8,128)(2,1)S(1)} collective-permute-done((bf16[320,512]{1,0:T(8,128)(2,1)S(1)}, bf16[320,512]{1,0:T(8,128)(2,1)S(1)}, u32[]{:S(2)}, u32[]{:S(2)}) %collective-permute-start.18) | collective-permute-done | bytes 327712 | tf_op jit(solution)/shard_map/ppermute | solution.py:339
  84.4 2.2 %collective-permute-start.22 = (bf16[160,384]{1,0:T(8,128)(2,1)S(1)}, bf16[160,384]{1,0:T(8,128)(2,1)S(1)}, u32[]{:S(2)}, u32[]{:S(2)}) collective-permute-start(bf16[160,384]{1,0:T(8,128)(2,1)S(1)} %get-tuple-element.46), channel_id=1, source_target_pairs={{0,192},{64,128},{128,64},{192,0},{1,193},{65,129},{129,65},{193,1... | collective-permute-start | bytes 368648 | tf_op jit(solution)/shard_map/ppermute | solution.py:336
  86.6 4.0 %collective-permute-done.22.g3 = bf16[160,384]{1,0:T(8,128)(2,1)S(1)} collective-permute-done((bf16[160,384]{1,0:T(8,128)(2,1)S(1)}, bf16[160,384]{1,0:T(8,128)(2,1)S(1)}, u32[]{:S(2)}, u32[]{:S(2)}) %collective-permute-start.22) | collective-permute-done | bytes 122912 | tf_op jit(solution)/shard_map/ppermute | solution.py:336
  90.6 0.9 shard_map.82
  91.6 8.5 %all-to-all-start = ((bf16[8,200,128]{2,1,0:T(8,128)(2,1)}), bf16[8,200,128]{2,1,0:T(8,128)(2,1)S(1)}, u32[]{:S(2)}, u32[]{:S(2)}) async-start(bf16[8,200,128]{2,1,0:T(8,128)(2,1)} %shard_map.82), calls=%async_computation | async-start | bytes 819200 | tf_op jit(solution)/shard_map/all_to_all | solution.py:376
  100.0 1.2 %copy.7 = f32[1,257,320]{2,0,1:T(1,128)} copy(f32[1,257,320]{2,1,0:T(8,128)S(1)} %bitcast.10) | data formatting | bytes 657920
  101.2 10.9 %all-to-all-done.got = bf16[8,200,128]{2,1,0:T(8,128)(2,1)S(1)} async-done(((bf16[8,200,128]{2,1,0:T(8,128)(2,1)}), bf16[8,200,128]{2,1,0:T(8,128)(2,1)S(1)}, u32[]{:S(2)}, u32[]{:S(2)}) %all-to-all-start) | async-done | bytes 409632 | tf_op jit(solution)/shard_map/all_to_all | solution.py:376
  (49 shorter events, 10.0 us)
Async XLA Ops:
  0.6 5.8 %copy-start.2 = (bf16[1,257,320]{2,1,0:T(8,128)(2,1)S(1)}, bf16[1,257,320]{2,1,0:T(8,128)(2,1)}, u32[]{:S(2)}) copy-start(bf16[1,257,320]{2,1,0:T(8,128)(2,1)} %param.4) | copy-start | bytes 493444
  0.6 8.1 %collective-permute-start.3 = (bf16[257,320]{1,0:T(8,128)(2,1)}, bf16[257,320]{1,0:T(8,128)(2,1)S(1)}, u32[]{:S(2)}, u32[]{:S(2)}) collective-permute-start(bf16[257,320]{1,0:T(8,128)(2,1)} %bitcast.11), channel_id=1, source_target_pairs={{0,2},{2,0},{1,3},{3,1},{4,6},{6,4},{5,7},{7,5},{8,10},{10,8},{9,1... | collective-permute-start | bytes 493448 | tf_op jit(solution)/shard_map/ppermute | solution.py:260
  3.9 1.7 %copy-start = (bf16[3,1280,320]{1,2,0:T(8,128)(2,1)S(1)}, bf16[3,1280,320]{1,2,0:T(8,128)(2,1)}, u32[]{:S(2)}) copy-start(bf16[3,1280,320]{1,2,0:T(8,128)(2,1)} %param.6) | copy-start | bytes 7372804
  5.6 6.6 %copy-start.1 = (bf16[320,1280]{1,0:T(8,128)(2,1)S(1)}, bf16[320,1280]{1,0:T(8,128)(2,1)}, u32[]{:S(2)}) copy-start(bf16[320,1280]{1,0:T(8,128)(2,1)} %w_out.1) | copy-start | bytes 2457604
  6.4 5.8 %collective-permute-start = (bf16[257,320]{1,0:T(8,128)(2,1)S(1)}, bf16[257,320]{1,0:T(8,128)(2,1)S(1)}, u32[]{:S(2)}, u32[]{:S(2)}) collective-permute-start(bf16[257,320]{1,0:T(8,128)(2,1)S(1)} %get-tuple-element.22.t0), channel_id=1, source_target_pairs={{0,2},{2,0},{1,3},{3,1},{4,6},{6,4},{5,7},{7,5},{8,10},{10,8},{9,1... | collective-permute-start | bytes 493448 | tf_op jit(solution)/shard_map/ppermute | solution.py:271
  6.5 6.0 %collective-permute-start.4 = (bf16[257,320]{1,0:T(8,128)(2,1)S(1)}, bf16[257,320]{1,0:T(8,128)(2,1)S(1)}, u32[]{:S(2)}, u32[]{:S(2)}) collective-permute-start(bf16[257,320]{1,0:T(8,128)(2,1)S(1)} %bitcast.12), channel_id=1, source_target_pairs={{0,1},{1,0},{2,3},{3,2},{4,5},{5,4},{6,7},{7,6},{8,9},{9,8},{10,11... | collective-permute-start | bytes 493448 | tf_op jit(solution)/shard_map/ppermute | solution.py:261
  8.7 3.7 %collective-permute-start.5 = (bf16[257,320]{1,0:T(8,128)(2,1)S(1)}, bf16[257,320]{1,0:T(8,128)(2,1)S(1)}, u32[]{:S(2)}, u32[]{:S(2)}) collective-permute-start(bf16[257,320]{1,0:T(8,128)(2,1)S(1)} %collective-permute-done.3.zy), channel_id=1, source_target_pairs={{0,1},{1,0},{2,3},{3,2},{4,5},{5,4},{6,7},{7,6},{8,9},{9,8},{10,11... | collective-permute-start | bytes 493448 | tf_op jit(solution)/shard_map/ppermute | solution.py:270
  8.7 6.7 %collective-permute-start.1 = (bf16[257,320]{1,0:T(8,128)(2,1)S(1)}, bf16[257,320]{1,0:T(8,128)(2,1)S(1)}, u32[]{:S(2)}, u32[]{:S(2)}) collective-permute-start(bf16[257,320]{1,0:T(8,128)(2,1)S(1)} %get-tuple-element.22.t0), channel_id=1, source_target_pairs={{0,1},{1,0},{2,3},{3,2},{4,5},{5,4},{6,7},{7,6},{8,9},{9,8},{10,11... | collective-permute-start | bytes 493448 | tf_op jit(solution)/shard_map/ppermute | solution.py:269
  12.2 3.2 %collective-permute-start.2 = (bf16[257,320]{1,0:T(8,128)(2,1)S(1)}, bf16[257,320]{1,0:T(8,128)(2,1)S(1)}, u32[]{:S(2)}, u32[]{:S(2)}) collective-permute-start(bf16[257,320]{1,0:T(8,128)(2,1)S(1)} %collective-permute-done.ty), channel_id=1, source_target_pairs={{0,1},{1,0},{2,3},{3,2},{4,5},{5,4},{6,7},{7,6},{8,9},{9,8},{10,11... | collective-permute-start | bytes 493448 | tf_op jit(solution)/shard_map/ppermute | solution.py:272
  18.3 1.9 %collective-permute-start.6 = (bf16[257,640]{1,0:T(8,128)(2,1)S(1)}, bf16[257,640]{1,0:T(8,128)(2,1)S(1)}, u32[]{:S(2)}, u32[]{:S(2)}) collective-permute-start(bf16[257,640]{1,0:T(8,128)(2,1)S(1)} %get-tuple-element.27), channel_id=1, source_target_pairs={{0,1},{1,0},{2,3},{3,2},{4,5},{5,4},{6,7},{7,6},{8,9},{9,8},{10,11... | collective-permute-start | bytes 986888 | tf_op jit(solution)/shard_map/ppermute | solution.py:241
  20.2 10.3 %collective-permute-start.7 = (bf16[257,640]{1,0:T(8,128)(2,1)S(1)}, bf16[257,640]{1,0:T(8,128)(2,1)S(1)}, u32[]{:S(2)}, u32[]{:S(2)}) collective-permute-start(bf16[257,640]{1,0:T(8,128)(2,1)S(1)} %add_convert_fusion.1.chip), channel_id=1, source_target_pairs={{0,2},{2,0},{1,3},{3,1},{4,6},{6,4},{5,7},{7,5},{8,10},{10,8},{9,1... | collective-permute-start | bytes 986888 | tf_op jit(solution)/shard_map/ppermute | solution.py:242
  21.3 9.2 %collective-permute-start.8 = (bf16[257,640]{1,0:T(8,128)(2,1)S(1)}, bf16[257,640]{1,0:T(8,128)(2,1)S(1)}, u32[]{:S(2)}, u32[]{:S(2)}) collective-permute-start(bf16[257,640]{1,0:T(8,128)(2,1)S(1)} %add_convert_fusion.1.chip), channel_id=1, source_target_pairs={{0,1},{1,0},{2,3},{3,2},{4,5},{5,4},{6,7},{7,6},{8,9},{9,8},{10,11... | collective-permute-start | bytes 986888 | tf_op jit(solution)/shard_map/ppermute | solution.py:243
  30.5 1.6 %collective-permute-start.9 = (bf16[257,640]{1,0:T(8,128)(2,1)S(1)}, bf16[257,640]{1,0:T(8,128)(2,1)S(1)}, u32[]{:S(2)}, u32[]{:S(2)}) collective-permute-start(bf16[257,640]{1,0:T(8,128)(2,1)S(1)} %collective-permute-done.7.far), channel_id=1, source_target_pairs={{0,1},{1,0},{2,3},{3,2},{4,5},{5,4},{6,7},{7,6},{8,9},{9,8},{10,11... | collective-permute-start | bytes 986888 | tf_op jit(solution)/shard_map/ppermute | solution.py:243
  35.6 1.7 %collective-permute-start.10 = (bf16[257,640]{1,0:T(8,128)(2,1)S(1)}, bf16[257,640]{1,0:T(8,128)(2,1)S(1)}, u32[]{:S(2)}, u32[]{:S(2)}) collective-permute-start(bf16[257,640]{1,0:T(8,128)(2,1)S(1)} %get-tuple-element.31), channel_id=1, source_target_pairs={{0,1},{1,0},{2,3},{3,2},{4,5},{5,4},{6,7},{7,6},{8,9},{9,8},{10,11... | collective-permute-start | bytes 986888 | tf_op jit(solution)/shard_map/ppermute | solution.py:241
  37.4 10.1 %collective-permute-start.11 = (bf16[257,640]{1,0:T(8,128)(2,1)S(1)}, bf16[257,640]{1,0:T(8,128)(2,1)S(1)}, u32[]{:S(2)}, u32[]{:S(2)}) collective-permute-start(bf16[257,640]{1,0:T(8,128)(2,1)S(1)} %add_convert_fusion.chip), channel_id=1, source_target_pairs={{0,2},{2,0},{1,3},{3,1},{4,6},{6,4},{5,7},{7,5},{8,10},{10,8},{9,1... | collective-permute-start | bytes 986888 | tf_op jit(solution)/shard_map/ppermute | solution.py:242
  38.5 9.0 %collective-permute-start.12 = (bf16[257,640]{1,0:T(8,128)(2,1)S(1)}, bf16[257,640]{1,0:T(8,128)(2,1)S(1)}, u32[]{:S(2)}, u32[]{:S(2)}) collective-permute-start(bf16[257,640]{1,0:T(8,128)(2,1)S(1)} %add_convert_fusion.chip), channel_id=1, source_target_pairs={{0,1},{1,0},{2,3},{3,2},{4,5},{5,4},{6,7},{7,6},{8,9},{9,8},{10,11... | collective-permute-start | bytes 986888 | tf_op jit(solution)/shard_map/ppermute | solution.py:243
  47.5 1.6 %collective-permute-start.13 = (bf16[257,640]{1,0:T(8,128)(2,1)S(1)}, bf16[257,640]{1,0:T(8,128)(2,1)S(1)}, u32[]{:S(2)}, u32[]{:S(2)}) collective-permute-start(bf16[257,640]{1,0:T(8,128)(2,1)S(1)} %collective-permute-done.11.far), channel_id=1, source_target_pairs={{0,1},{1,0},{2,3},{3,2},{4,5},{5,4},{6,7},{7,6},{8,9},{9,8},{10,11... | collective-permute-start | bytes 986888 | tf_op jit(solution)/shard_map/ppermute | solution.py:243
  52.7 13.4 %collective-permute-start.14 = (bf16[640,384]{1,0:T(8,128)(2,1)S(1)}, bf16[640,384]{1,0:T(8,128)(2,1)S(1)}, u32[]{:S(2)}, u32[]{:S(2)}) collective-permute-start(bf16[640,384]{1,0:T(8,128)(2,1)S(1)} %shard_map.76), channel_id=1, source_target_pairs={{0,64},{64,0},{128,192},{192,128},{1,65},{65,1},{129,193},{193,129... | collective-permute-start | bytes 1474568 | tf_op jit(solution)/shard_map/ppermute | solution.py:336
  54.7 18.9 %collective-permute-start.17 = (bf16[640,512]{1,0:T(8,128)(2,1)S(1)}, bf16[640,512]{1,0:T(8,128)(2,1)S(1)}, u32[]{:S(2)}, u32[]{:S(2)}) collective-permute-start(bf16[640,512]{1,0:T(8,128)(2,1)S(1)} %shard_map.78), channel_id=1, source_target_pairs={{0,192},{64,128},{128,64},{192,0},{1,193},{65,129},{129,65},{193,1... | collective-permute-start | bytes 1966088 | tf_op jit(solution)/shard_map/ppermute | solution.py:336
  58.0 18.1 %collective-permute-start.20 = (bf16[640,384]{1,0:T(8,128)(2,1)S(1)}, bf16[640,384]{1,0:T(8,128)(2,1)S(1)}, u32[]{:S(2)}, u32[]{:S(2)}) collective-permute-start(bf16[640,384]{1,0:T(8,128)(2,1)S(1)} %shard_map.81), channel_id=1, source_target_pairs={{0,32},{32,0},{1,33},{33,1},{2,34},{34,2},{3,35},{35,3},{4,36},{36... | collective-permute-start | bytes 1474568 | tf_op jit(solution)/shard_map/ppermute | solution.py:339
  66.2 11.6 %collective-permute-start.15 = (bf16[320,384]{1,0:T(8,128)(2,1)S(1)}, bf16[320,384]{1,0:T(8,128)(2,1)S(1)}, u32[]{:S(2)}, u32[]{:S(2)}) collective-permute-start(bf16[320,384]{1,0:T(8,128)(2,1)S(1)} %add_convert_fusion.4), channel_id=1, source_target_pairs={{0,192},{64,128},{128,64},{192,0},{1,193},{65,129},{129,65},{193,1... | collective-permute-start | bytes 737288 | tf_op jit(solution)/shard_map/ppermute | solution.py:336
  73.7 10.4 %collective-permute-start.18 = (bf16[320,512]{1,0:T(8,128)(2,1)S(1)}, bf16[320,512]{1,0:T(8,128)(2,1)S(1)}, u32[]{:S(2)}, u32[]{:S(2)}) collective-permute-start(bf16[320,512]{1,0:T(8,128)(2,1)S(1)} %add_convert_fusion.2), channel_id=1, source_target_pairs={{0,32},{32,0},{1,33},{33,1},{2,34},{34,2},{3,35},{35,3},{4,36},{36... | collective-permute-start | bytes 983048 | tf_op jit(solution)/shard_map/ppermute | solution.py:339
  76.1 8.2 %collective-permute-start.21 = (bf16[320,384]{1,0:T(8,128)(2,1)S(1)}, bf16[320,384]{1,0:T(8,128)(2,1)S(1)}, u32[]{:S(2)}, u32[]{:S(2)}) collective-permute-start(bf16[320,384]{1,0:T(8,128)(2,1)S(1)} %add_convert_fusion.3), channel_id=1, source_target_pairs={{0,64},{64,0},{128,192},{192,128},{1,65},{65,1},{129,193},{193,129... | collective-permute-start | bytes 737288 | tf_op jit(solution)/shard_map/ppermute | solution.py:336
  77.9 8.8 %collective-permute-start.16 = (bf16[160,384]{1,0:T(8,128)(2,1)S(1)}, bf16[160,384]{1,0:T(8,128)(2,1)S(1)}, u32[]{:S(2)}, u32[]{:S(2)}) collective-permute-start(bf16[160,384]{1,0:T(8,128)(2,1)S(1)} %get-tuple-element.48), channel_id=1, source_target_pairs={{0,32},{32,0},{1,33},{33,1},{2,34},{34,2},{3,35},{35,3},{4,36},{36... | collective-permute-start | bytes 368648 | tf_op jit(solution)/shard_map/ppermute | solution.py:339
  84.2 6.4 %collective-permute-start.19 = (bf16[160,512]{1,0:T(8,128)(2,1)S(1)}, bf16[160,512]{1,0:T(8,128)(2,1)S(1)}, u32[]{:S(2)}, u32[]{:S(2)}) collective-permute-start(bf16[160,512]{1,0:T(8,128)(2,1)S(1)} %get-tuple-element.44), channel_id=1, source_target_pairs={{0,64},{64,0},{128,192},{192,128},{1,65},{65,1},{129,193},{193,129... | collective-permute-start | bytes 491528 | tf_op jit(solution)/shard_map/ppermute | solution.py:336
  84.4 6.2 %collective-permute-start.22 = (bf16[160,384]{1,0:T(8,128)(2,1)S(1)}, bf16[160,384]{1,0:T(8,128)(2,1)S(1)}, u32[]{:S(2)}, u32[]{:S(2)}) collective-permute-start(bf16[160,384]{1,0:T(8,128)(2,1)S(1)} %get-tuple-element.46), channel_id=1, source_target_pairs={{0,192},{64,128},{128,64},{192,0},{1,193},{65,129},{129,65},{193,1... | collective-permute-start | bytes 368648 | tf_op jit(solution)/shard_map/ppermute | solution.py:336
  91.6 20.5 %all-to-all-start = ((bf16[8,200,128]{2,1,0:T(8,128)(2,1)}), bf16[8,200,128]{2,1,0:T(8,128)(2,1)S(1)}, u32[]{:S(2)}, u32[]{:S(2)}) async-start(bf16[8,200,128]{2,1,0:T(8,128)(2,1)} %shard_map.82), calls=%async_computation | async-start | bytes 819200 | tf_op jit(solution)/shard_map/all_to_all | solution.py:376

commit v4 on v3

--- a/solution.py
+++ b/solution.py
@@ -158,7 +158,7 @@
     oth_o[...] = input_back(OTHER, grads_o, w)
 
 
-def last_body(chip, far, chip_c, far_c, normal, inv, w_out, qkv, probs, cot, term, mine, imp_o, grads_o, total_o, spot):
+def total_body(picks, chip, far, chip_c, far_c, normal, inv, cot, term, mine, att, imp_o, total_o, tt_o, out, spot, rows):
     spot[...] = put_term(spot, chip, far, chip_c, far_c, normal, inv) + term[...]
     narrow = mine.shape[1]
     for yl in range(2):
@@ -169,7 +169,16 @@
 
     total = (spot[...] + cot[...].astype(f32)).astype(bf16)
     total_o[...] = total
-    attention_back(total, w_out, qkv, probs, grads_o)
+    tt_o[...] = total.T
+    gather_rows(tt_o, rows, picks, narrow)
+    out[...] = dot(rows[...], att[...]).astype(bf16)
+
+
+def last_body(total, w_out, qkv, probs, one_o, two_o, grads):
+    attention_back(total[...], w_out, qkv, probs, grads)
+    cols = one_o.shape[1]
+    one_o[...] = grads[:, :cols]
+    two_o[...] = grads[:, cols:]
 
 
 def spot_of(x, narrow):
@@ -185,24 +194,18 @@
         dst[i * rows : (i + 1) * rows, :] = src[pl.ds(pl.multiple_of(at, 16), rows), :]
 
 
-def rows_body(picks, first, xt, grads, out, xs):
-    gather_rows(xt, xs, picks, grads.shape[1] // 3)
-    out[...] = dot(xs[...], grads[:, first : first + out.shape[1]]).astype(bf16)
-
-
-def turn_body(total, tt_o):
-    tt_o[...] = total[...].T
-
-
-def tail_rows_body(picks, xt, tt, grads, att, out, xs):
-    narrow = att.shape[1]
-    left = out.shape[1] - narrow
-    gather_rows(xt, xs, picks, narrow)
-    one = dot(xs[...], grads[:, grads.shape[1] - left :])
-    gather_rows(tt, xs, picks, narrow)
-    two = dot(xs[...], att[...])
-    out[:, :left] = one.astype(bf16)
-    out[:, left:] = two.astype(bf16)
+def pick_body(picks, xt, out):
+    gather_rows(xt, out, picks, xt.shape[0] // 4)
+
+
+def rows_body(picks, x, g, out, rows):
+    gather_rows(x, rows, picks, x.shape[0] // 4)
+    out[...] = dot(rows[...], g[...]).astype(out.dtype)
+
+
+def both_body(start, mine, x, g, out):
+    at = slice(start, start + out.shape[0])
+    out[...] = (mine[at, :] + dot(x[at, :], g[...])).astype(bf16)
 
 
 def pack_body(k1, g1, k2, g2, k3, g3, out, spot):
@@ -240,7 +243,8 @@
 def mp_sum(oth, own):
     chip = add(own(), lax.ppermute(oth, "c", SWAP))
     far = lax.ppermute(chip, "yl", SWAP)
-    return chip, far, lax.ppermute(chip, "c", SWAP), lax.ppermute(far, "c", SWAP)
+    far_c = lax.ppermute(far, "c", SWAP)
+    return chip, far, lax.ppermute(chip, "c", SWAP), far_c
 
 
 def shards(z_star, cotangent, w_qkv, w_out):
@@ -302,69 +306,95 @@
         flops=3 * proj + 4 * small,
     )
     sums = mp_sum(oth, lambda: own_of(grads))
-    implicit, grads, total = call(
-        last_body,
-        (like((tokens, narrow), f32), g_like, wide),
-        (*sums, normal, inv, wo, qkv, probs, cot, term, cotangent[0]),
-        [pltpu.VMEM((tokens, width), f32)],
-        flops=proj + 4 * small,
-    )
 
     rows = width // (nx * ny)
     each = rows // nz
-    tall = [pltpu.VMEM((4 * rows, tokens), bf16)]
-
-    def block(picks, first, cols):
+    tall = pltpu.VMEM((4 * rows, tokens), bf16)
+    tall_like = like((4 * rows, tokens), bf16)
+    one, two, three = 448, 512, narrow
+    give_one = ((1, 0), (1, 1), (2, 0), (2, 1))
+    keep_one = ((0, 0), (0, 1), (3, 0), (3, 1))
+    give_two = ((3, 0), (2, 0), (3, 1), (2, 1))
+    keep_two = ((0, 0), (1, 0), (0, 1), (1, 1))
+    give_three = ((0, 1), (3, 1), (1, 1), (2, 1))
+    keep_three = ((0, 0), (3, 0), (1, 0), (2, 0))
+
+    def swap_x(value, by):
+        return lax.ppermute(value, "x", [(i, i ^ by) for i in range(nx)])
+
+    def swap_yh(value):
+        return lax.ppermute(value, "yh", SWAP)
+
+    def pick(picks):
+        body = functools.partial(pick_body, picks)
+        (part,) = call(body, (tall_like,), (xt,), flops=proj)
+        return part
+
+    x_two = swap_x(pick(give_two), 3)
+    x_one = swap_x(pick(give_one), 1)
+
+    implicit, total, tt, s3 = call(
+        functools.partial(total_body, give_three),
+        (
+            like((tokens, narrow), f32),
+            wide,
+            like((width, tokens), bf16),
+            like((4 * rows, three), bf16),
+        ),
+        (*sums, normal, inv, cot, term, cotangent[0], att),
+        [pltpu.VMEM((tokens, width), f32), tall],
+        flops=proj,
+    )
+    g3 = swap_yh(s3)
+    g_one, g_two = call(
+        last_body,
+        (like((tokens, one), bf16), like((tokens, two), bf16)),
+        (total, wo, qkv, probs),
+        [pltpu.VMEM((tokens, 3 * narrow), bf16)],
+        flops=proj + 4 * small,
+    )
+    p_two = swap_x(g_two, 3)
+    p_one = swap_x(g_one, 1)
+
+    def block(picks, x, g, dtype):
+        cols = g.shape[1]
         return call(
-            functools.partial(rows_body, picks, first),
-            (like((4 * rows, cols), bf16),),
-            (xt, grads),
-            tall,
+            functools.partial(rows_body, picks),
+            (like((4 * rows, cols), dtype),),
+            (x, g),
+            [tall],
             flops=2 * tokens * 4 * rows * cols,
         )[0]
 
-    def tail_block(picks, cols):
+    def both(start, mine, x, g):
         return call(
-            functools.partial(tail_rows_body, picks),
-            (like((4 * rows, cols), bf16),),
-            (xt, tt, grads, att),
-            tall,
-            flops=2 * tokens * 4 * rows * cols,
+            functools.partial(both_body, start * rows),
+            (like((2 * rows, g.shape[1]), bf16),),
+            (mine, x, g),
+            flops=2 * tokens * 2 * rows * g.shape[1],
         )[0]
 
-    def swap_x(value, by):
-        return lax.ppermute(value, "x", [(i, i ^ by) for i in range(nx)])
-
-    def swap_yh(value):
-        return lax.ppermute(value, "yh", SWAP)
+    m2 = block(keep_two, xt, g_two, f32)
+    m1 = block(keep_one, xt, g_one, f32)
+    k3 = block(keep_three, tt, att, bf16)
 
     def at(value, start, count):
         return value[start * rows : (start + count) * rows]
 
-    one, two, three = 384, 512, 384
-    s2 = block(((3, 0), (2, 0), (3, 1), (2, 1)), one, two)
-    g2 = swap_x(s2, 3)
-    s1 = block(((1, 0), (1, 1), (2, 0), (2, 1)), 0, one)
-    g1 = swap_x(s1, 1)
-    (tt,) = call(turn_body, (like((width, tokens), bf16),), (total,), flops=proj)
-    s3 = tail_block(((0, 1), (3, 1), (1, 1), (2, 1)), three)
-    g3 = swap_yh(s3)
-    k2 = block(((0, 0), (1, 0), (0, 1), (1, 1)), one, two)
-    k1 = block(((0, 0), (0, 1), (3, 0), (3, 1)), 0, one)
-    k3 = tail_block(((0, 0), (3, 0), (1, 0), (2, 0)), three)
-
-    h2 = swap_yh(add(at(k2, 2, 2), at(g2, 2, 2)))
-    h1 = swap_x(add(at(k1, 2, 2), at(g1, 2, 2)), 3)
+    h2 = swap_yh(both(2, m2, x_two, p_two))
+    h1 = swap_x(both(2, m1, x_one, p_one), 3)
     h3 = swap_x(add(at(k3, 2, 2), at(g3, 2, 2)), 1)
-
-    def last_half(k, g, h, swap):
-        send = add(at(k, 1, 1), at(g, 1, 1), at(h, 1, 1))
-        got = swap(send)
-        return add(at(k, 0, 1), at(g, 0, 1), at(h, 0, 1)), got
-
-    e2 = last_half(k2, g2, h2, lambda v: swap_x(v, 1))
-    e1 = last_half(k1, g1, h1, swap_yh)
-    e3 = last_half(k3, g3, h3, lambda v: swap_x(v, 3))
+    k2 = both(0, m2, x_two, p_two)
+    k1 = both(0, m1, x_one, p_one)
+    k3 = add(at(k3, 0, 2), at(g3, 0, 2))
+
+    def last_half(k, h, swap):
+        got = swap(add(at(k, 1, 1), at(h, 1, 1)))
+        return add(at(k, 0, 1), at(h, 0, 1)), got
+
+    e2 = last_half(k2, h2, lambda v: swap_x(v, 1))
+    e1 = last_half(k1, h1, swap_yh)
+    e3 = last_half(k3, h3, lambda v: swap_x(v, 3))
     dense = each * width // 128
     (packed,) = call(
         pack_body,

time: 113 us -> 117 us (1.035)
  waiting for transfers between devices: 56.8 us -> 63.3 us
  starting transfers between devices: 30.6 us -> 28 us
    ppermute x6 -> x8, waiting for transfers between devices: 14 us -> 18.9 us  [swap_x(): return lax.ppermute(value, 'x', [(i, i ^ by) for i in range(nx)])]
    ppermute x3, starting transfers between devices: 7.37 us -> 5.03 us  [swap_yh(): return lax.ppermute(value, 'yh', SWAP)]
    ppermute x3, waiting for transfers between devices: 3.87 us -> 5.38 us  [swap_yh(): return lax.ppermute(value, 'yh', SWAP)]
    pallas_call x17 -> x20, Pallas kernels: 20 us -> 20.3 us  [call(): pl.pallas_call(body, out_shape=outs, in_specs=[vmem] * len(ins), out_spec...]
    ppermute x6 -> x8, starting transfers between devices: 8.75 us -> 8.61 us  [swap_x(): return lax.ppermute(value, 'x', [(i, i ^ by) for i in range(nx)])]
  transfers between devices with their start and end apart: 24 -> 26, of which waited for: 14 -> 15; matrix products, arithmetic and copies ran while one was open for 2% -> 2% of each run, Pallas kernels for 7% -> 9%
where the time goes in v4:
time: 117 us
  waiting for transfers between devices  63.3 us (54%)
  starting transfers between devices  28 us (24%)
  Pallas kernels  20.3 us (17%)
  local copies, waits for them, and re-layouts  3.91 us (3%)
    pallas_call x20, Pallas kernels, call(): pl.pallas_call(body, out_shape=outs, in_specs=[vmem] * len(ins), out_spec...  20.3 us
    ppermute x8, waiting for transfers between devices, swap_x(): return lax.ppermute(value, 'x', [(i, i ^ by) for i in range(nx)])  18.9 us
    ppermute x2, waiting for transfers between devices, mp_sum(): far = lax.ppermute(chip, 'yl', SWAP)  18.2 us
    all_to_all x1, waiting for transfers between devices, shards(): got = lax.all_to_all(packed, 'z', 0, 0, tiled=True)  10.9 us
    ppermute x8, starting transfers between devices, swap_x(): return lax.ppermute(value, 'x', [(i, i ^ by) for i in range(nx)])  8.61 us
    all_to_all x1, starting transfers between devices, shards(): got = lax.all_to_all(packed, 'z', 0, 0, tiled=True)  8.44 us
    ppermute x3, waiting for transfers between devices, swap_yh(): return lax.ppermute(value, 'yh', SWAP)  5.38 us
    ppermute x3, starting transfers between devices, swap_yh(): return lax.ppermute(value, 'yh', SWAP)  5.03 us
  transfers between devices with their start and end apart: 26, of which 15 were waited for; matrix products, arithmetic and copies ran while one was open for 2% of the time, Pallas kernels for 9%

profile of v4, /device:TPU:8, one launch (start us, length us, event | category | flops | bytes accessed | tf_op | source)
XLA Modules:
  0.0 116.9 jit_solution(9229756388423101969)
XLA Ops:
  0.6 2.2 %collective-permute-start.3 = (bf16[257,320]{1,0:T(8,128)(2,1)}, bf16[257,320]{1,0:T(8,128)(2,1)S(1)}, u32[]{:S(2)}, u32[]{:S(2)}) collective-permute-start(bf16[257,320]{1,0:T(8,128)(2,1)} %bitcast.11), channel_id=1, source_target_pairs={{0,2},{2,0},{1,3},{3,1},{4,6},{6,4},{5,7},{7,5},{8,10},{10,8},{9,1... | collective-permute-start | bytes 493448 | tf_op jit(solution)/shard_map/ppermute | solution.py:264
  2.9 1.1 copy.10
  4.0 1.7 %copy-done = bf16[3,1280,320]{1,2,0:T(8,128)(2,1)S(1)} copy-done((bf16[3,1280,320]{1,2,0:T(8,128)(2,1)S(1)}, bf16[3,1280,320]{1,2,0:T(8,128)(2,1)}, u32[]{:S(2)}) %copy-start) | copy-done | bytes 2457624
  6.6 2.0 %collective-permute-done.3.zy = bf16[257,320]{1,0:T(8,128)(2,1)S(1)} collective-permute-done((bf16[257,320]{1,0:T(8,128)(2,1)}, bf16[257,320]{1,0:T(8,128)(2,1)S(1)}, u32[]{:S(2)}, u32[]{:S(2)}) %collective-permute-start.3) | collective-permute-done | bytes 164512 | tf_op jit(solution)/shard_map/ppermute | solution.py:264
  9.2 3.1 %collective-permute-done.ty = bf16[257,320]{1,0:T(8,128)(2,1)S(1)} collective-permute-done((bf16[257,320]{1,0:T(8,128)(2,1)S(1)}, bf16[257,320]{1,0:T(8,128)(2,1)S(1)}, u32[]{:S(2)}, u32[]{:S(2)}) %collective-permute-start) | collective-permute-done | bytes 164512 | tf_op jit(solution)/shard_map/ppermute | solution.py:275
  12.5 2.9 %shard_map.69 = (bf16[257,1280]{1,0:T(8,128)(2,1)S(1)}, bf16[1280,257]{1,0:T(8,128)(2,1)S(1)}, f32[257,128]{1,0:T(8,128)S(1)}, bf16[12,257,80]{2,1,0:T(8,128)(2,...) custom-call(bf16[257,320]{1,0:T(8,128)(2,1)S(1)} %bitcast.13, ...), custom_call_target="tpu_custom_call" | custom-call | flops 716145920 | bytes 6277648 | tf_op jit(solution)/shard_map/pallas_call | solution.py:35
  15.4 2.9 %shard_map.70 = (bf16[257,1280]{1,0:T(8,128)(2,1)S(1)}, bf16[257,960]{1,0:T(8,128)(2,1)S(1)}, bf16[257,640]{1,0:T(8,128)(2,1)S(1)}) custom-call(bf16[257,320]{1,0:T(8,128)(2,1)S(1)} %get-tuple-element.25.t0, bf16[257,320]{1,0:T(8,128)(2,1)S(1)} %collective-permute-done.ty, bf16[257,320]{1,0:T(8,128)(2,1)S(1)} %collective-permute-done.1.tc, ...), custom_call_target="tpu_custom_call" | custom-call | flops 800688640 | bytes 6965264 | tf_op jit(solution)/shard_map/pallas_call | solution.py:35
  21.4 9.2 %collective-permute-done.7.far = bf16[257,640]{1,0:T(8,128)(2,1)S(1)} collective-permute-done((bf16[257,640]{1,0:T(8,128)(2,1)S(1)}, bf16[257,640]{1,0:T(8,128)(2,1)S(1)}, u32[]{:S(2)}, u32[]{:S(2)}) %collective-permute-start.7) | collective-permute-done | bytes 328992 | tf_op jit(solution)/shard_map/ppermute | solution.py:245
  30.6 1.6 %collective-permute-done.9.far_c = bf16[257,640]{1,0:T(8,128)(2,1)S(1)} collective-permute-done((bf16[257,640]{1,0:T(8,128)(2,1)S(1)}, bf16[257,640]{1,0:T(8,128)(2,1)S(1)}, u32[]{:S(2)}, u32[]{:S(2)}) %collective-permute-start.9) | collective-permute-done | bytes 328992 | tf_op jit(solution)/shard_map/ppermute | solution.py:246
  32.2 3.4 %shard_map.72 = (f32[257,1280]{1,0:T(8,128)S(1)}, bf16[257,960]{1,0:T(8,128)(2,1)S(1)}, bf16[257,640]{1,0:T(8,128)(2,1)S(1)}) custom-call(bf16[257,640]{1,0:T(8,128)(2,1)S(1)} %add_convert_fusion.1.chip, bf16[257,640]{1,0:T(8,128)(2,1)S(1)} %collective-permute-done.7.far, bf16[257,640]{1,0:T(8,128)(2,1)S(1)} %collective-permute-done.8.chip_c, ...), custom_call_target="tpu_custom_call" | custom-call | flops 800688640 | bytes 9070608 | tf_op jit(solution)/shard_map/pallas_call | solution.py:35
  37.4 1.0 collective-permute-start.11
  38.5 9.0 %collective-permute-done.11.far = bf16[257,640]{1,0:T(8,128)(2,1)S(1)} collective-permute-done((bf16[257,640]{1,0:T(8,128)(2,1)S(1)}, bf16[257,640]{1,0:T(8,128)(2,1)S(1)}, u32[]{:S(2)}, u32[]{:S(2)}) %collective-permute-start.11) | collective-permute-done | bytes 328992 | tf_op jit(solution)/shard_map/ppermute | solution.py:245
  47.5 1.6 %collective-permute-done.13.far_c = bf16[257,640]{1,0:T(8,128)(2,1)S(1)} collective-permute-done((bf16[257,640]{1,0:T(8,128)(2,1)S(1)}, bf16[257,640]{1,0:T(8,128)(2,1)S(1)}, u32[]{:S(2)}, u32[]{:S(2)}) %collective-permute-start.13) | collective-permute-done | bytes 328992 | tf_op jit(solution)/shard_map/ppermute | solution.py:246
  49.1 1.7 %shard_map.74 = (f32[257,320]{1,0:T(8,128)S(1)}, bf16[257,1280]{1,0:T(8,128)(2,1)S(1)}, bf16[1280,257]{1,0:T(8,128)(2,1)S(1)}, bf16[640,320]{1,0:T(8,128)(2,1)S(1)}) custom-call(bf16[257,640]{1,0:T(8,128)(2,1)S(1)} %add_convert_fusion.chip, bf16[257,640]{1,0:T(8,128)(2,1)S(1)} %collective-permute-done.11.far, ...), custom_call_target="tpu_custom_call" | custom-call | flops 210534400 | bytes 6626944 | tf_op jit(solution)/shard_map/pallas_call | solution.py:35
  50.9 2.2 %collective-permute-start.22 = (bf16[640,320]{1,0:T(8,128)(2,1)S(1)}, bf16[640,320]{1,0:T(8,128)(2,1)S(1)}, u32[]{:S(2)}, u32[]{:S(2)}) collective-permute-start(bf16[640,320]{1,0:T(8,128)(2,1)S(1)} %get-tuple-element.44), channel_id=1, source_target_pairs={{0,32},{32,0},{1,33},{33,1},{2,34},{34,2},{3,35},{35,3},{4,36},{36... | collective-permute-start | bytes 1228808 | tf_op jit(solution)/shard_map/ppermute | solution.py:326
  53.2 1.6 %collective-permute-start.14 = (bf16[640,257]{1,0:T(8,128)(2,1)S(1)}, bf16[640,257]{1,0:T(8,128)(2,1)S(1)}, u32[]{:S(2)}, u32[]{:S(2)}) collective-permute-start(bf16[640,257]{1,0:T(8,128)(2,1)S(1)} %shard_map.77), channel_id=1, source_target_pairs={{0,64},{64,0},{128,192},{192,128},{1,65},{65,1},{129,193},{193,129... | collective-permute-start | bytes 986888 | tf_op jit(solution)/shard_map/ppermute | solution.py:323
  54.8 2.2 %collective-permute-start.18 = (bf16[640,257]{1,0:T(8,128)(2,1)S(1)}, bf16[640,257]{1,0:T(8,128)(2,1)S(1)}, u32[]{:S(2)}, u32[]{:S(2)}) collective-permute-start(bf16[640,257]{1,0:T(8,128)(2,1)S(1)} %shard_map.81), channel_id=1, source_target_pairs={{0,192},{64,128},{128,64},{192,0},{1,193},{65,129},{129,65},{193,1... | collective-permute-start | bytes 986888 | tf_op jit(solution)/shard_map/ppermute | solution.py:323
  57.0 2.4 %shard_map.75 = (bf16[257,448]{1,0:T(8,128)(2,1)S(1)}, bf16[257,512]{1,0:T(8,128)(2,1)S(1)}) custom-call(bf16[257,1280]{1,0:T(8,128)(2,1)S(1)} %get-tuple-element.40.total, bf16[320,1280]{1,0:T(8,128)(2,1)S(1)} %shard_map.68.w_out, bf16[12,257,80]{2,1,0:T(8,128)(2,1)S(1)} %get-tuple-element.27.qkv, f32[4,257,257]{2,1,0:T(8,128)S(1)} %get-tuple-element.28.probs), custom_call_target="tpu_custom_call" | custom-call | flops 379619840 | bytes 3520784 | tf_op jit(solution)/shard_map/pallas_call | solution.py:35
  59.4 1.2 %collective-permute-start.19 = (bf16[257,512]{1,0:T(8,128)(2,1)S(1)}, bf16[257,512]{1,0:T(8,128)(2,1)S(1)}, u32[]{:S(2)}, u32[]{:S(2)}) collective-permute-start(bf16[257,512]{1,0:T(8,128)(2,1)S(1)} %get-tuple-element.42.g), channel_id=1, source_target_pairs={{0,192},{64,128},{128,64},{192,0},{1,193},{65,129},{129,65},{193,1... | collective-permute-start | bytes 789512 | tf_op jit(solution)/shard_map/ppermute | solution.py:323
  61.6 5.7 %collective-permute-done.14.x = bf16[640,257]{1,0:T(8,128)(2,1)S(1)} collective-permute-done((bf16[640,257]{1,0:T(8,128)(2,1)S(1)}, bf16[640,257]{1,0:T(8,128)(2,1)S(1)}, u32[]{:S(2)}, u32[]{:S(2)}) %collective-permute-start.14) | collective-permute-done | bytes 328992 | tf_op jit(solution)/shard_map/ppermute | solution.py:323
  67.3 4.7 %collective-permute-done.15.g = bf16[257,448]{1,0:T(8,128)(2,1)S(1)} collective-permute-done((bf16[257,448]{1,0:T(8,128)(2,1)S(1)}, bf16[257,448]{1,0:T(8,128)(2,1)S(1)}, u32[]{:S(2)}, u32[]{:S(2)}) %collective-permute-start.15) | collective-permute-done | bytes 230304 | tf_op jit(solution)/shard_map/ppermute | solution.py:323
  72.4 2.8 %collective-permute-start.16 = (bf16[320,448]{1,0:T(8,128)(2,1)S(1)}, bf16[320,448]{1,0:T(8,128)(2,1)S(1)}, u32[]{:S(2)}, u32[]{:S(2)}) collective-permute-start(bf16[320,448]{1,0:T(8,128)(2,1)S(1)} %shard_map.79), channel_id=1, source_target_pairs={{0,192},{64,128},{128,64},{192,0},{1,193},{65,129},{129,65},{193,1... | collective-permute-start | bytes 860168 | tf_op jit(solution)/shard_map/ppermute | solution.py:323
  76.4 1.3 %collective-permute-start.20 = (bf16[320,512]{1,0:T(8,128)(2,1)S(1)}, bf16[320,512]{1,0:T(8,128)(2,1)S(1)}, u32[]{:S(2)}, u32[]{:S(2)}) collective-permute-start(bf16[320,512]{1,0:T(8,128)(2,1)S(1)} %shard_map.83), channel_id=1, source_target_pairs={{0,32},{32,0},{1,33},{33,1},{2,34},{34,2},{3,35},{35,3},{4,36},{36... | collective-permute-start | bytes 983048 | tf_op jit(solution)/shard_map/ppermute | solution.py:326
  78.5 3.8 %collective-permute-done.16 = bf16[320,448]{1,0:T(8,128)(2,1)S(1)} collective-permute-done((bf16[320,448]{1,0:T(8,128)(2,1)S(1)}, bf16[320,448]{1,0:T(8,128)(2,1)S(1)}, u32[]{:S(2)}, u32[]{:S(2)}) %collective-permute-start.16) | collective-permute-done | bytes 286752 | tf_op jit(solution)/shard_map/ppermute | solution.py:323
  82.4 1.5 %collective-permute-start.17 = (bf16[160,448]{1,0:T(8,128)(2,1)S(1)}, bf16[160,448]{1,0:T(8,128)(2,1)S(1)}, u32[]{:S(2)}, u32[]{:S(2)}) collective-permute-start(bf16[160,448]{1,0:T(8,128)(2,1)S(1)} %get-tuple-element.54), channel_id=1, source_target_pairs={{0,32},{32,0},{1,33},{33,1},{2,34},{34,2},{3,35},{35,3},{4,36},{36... | collective-permute-start | bytes 430088 | tf_op jit(solution)/shard_map/ppermute | solution.py:326
  83.9 4.2 %collective-permute-done.20 = bf16[320,512]{1,0:T(8,128)(2,1)S(1)} collective-permute-done((bf16[320,512]{1,0:T(8,128)(2,1)S(1)}, bf16[320,512]{1,0:T(8,128)(2,1)S(1)}, u32[]{:S(2)}, u32[]{:S(2)}) %collective-permute-start.20) | collective-permute-done | bytes 327712 | tf_op jit(solution)/shard_map/ppermute | solution.py:326
  88.6 1.2 %collective-permute-done.17.g1 = bf16[160,448]{1,0:T(8,128)(2,1)S(1)} collective-permute-done((bf16[160,448]{1,0:T(8,128)(2,1)S(1)}, bf16[160,448]{1,0:T(8,128)(2,1)S(1)}, u32[]{:S(2)}, u32[]{:S(2)}) %collective-permute-start.17) | collective-permute-done | bytes 143392 | tf_op jit(solution)/shard_map/ppermute | solution.py:326
  89.9 4.7 %collective-permute-done.24.g3 = bf16[160,320]{1,0:T(8,128)(2,1)S(1)} collective-permute-done((bf16[160,320]{1,0:T(8,128)(2,1)S(1)}, bf16[160,320]{1,0:T(8,128)(2,1)S(1)}, u32[]{:S(2)}, u32[]{:S(2)}) %collective-permute-start.24) | collective-permute-done | bytes 102432 | tf_op jit(solution)/shard_map/ppermute | solution.py:323
  94.6 1.0 shard_map.85
  95.6 8.4 %all-to-all-start = ((bf16[8,200,128]{2,1,0:T(8,128)(2,1)}), bf16[8,200,128]{2,1,0:T(8,128)(2,1)S(1)}, u32[]{:S(2)}, u32[]{:S(2)}) async-start(bf16[8,200,128]{2,1,0:T(8,128)(2,1)} %shard_map.85), calls=%async_computation | async-start | bytes 819200 | tf_op jit(solution)/shard_map/all_to_all | solution.py:406
  104.1 1.2 copy.7
  105.2 10.9 %all-to-all-done.got = bf16[8,200,128]{2,1,0:T(8,128)(2,1)S(1)} async-done(((bf16[8,200,128]{2,1,0:T(8,128)(2,1)}), bf16[8,200,128]{2,1,0:T(8,128)(2,1)S(1)}, u32[]{:S(2)}, u32[]{:S(2)}) %all-to-all-start) | async-done | bytes 409632 | tf_op jit(solution)/shard_map/all_to_all | solution.py:406
  (54 shorter events, 11.4 us)
Async XLA Ops:
  0.6 8.0 %collective-permute-start.3 = (bf16[257,320]{1,0:T(8,128)(2,1)}, bf16[257,320]{1,0:T(8,128)(2,1)S(1)}, u32[]{:S(2)}, u32[]{:S(2)}) collective-permute-start(bf16[257,320]{1,0:T(8,128)(2,1)} %bitcast.11), channel_id=1, source_target_pairs={{0,2},{2,0},{1,3},{3,1},{4,6},{6,4},{5,7},{7,5},{8,10},{10,8},{9,1... | collective-permute-start | bytes 493448 | tf_op jit(solution)/shard_map/ppermute | solution.py:264
  2.9 3.6 %copy-start.2 = (bf16[1,257,320]{2,1,0:T(8,128)(2,1)S(1)}, bf16[1,257,320]{2,1,0:T(8,128)(2,1)}, u32[]{:S(2)}) copy-start(bf16[1,257,320]{2,1,0:T(8,128)(2,1)} %param.4) | copy-start | bytes 493444
  3.9 1.7 %copy-start = (bf16[3,1280,320]{1,2,0:T(8,128)(2,1)S(1)}, bf16[3,1280,320]{1,2,0:T(8,128)(2,1)}, u32[]{:S(2)}) copy-start(bf16[3,1280,320]{1,2,0:T(8,128)(2,1)} %param.6) | copy-start | bytes 7372804
  5.6 6.6 %copy-start.1 = (bf16[320,1280]{1,0:T(8,128)(2,1)S(1)}, bf16[320,1280]{1,0:T(8,128)(2,1)}, u32[]{:S(2)}) copy-start(bf16[320,1280]{1,0:T(8,128)(2,1)} %w_out.1) | copy-start | bytes 2457604
  6.4 5.8 %collective-permute-start = (bf16[257,320]{1,0:T(8,128)(2,1)S(1)}, bf16[257,320]{1,0:T(8,128)(2,1)S(1)}, u32[]{:S(2)}, u32[]{:S(2)}) collective-permute-start(bf16[257,320]{1,0:T(8,128)(2,1)S(1)} %get-tuple-element.25.t0), channel_id=1, source_target_pairs={{0,2},{2,0},{1,3},{3,1},{4,6},{6,4},{5,7},{7,5},{8,10},{10,8},{9,1... | collective-permute-start | bytes 493448 | tf_op jit(solution)/shard_map/ppermute | solution.py:275
  6.5 6.0 %collective-permute-start.4 = (bf16[257,320]{1,0:T(8,128)(2,1)S(1)}, bf16[257,320]{1,0:T(8,128)(2,1)S(1)}, u32[]{:S(2)}, u32[]{:S(2)}) collective-permute-start(bf16[257,320]{1,0:T(8,128)(2,1)S(1)} %bitcast.12), channel_id=1, source_target_pairs={{0,1},{1,0},{2,3},{3,2},{4,5},{5,4},{6,7},{7,6},{8,9},{9,8},{10,11... | collective-permute-start | bytes 493448 | tf_op jit(solution)/shard_map/ppermute | solution.py:265
  8.6 3.8 %collective-permute-start.5 = (bf16[257,320]{1,0:T(8,128)(2,1)S(1)}, bf16[257,320]{1,0:T(8,128)(2,1)S(1)}, u32[]{:S(2)}, u32[]{:S(2)}) collective-permute-start(bf16[257,320]{1,0:T(8,128)(2,1)S(1)} %collective-permute-done.3.zy), channel_id=1, source_target_pairs={{0,1},{1,0},{2,3},{3,2},{4,5},{5,4},{6,7},{7,6},{8,9},{9,8},{10,11... | collective-permute-start | bytes 493448 | tf_op jit(solution)/shard_map/ppermute | solution.py:274
  8.6 6.8 %collective-permute-start.1 = (bf16[257,320]{1,0:T(8,128)(2,1)S(1)}, bf16[257,320]{1,0:T(8,128)(2,1)S(1)}, u32[]{:S(2)}, u32[]{:S(2)}) collective-permute-start(bf16[257,320]{1,0:T(8,128)(2,1)S(1)} %get-tuple-element.25.t0), channel_id=1, source_target_pairs={{0,1},{1,0},{2,3},{3,2},{4,5},{5,4},{6,7},{7,6},{8,9},{9,8},{10,11... | collective-permute-start | bytes 493448 | tf_op jit(solution)/shard_map/ppermute | solution.py:273
  12.2 3.2 %collective-permute-start.2 = (bf16[257,320]{1,0:T(8,128)(2,1)S(1)}, bf16[257,320]{1,0:T(8,128)(2,1)S(1)}, u32[]{:S(2)}, u32[]{:S(2)}) collective-permute-start(bf16[257,320]{1,0:T(8,128)(2,1)S(1)} %collective-permute-done.ty), channel_id=1, source_target_pairs={{0,1},{1,0},{2,3},{3,2},{4,5},{5,4},{6,7},{7,6},{8,9},{9,8},{10,11... | collective-permute-start | bytes 493448 | tf_op jit(solution)/shard_map/ppermute | solution.py:276
  18.3 1.9 %collective-permute-start.6 = (bf16[257,640]{1,0:T(8,128)(2,1)S(1)}, bf16[257,640]{1,0:T(8,128)(2,1)S(1)}, u32[]{:S(2)}, u32[]{:S(2)}) collective-permute-start(bf16[257,640]{1,0:T(8,128)(2,1)S(1)} %get-tuple-element.30), channel_id=1, source_target_pairs={{0,1},{1,0},{2,3},{3,2},{4,5},{5,4},{6,7},{7,6},{8,9},{9,8},{10,11... | collective-permute-start | bytes 986888 | tf_op jit(solution)/shard_map/ppermute | solution.py:244
  20.3 10.3 %collective-permute-start.7 = (bf16[257,640]{1,0:T(8,128)(2,1)S(1)}, bf16[257,640]{1,0:T(8,128)(2,1)S(1)}, u32[]{:S(2)}, u32[]{:S(2)}) collective-permute-start(bf16[257,640]{1,0:T(8,128)(2,1)S(1)} %add_convert_fusion.1.chip), channel_id=1, source_target_pairs={{0,2},{2,0},{1,3},{3,1},{4,6},{6,4},{5,7},{7,5},{8,10},{10,8},{9,1... | collective-permute-start | bytes 986888 | tf_op jit(solution)/shard_map/ppermute | solution.py:245
  21.3 9.3 %collective-permute-start.8 = (bf16[257,640]{1,0:T(8,128)(2,1)S(1)}, bf16[257,640]{1,0:T(8,128)(2,1)S(1)}, u32[]{:S(2)}, u32[]{:S(2)}) collective-permute-start(bf16[257,640]{1,0:T(8,128)(2,1)S(1)} %add_convert_fusion.1.chip), channel_id=1, source_target_pairs={{0,1},{1,0},{2,3},{3,2},{4,5},{5,4},{6,7},{7,6},{8,9},{9,8},{10,11... | collective-permute-start | bytes 986888 | tf_op jit(solution)/shard_map/ppermute | solution.py:247
  30.6 1.6 %collective-permute-start.9 = (bf16[257,640]{1,0:T(8,128)(2,1)S(1)}, bf16[257,640]{1,0:T(8,128)(2,1)S(1)}, u32[]{:S(2)}, u32[]{:S(2)}) collective-permute-start(bf16[257,640]{1,0:T(8,128)(2,1)S(1)} %collective-permute-done.7.far), channel_id=1, source_target_pairs={{0,1},{1,0},{2,3},{3,2},{4,5},{5,4},{6,7},{7,6},{8,9},{9,8},{10,11... | collective-permute-start | bytes 986888 | tf_op jit(solution)/shard_map/ppermute | solution.py:246
  35.6 1.7 %collective-permute-start.10 = (bf16[257,640]{1,0:T(8,128)(2,1)S(1)}, bf16[257,640]{1,0:T(8,128)(2,1)S(1)}, u32[]{:S(2)}, u32[]{:S(2)}) collective-permute-start(bf16[257,640]{1,0:T(8,128)(2,1)S(1)} %get-tuple-element.34), channel_id=1, source_target_pairs={{0,1},{1,0},{2,3},{3,2},{4,5},{5,4},{6,7},{7,6},{8,9},{9,8},{10,11... | collective-permute-start | bytes 986888 | tf_op jit(solution)/shard_map/ppermute | solution.py:244
  37.4 10.1 %collective-permute-start.11 = (bf16[257,640]{1,0:T(8,128)(2,1)S(1)}, bf16[257,640]{1,0:T(8,128)(2,1)S(1)}, u32[]{:S(2)}, u32[]{:S(2)}) collective-permute-start(bf16[257,640]{1,0:T(8,128)(2,1)S(1)} %add_convert_fusion.chip), channel_id=1, source_target_pairs={{0,2},{2,0},{1,3},{3,1},{4,6},{6,4},{5,7},{7,5},{8,10},{10,8},{9,1... | collective-permute-start | bytes 986888 | tf_op jit(solution)/shard_map/ppermute | solution.py:245
  38.5 9.0 %collective-permute-start.12 = (bf16[257,640]{1,0:T(8,128)(2,1)S(1)}, bf16[257,640]{1,0:T(8,128)(2,1)S(1)}, u32[]{:S(2)}, u32[]{:S(2)}) collective-permute-start(bf16[257,640]{1,0:T(8,128)(2,1)S(1)} %add_convert_fusion.chip), channel_id=1, source_target_pairs={{0,1},{1,0},{2,3},{3,2},{4,5},{5,4},{6,7},{7,6},{8,9},{9,8},{10,11... | collective-permute-start | bytes 986888 | tf_op jit(solution)/shard_map/ppermute | solution.py:247
  47.5 1.6 %collective-permute-start.13 = (bf16[257,640]{1,0:T(8,128)(2,1)S(1)}, bf16[257,640]{1,0:T(8,128)(2,1)S(1)}, u32[]{:S(2)}, u32[]{:S(2)}) collective-permute-start(bf16[257,640]{1,0:T(8,128)(2,1)S(1)} %collective-permute-done.11.far), channel_id=1, source_target_pairs={{0,1},{1,0},{2,3},{3,2},{4,5},{5,4},{6,7},{7,6},{8,9},{9,8},{10,11... | collective-permute-start | bytes 986888 | tf_op jit(solution)/shard_map/ppermute | solution.py:246
  50.9 27.2 %collective-permute-start.22 = (bf16[640,320]{1,0:T(8,128)(2,1)S(1)}, bf16[640,320]{1,0:T(8,128)(2,1)S(1)}, u32[]{:S(2)}, u32[]{:S(2)}) collective-permute-start(bf16[640,320]{1,0:T(8,128)(2,1)S(1)} %get-tuple-element.44), channel_id=1, source_target_pairs={{0,32},{32,0},{1,33},{33,1},{2,34},{34,2},{3,35},{35,3},{4,36},{36... | collective-permute-start | bytes 1228808 | tf_op jit(solution)/shard_map/ppermute | solution.py:326
  53.2 14.2 %collective-permute-start.14 = (bf16[640,257]{1,0:T(8,128)(2,1)S(1)}, bf16[640,257]{1,0:T(8,128)(2,1)S(1)}, u32[]{:S(2)}, u32[]{:S(2)}) collective-permute-start(bf16[640,257]{1,0:T(8,128)(2,1)S(1)} %shard_map.77), channel_id=1, source_target_pairs={{0,64},{64,0},{128,192},{192,128},{1,65},{65,1},{129,193},{193,129... | collective-permute-start | bytes 986888 | tf_op jit(solution)/shard_map/ppermute | solution.py:323
  54.8 21.3 %collective-permute-start.18 = (bf16[640,257]{1,0:T(8,128)(2,1)S(1)}, bf16[640,257]{1,0:T(8,128)(2,1)S(1)}, u32[]{:S(2)}, u32[]{:S(2)}) collective-permute-start(bf16[640,257]{1,0:T(8,128)(2,1)S(1)} %shard_map.81), channel_id=1, source_target_pairs={{0,192},{64,128},{128,64},{192,0},{1,193},{65,129},{129,65},{193,1... | collective-permute-start | bytes 986888 | tf_op jit(solution)/shard_map/ppermute | solution.py:323
  59.4 16.6 %collective-permute-start.19 = (bf16[257,512]{1,0:T(8,128)(2,1)S(1)}, bf16[257,512]{1,0:T(8,128)(2,1)S(1)}, u32[]{:S(2)}, u32[]{:S(2)}) collective-permute-start(bf16[257,512]{1,0:T(8,128)(2,1)S(1)} %get-tuple-element.42.g), channel_id=1, source_target_pairs={{0,192},{64,128},{128,64},{192,0},{1,193},{65,129},{129,65},{193,1... | collective-permute-start | bytes 789512 | tf_op jit(solution)/shard_map/ppermute | solution.py:323
  60.7 11.4 %collective-permute-start.15 = (bf16[257,448]{1,0:T(8,128)(2,1)S(1)}, bf16[257,448]{1,0:T(8,128)(2,1)S(1)}, u32[]{:S(2)}, u32[]{:S(2)}) collective-permute-start(bf16[257,448]{1,0:T(8,128)(2,1)S(1)} %get-tuple-element.41.g), channel_id=1, source_target_pairs={{0,64},{64,0},{128,192},{192,128},{1,65},{65,1},{129,193},{193,129... | collective-permute-start | bytes 690824 | tf_op jit(solution)/shard_map/ppermute | solution.py:323
  72.4 9.9 %collective-permute-start.16 = (bf16[320,448]{1,0:T(8,128)(2,1)S(1)}, bf16[320,448]{1,0:T(8,128)(2,1)S(1)}, u32[]{:S(2)}, u32[]{:S(2)}) collective-permute-start(bf16[320,448]{1,0:T(8,128)(2,1)S(1)} %shard_map.79), channel_id=1, source_target_pairs={{0,192},{64,128},{128,64},{192,0},{1,193},{65,129},{129,65},{193,1... | collective-permute-start | bytes 860168 | tf_op jit(solution)/shard_map/ppermute | solution.py:323
  76.4 11.6 %collective-permute-start.20 = (bf16[320,512]{1,0:T(8,128)(2,1)S(1)}, bf16[320,512]{1,0:T(8,128)(2,1)S(1)}, u32[]{:S(2)}, u32[]{:S(2)}) collective-permute-start(bf16[320,512]{1,0:T(8,128)(2,1)S(1)} %shard_map.83), channel_id=1, source_target_pairs={{0,32},{32,0},{1,33},{33,1},{2,34},{34,2},{3,35},{35,3},{4,36},{36... | collective-permute-start | bytes 983048 | tf_op jit(solution)/shard_map/ppermute | solution.py:326
  78.2 10.1 %collective-permute-start.23 = (bf16[320,320]{1,0:T(8,128)(2,1)S(1)}, bf16[320,320]{1,0:T(8,128)(2,1)S(1)}, u32[]{:S(2)}, u32[]{:S(2)}) collective-permute-start(bf16[320,320]{1,0:T(8,128)(2,1)S(1)} %get-tuple-element.51), channel_id=1, source_target_pairs={{0,64},{64,0},{128,192},{192,128},{1,65},{65,1},{129,193},{193,129... | collective-permute-start | bytes 614408 | tf_op jit(solution)/shard_map/ppermute | solution.py:323
  82.4 7.5 %collective-permute-start.17 = (bf16[160,448]{1,0:T(8,128)(2,1)S(1)}, bf16[160,448]{1,0:T(8,128)(2,1)S(1)}, u32[]{:S(2)}, u32[]{:S(2)}) collective-permute-start(bf16[160,448]{1,0:T(8,128)(2,1)S(1)} %get-tuple-element.54), channel_id=1, source_target_pairs={{0,32},{32,0},{1,33},{33,1},{2,34},{34,2},{3,35},{35,3},{4,36},{36... | collective-permute-start | bytes 430088 | tf_op jit(solution)/shard_map/ppermute | solution.py:326
  88.1 6.5 %collective-permute-start.21 = (bf16[160,512]{1,0:T(8,128)(2,1)S(1)}, bf16[160,512]{1,0:T(8,128)(2,1)S(1)}, u32[]{:S(2)}, u32[]{:S(2)}) collective-permute-start(bf16[160,512]{1,0:T(8,128)(2,1)S(1)} %get-tuple-element.52), channel_id=1, source_target_pairs={{0,64},{64,0},{128,192},{192,128},{1,65},{65,1},{129,193},{193,129... | collective-permute-start | bytes 491528 | tf_op jit(solution)/shard_map/ppermute | solution.py:323
  88.4 6.2 %collective-permute-start.24 = (bf16[160,320]{1,0:T(8,128)(2,1)S(1)}, bf16[160,320]{1,0:T(8,128)(2,1)S(1)}, u32[]{:S(2)}, u32[]{:S(2)}) collective-permute-start(bf16[160,320]{1,0:T(8,128)(2,1)S(1)} %get-tuple-element.56), channel_id=1, source_target_pairs={{0,192},{64,128},{128,64},{192,0},{1,193},{65,129},{129,65},{193,1... | collective-permute-start | bytes 307208 | tf_op jit(solution)/shard_map/ppermute | solution.py:323
  95.6 20.5 %all-to-all-start = ((bf16[8,200,128]{2,1,0:T(8,128)(2,1)}), bf16[8,200,128]{2,1,0:T(8,128)(2,1)S(1)}, u32[]{:S(2)}, u32[]{:S(2)}) async-start(bf16[8,200,128]{2,1,0:T(8,128)(2,1)} %shard_map.85), calls=%async_computation | async-start | bytes 819200 | tf_op jit(solution)/shard_map/all_to_all | solution.py:406

commit v5 on v4

--- a/solution.py
+++ b/solution.py
@@ -158,6 +158,41 @@
     oth_o[...] = input_back(OTHER, grads_o, w)
 
 
+LANES = 128
+PART = 160
+
+
+def folded(cols):
+    return PART * cols // LANES
+
+
+def fold(out, value):
+    rows, cols = value.shape
+    size = folded(cols)
+    whole = cols // LANES
+    for p in range(rows // PART):
+        top, base = p * PART, p * size
+        for b in range(whole):
+            block = value[top : top + PART, b * LANES : (b + 1) * LANES]
+            out[base + b * PART : base + (b + 1) * PART, :] = block.astype(out.dtype)
+        if cols % LANES:
+            base += whole * PART
+            for k in range(2):
+                block = value[top + k * PART // 2 : top + (k + 1) * PART // 2, whole * LANES :]
+                out[base : base + PART // 2, k * LANES // 2 : (k + 1) * LANES // 2] = block.astype(out.dtype)
+
+
+def unfold(out, at, value, cols):
+    whole = cols // LANES
+    for b in range(whole):
+        out[:, at + b * LANES : at + (b + 1) * LANES] = value[b * PART : (b + 1) * PART, :]
+    if cols % LANES:
+        at += whole * LANES
+        for k in range(2):
+            block = value[whole * PART :, k * LANES // 2 : (k + 1) * LANES // 2]
+            out[k * PART // 2 : (k + 1) * PART // 2, at : at + LANES // 2] = block
+
+
 def total_body(picks, chip, far, chip_c, far_c, normal, inv, cot, term, mine, att, imp_o, total_o, tt_o, out, spot, rows):
     spot[...] = put_term(spot, chip, far, chip_c, far_c, normal, inv) + term[...]
     narrow = mine.shape[1]
@@ -171,7 +206,7 @@
     total_o[...] = total
     tt_o[...] = total.T
     gather_rows(tt_o, rows, picks, narrow)
-    out[...] = dot(rows[...], att[...]).astype(bf16)
+    fold(out, dot(rows[...], att[...]))
 
 
 def last_body(total, w_out, qkv, probs, one_o, two_o, grads):
@@ -203,16 +238,21 @@
     out[...] = dot(rows[...], g[...]).astype(out.dtype)
 
 
+def folded_rows_body(picks, x, g, out, rows):
+    gather_rows(x, rows, picks, x.shape[0] // 4)
+    fold(out, dot(rows[...], g[...]))
+
+
 def both_body(start, mine, x, g, out):
-    at = slice(start, start + out.shape[0])
-    out[...] = (mine[at, :] + dot(x[at, :], g[...])).astype(bf16)
-
-
-def pack_body(k1, g1, k2, g2, k3, g3, out, spot):
+    at = slice(start, start + x.shape[0] // 2)
+    fold(out, mine[at, :] + dot(x[at, :], g[...]))
+
+
+def pack_body(widths, k1, g1, k2, g2, k3, g3, out, spot):
     at = 0
-    for k, g in ((k1, g1), (k2, g2), (k3, g3)):
-        spot[:, at : at + k.shape[1]] = k[...].astype(f32) + g[...].astype(f32)
-        at += k.shape[1]
+    for cols, k, g in zip(widths, (k1, k2, k3), (g1, g2, g3)):
+        unfold(spot, at, k[...].astype(f32) + g[...].astype(f32), cols)
+        at += cols
     nz, _, lanes = out.shape
     each = spot.shape[0] // nz
     for z in range(nz):
@@ -339,7 +379,7 @@
             like((tokens, narrow), f32),
             wide,
             like((width, tokens), bf16),
-            like((4 * rows, three), bf16),
+            like((4 * folded(three), LANES), bf16),
         ),
         (*sums, normal, inv, cot, term, cotangent[0], att),
         [pltpu.VMEM((tokens, width), f32), tall],
@@ -369,35 +409,42 @@
     def both(start, mine, x, g):
         return call(
             functools.partial(both_body, start * rows),
-            (like((2 * rows, g.shape[1]), bf16),),
+            (like((2 * folded(g.shape[1]), LANES), bf16),),
             (mine, x, g),
             flops=2 * tokens * 2 * rows * g.shape[1],
         )[0]
 
     m2 = block(keep_two, xt, g_two, f32)
     m1 = block(keep_one, xt, g_one, f32)
-    k3 = block(keep_three, tt, att, bf16)
-
-    def at(value, start, count):
-        return value[start * rows : (start + count) * rows]
+    (k3,) = call(
+        functools.partial(folded_rows_body, keep_three),
+        (like((4 * folded(three), LANES), bf16),),
+        (tt, att),
+        [tall],
+        flops=2 * tokens * 4 * rows * three,
+    )
+
+    def at(value, start, count, parts):
+        size = value.shape[0] // parts
+        return value[start * size : (start + count) * size]
 
     h2 = swap_yh(both(2, m2, x_two, p_two))
     h1 = swap_x(both(2, m1, x_one, p_one), 3)
-    h3 = swap_x(add(at(k3, 2, 2), at(g3, 2, 2)), 1)
+    h3 = swap_x(add(at(k3, 2, 2, 4), at(g3, 2, 2, 4)), 1)
     k2 = both(0, m2, x_two, p_two)
     k1 = both(0, m1, x_one, p_one)
-    k3 = add(at(k3, 0, 2), at(g3, 0, 2))
+    k3 = add(at(k3, 0, 2, 4), at(g3, 0, 2, 4))
 
     def last_half(k, h, swap):
-        got = swap(add(at(k, 1, 1), at(h, 1, 1)))
-        return add(at(k, 0, 1), at(h, 0, 1)), got
+        got = swap(add(at(k, 1, 1, 2), at(h, 1, 1, 2)))
+        return add(at(k, 0, 1, 2), at(h, 0, 1, 2)), got
 
     e2 = last_half(k2, h2, lambda v: swap_x(v, 1))
     e1 = last_half(k1, h1, swap_yh)
     e3 = last_half(k3, h3, lambda v: swap_x(v, 3))
     dense = each * width // 128
     (packed,) = call(
-        pack_body,
+        functools.partial(pack_body, (one, two, three)),
         (like((nz, dense, 128), bf16),),
         (*e1, *e2, *e3),
         [pltpu.VMEM((rows, width), f32)],

time: 117 us -> 118 us (level)
  starting transfers between devices: 28 us -> 29.4 us
  waiting for transfers between devices: 63.3 us -> 62.1 us
    ppermute x8, starting transfers between devices: 8.61 us -> 9.99 us  [swap_x(): return lax.ppermute(value, 'x', [(i, i ^ by) for i in range(nx)])]
    ppermute x8, waiting for transfers between devices: 18.9 us -> 17.6 us  [swap_x(): return lax.ppermute(value, 'x', [(i, i ^ by) for i in range(nx)])]
  transfers between devices with their start and end apart: 26 -> 26, of which waited for: 15 -> 14; matrix products, arithmetic and copies ran while one was open for 2% -> 2% of each run, Pallas kernels for 9% -> 9%
where the time goes in v5:
time: 118 us; the launch traced here: 117 us
  waiting for transfers between devices  62.1 us (53%)
  starting transfers between devices  29.4 us (25%)
  Pallas kernels  20.6 us (17%)
  local copies, waits for them, and re-layouts  3.91 us (3%)
    pallas_call x20, Pallas kernels, call(): pl.pallas_call(body, out_shape=outs, in_specs=[vmem] * len(ins), out_spec...  20.6 us
    ppermute x2, waiting for transfers between devices, mp_sum(): far = lax.ppermute(chip, 'yl', SWAP)  18.2 us
    ppermute x8, waiting for transfers between devices, swap_x(): return lax.ppermute(value, 'x', [(i, i ^ by) for i in range(nx)])  17.6 us
    all_to_all x1, waiting for transfers between devices, shards(): got = lax.all_to_all(packed, 'z', 0, 0, tiled=True)  10.9 us
    ppermute x8, starting transfers between devices, swap_x(): return lax.ppermute(value, 'x', [(i, i ^ by) for i in range(nx)])  9.99 us
    all_to_all x1, starting transfers between devices, shards(): got = lax.all_to_all(packed, 'z', 0, 0, tiled=True)  8.46 us
    ppermute x3, waiting for transfers between devices, swap_yh(): return lax.ppermute(value, 'yh', SWAP)  5.53 us
    ppermute x3, starting transfers between devices, swap_yh(): return lax.ppermute(value, 'yh', SWAP)  5.02 us
  transfers between devices with their start and end apart: 26, of which 14 were waited for; matrix products, arithmetic and copies ran while one was open for 2% of the time, Pallas kernels for 9%

profile of v5, /device:TPU:8, one launch (start us, length us, event | category | flops | bytes accessed | tf_op | source)
XLA Modules:
  0.0 117.4 jit_solution(7610688696556334)
XLA Ops:
  0.6 2.2 %collective-permute-start.3 = (bf16[257,320]{1,0:T(8,128)(2,1)}, bf16[257,320]{1,0:T(8,128)(2,1)S(1)}, u32[]{:S(2)}, u32[]{:S(2)}) collective-permute-start(bf16[257,320]{1,0:T(8,128)(2,1)} %bitcast.11), channel_id=1, source_target_pairs={{0,2},{2,0},{1,3},{3,1},{4,6},{6,4},{5,7},{7,5},{8,10},{10,8},{9,1... | collective-permute-start | bytes 493448 | tf_op jit(solution)/shard_map/ppermute | solution.py:304
  2.9 1.1 copy.10
  4.0 1.7 %copy-done = bf16[3,1280,320]{1,2,0:T(8,128)(2,1)S(1)} copy-done((bf16[3,1280,320]{1,2,0:T(8,128)(2,1)S(1)}, bf16[3,1280,320]{1,2,0:T(8,128)(2,1)}, u32[]{:S(2)}) %copy-start) | copy-done | bytes 2457624
  6.6 2.0 %collective-permute-done.3.zy = bf16[257,320]{1,0:T(8,128)(2,1)S(1)} collective-permute-done((bf16[257,320]{1,0:T(8,128)(2,1)}, bf16[257,320]{1,0:T(8,128)(2,1)S(1)}, u32[]{:S(2)}, u32[]{:S(2)}) %collective-permute-start.3) | collective-permute-done | bytes 164512 | tf_op jit(solution)/shard_map/ppermute | solution.py:304
  9.2 3.1 %collective-permute-done.ty = bf16[257,320]{1,0:T(8,128)(2,1)S(1)} collective-permute-done((bf16[257,320]{1,0:T(8,128)(2,1)S(1)}, bf16[257,320]{1,0:T(8,128)(2,1)S(1)}, u32[]{:S(2)}, u32[]{:S(2)}) %collective-permute-start) | collective-permute-done | bytes 164512 | tf_op jit(solution)/shard_map/ppermute | solution.py:315
  12.5 2.9 %shard_map.69 = (bf16[257,1280]{1,0:T(8,128)(2,1)S(1)}, bf16[1280,257]{1,0:T(8,128)(2,1)S(1)}, f32[257,128]{1,0:T(8,128)S(1)}, bf16[12,257,80]{2,1,0:T(8,128)(2,...) custom-call(bf16[257,320]{1,0:T(8,128)(2,1)S(1)} %bitcast.13, ...), custom_call_target="tpu_custom_call" | custom-call | flops 716145920 | bytes 6277648 | tf_op jit(solution)/shard_map/pallas_call | solution.py:35
  15.4 2.9 %shard_map.70 = (bf16[257,1280]{1,0:T(8,128)(2,1)S(1)}, bf16[257,960]{1,0:T(8,128)(2,1)S(1)}, bf16[257,640]{1,0:T(8,128)(2,1)S(1)}) custom-call(bf16[257,320]{1,0:T(8,128)(2,1)S(1)} %get-tuple-element.25.t0, bf16[257,320]{1,0:T(8,128)(2,1)S(1)} %collective-permute-done.ty, bf16[257,320]{1,0:T(8,128)(2,1)S(1)} %collective-permute-done.1.tc, ...), custom_call_target="tpu_custom_call" | custom-call | flops 800688640 | bytes 6965264 | tf_op jit(solution)/shard_map/pallas_call | solution.py:35
  20.3 1.0 collective-permute-start.7
  21.4 9.2 %collective-permute-done.7.far = bf16[257,640]{1,0:T(8,128)(2,1)S(1)} collective-permute-done((bf16[257,640]{1,0:T(8,128)(2,1)S(1)}, bf16[257,640]{1,0:T(8,128)(2,1)S(1)}, u32[]{:S(2)}, u32[]{:S(2)}) %collective-permute-start.7) | collective-permute-done | bytes 328992 | tf_op jit(solution)/shard_map/ppermute | solution.py:285
  30.6 1.6 %collective-permute-done.9.far_c = bf16[257,640]{1,0:T(8,128)(2,1)S(1)} collective-permute-done((bf16[257,640]{1,0:T(8,128)(2,1)S(1)}, bf16[257,640]{1,0:T(8,128)(2,1)S(1)}, u32[]{:S(2)}, u32[]{:S(2)}) %collective-permute-start.9) | collective-permute-done | bytes 328992 | tf_op jit(solution)/shard_map/ppermute | solution.py:286
  32.2 3.4 %shard_map.72 = (f32[257,1280]{1,0:T(8,128)S(1)}, bf16[257,960]{1,0:T(8,128)(2,1)S(1)}, bf16[257,640]{1,0:T(8,128)(2,1)S(1)}) custom-call(bf16[257,640]{1,0:T(8,128)(2,1)S(1)} %add_convert_fusion.1.chip, bf16[257,640]{1,0:T(8,128)(2,1)S(1)} %collective-permute-done.7.far, bf16[257,640]{1,0:T(8,128)(2,1)S(1)} %collective-permute-done.8.chip_c, ...), custom_call_target="tpu_custom_call" | custom-call | flops 800688640 | bytes 9070608 | tf_op jit(solution)/shard_map/pallas_call | solution.py:35
  37.4 1.0 collective-permute-start.11
  38.5 9.0 %collective-permute-done.11.far = bf16[257,640]{1,0:T(8,128)(2,1)S(1)} collective-permute-done((bf16[257,640]{1,0:T(8,128)(2,1)S(1)}, bf16[257,640]{1,0:T(8,128)(2,1)S(1)}, u32[]{:S(2)}, u32[]{:S(2)}) %collective-permute-start.11) | collective-permute-done | bytes 328992 | tf_op jit(solution)/shard_map/ppermute | solution.py:285
  47.5 1.6 %collective-permute-done.13.far_c = bf16[257,640]{1,0:T(8,128)(2,1)S(1)} collective-permute-done((bf16[257,640]{1,0:T(8,128)(2,1)S(1)}, bf16[257,640]{1,0:T(8,128)(2,1)S(1)}, u32[]{:S(2)}, u32[]{:S(2)}) %collective-permute-start.13) | collective-permute-done | bytes 328992 | tf_op jit(solution)/shard_map/ppermute | solution.py:286
  49.1 1.8 %shard_map.74 = (f32[257,320]{1,0:T(8,128)S(1)}, bf16[257,1280]{1,0:T(8,128)(2,1)S(1)}, bf16[1280,257]{1,0:T(8,128)(2,1)S(1)}, bf16[1600,128]{1,0:T(8,128)(2,1)S(1)}) custom-call(bf16[257,640]{1,0:T(8,128)(2,1)S(1)} %add_convert_fusion.chip, bf16[257,640]{1,0:T(8,128)(2,1)S(1)} %collective-permute-done.11.far, ...), custom_call_target="tpu_custom_call" | custom-call | flops 210534400 | bytes 6626944 | tf_op jit(solution)/shard_map/pallas_call | solution.py:35
  51.0 2.2 %collective-permute-start.22 = (bf16[1600,128]{1,0:T(8,128)(2,1)S(1)}, bf16[1600,128]{1,0:T(8,128)(2,1)S(1)}, u32[]{:S(2)}, u32[]{:S(2)}) collective-permute-start(bf16[1600,128]{1,0:T(8,128)(2,1)S(1)} %get-tuple-element.44), channel_id=1, source_target_pairs={{0,32},{32,0},{1,33},{33,1},{2,34},{34,2},{3,35},{35,3},{4,36},{36... | collective-permute-start | bytes 1228808 | tf_op jit(solution)/shard_map/ppermute | solution.py:366
  53.2 1.6 %collective-permute-start.14 = (bf16[640,257]{1,0:T(8,128)(2,1)S(1)}, bf16[640,257]{1,0:T(8,128)(2,1)S(1)}, u32[]{:S(2)}, u32[]{:S(2)}) collective-permute-start(bf16[640,257]{1,0:T(8,128)(2,1)S(1)} %shard_map.77), channel_id=1, source_target_pairs={{0,64},{64,0},{128,192},{192,128},{1,65},{65,1},{129,193},{193,129... | collective-permute-start | bytes 986888 | tf_op jit(solution)/shard_map/ppermute | solution.py:363
  54.9 2.2 %collective-permute-start.18 = (bf16[640,257]{1,0:T(8,128)(2,1)S(1)}, bf16[640,257]{1,0:T(8,128)(2,1)S(1)}, u32[]{:S(2)}, u32[]{:S(2)}) collective-permute-start(bf16[640,257]{1,0:T(8,128)(2,1)S(1)} %shard_map.81), channel_id=1, source_target_pairs={{0,192},{64,128},{128,64},{192,0},{1,193},{65,129},{129,65},{193,1... | collective-permute-start | bytes 986888 | tf_op jit(solution)/shard_map/ppermute | solution.py:363
  57.0 2.4 %shard_map.75 = (bf16[257,448]{1,0:T(8,128)(2,1)S(1)}, bf16[257,512]{1,0:T(8,128)(2,1)S(1)}) custom-call(bf16[257,1280]{1,0:T(8,128)(2,1)S(1)} %get-tuple-element.40.total, bf16[320,1280]{1,0:T(8,128)(2,1)S(1)} %shard_map.68.w_out, bf16[12,257,80]{2,1,0:T(8,128)(2,1)S(1)} %get-tuple-element.27.qkv, f32[4,257,257]{2,1,0:T(8,128)S(1)} %get-tuple-element.28.probs), custom_call_target="tpu_custom_call" | custom-call | flops 379619840 | bytes 3520784 | tf_op jit(solution)/shard_map/pallas_call | solution.py:35
  61.6 5.8 %collective-permute-done.14.x = bf16[640,257]{1,0:T(8,128)(2,1)S(1)} collective-permute-done((bf16[640,257]{1,0:T(8,128)(2,1)S(1)}, bf16[640,257]{1,0:T(8,128)(2,1)S(1)}, u32[]{:S(2)}, u32[]{:S(2)}) %collective-permute-start.14) | collective-permute-done | bytes 328992 | tf_op jit(solution)/shard_map/ppermute | solution.py:363
  67.4 4.7 %collective-permute-done.15.g = bf16[257,448]{1,0:T(8,128)(2,1)S(1)} collective-permute-done((bf16[257,448]{1,0:T(8,128)(2,1)S(1)}, bf16[257,448]{1,0:T(8,128)(2,1)S(1)}, u32[]{:S(2)}, u32[]{:S(2)}) %collective-permute-start.15) | collective-permute-done | bytes 230304 | tf_op jit(solution)/shard_map/ppermute | solution.py:363
  72.5 2.8 %collective-permute-start.16 = (bf16[1120,128]{1,0:T(8,128)(2,1)S(1)}, bf16[1120,128]{1,0:T(8,128)(2,1)S(1)}, u32[]{:S(2)}, u32[]{:S(2)}) collective-permute-start(bf16[1120,128]{1,0:T(8,128)(2,1)S(1)} %shard_map.79), channel_id=1, source_target_pairs={{0,192},{64,128},{128,64},{192,0},{1,193},{65,129},{129,65},{193,1... | collective-permute-start | bytes 860168 | tf_op jit(solution)/shard_map/ppermute | solution.py:363
  77.1 1.3 %collective-permute-start.20 = (bf16[1280,128]{1,0:T(8,128)(2,1)S(1)}, bf16[1280,128]{1,0:T(8,128)(2,1)S(1)}, u32[]{:S(2)}, u32[]{:S(2)}) collective-permute-start(bf16[1280,128]{1,0:T(8,128)(2,1)S(1)} %shard_map.83), channel_id=1, source_target_pairs={{0,32},{32,0},{1,33},{33,1},{2,34},{34,2},{3,35},{35,3},{4,36},{36... | collective-permute-start | bytes 983048 | tf_op jit(solution)/shard_map/ppermute | solution.py:366
  79.2 2.3 %collective-permute-done.16 = bf16[1120,128]{1,0:T(8,128)(2,1)S(1)} collective-permute-done((bf16[1120,128]{1,0:T(8,128)(2,1)S(1)}, bf16[1120,128]{1,0:T(8,128)(2,1)S(1)}, u32[]{:S(2)}, u32[]{:S(2)}) %collective-permute-start.16) | collective-permute-done | bytes 286752 | tf_op jit(solution)/shard_map/ppermute | solution.py:363
  81.6 1.5 %collective-permute-start.17 = (bf16[560,128]{1,0:T(8,128)(2,1)S(1)}, bf16[560,128]{1,0:T(8,128)(2,1)S(1)}, u32[]{:S(2)}, u32[]{:S(2)}) collective-permute-start(bf16[560,128]{1,0:T(8,128)(2,1)S(1)} %get-tuple-element.54), channel_id=1, source_target_pairs={{0,32},{32,0},{1,33},{33,1},{2,34},{34,2},{3,35},{35,3},{4,36},{36... | collective-permute-start | bytes 430088 | tf_op jit(solution)/shard_map/ppermute | solution.py:366
  83.1 5.5 %collective-permute-done.20 = bf16[1280,128]{1,0:T(8,128)(2,1)S(1)} collective-permute-done((bf16[1280,128]{1,0:T(8,128)(2,1)S(1)}, bf16[1280,128]{1,0:T(8,128)(2,1)S(1)}, u32[]{:S(2)}, u32[]{:S(2)}) %collective-permute-start.20) | collective-permute-done | bytes 327712 | tf_op jit(solution)/shard_map/ppermute | solution.py:366
  89.1 1.2 %collective-permute-start.24 = (bf16[400,128]{1,0:T(8,128)(2,1)S(1)}, bf16[400,128]{1,0:T(8,128)(2,1)S(1)}, u32[]{:S(2)}, u32[]{:S(2)}) collective-permute-start(bf16[400,128]{1,0:T(8,128)(2,1)S(1)} %get-tuple-element.56), channel_id=1, source_target_pairs={{0,192},{64,128},{128,64},{192,0},{1,193},{65,129},{129,65},{193,1... | collective-permute-start | bytes 307208 | tf_op jit(solution)/shard_map/ppermute | solution.py:363
  90.3 4.7 %collective-permute-done.24.g3 = bf16[400,128]{1,0:T(8,128)(2,1)S(1)} collective-permute-done((bf16[400,128]{1,0:T(8,128)(2,1)S(1)}, bf16[400,128]{1,0:T(8,128)(2,1)S(1)}, u32[]{:S(2)}, u32[]{:S(2)}) %collective-permute-start.24) | collective-permute-done | bytes 102432 | tf_op jit(solution)/shard_map/ppermute | solution.py:363
  95.0 1.1 shard_map.85
  96.1 8.5 %all-to-all-start = ((bf16[8,200,128]{2,1,0:T(8,128)(2,1)}), bf16[8,200,128]{2,1,0:T(8,128)(2,1)S(1)}, u32[]{:S(2)}, u32[]{:S(2)}) async-start(bf16[8,200,128]{2,1,0:T(8,128)(2,1)} %shard_map.85), calls=%async_computation | async-start | bytes 819200 | tf_op jit(solution)/shard_map/all_to_all | solution.py:453
  104.6 1.2 copy.7
  105.7 10.9 %all-to-all-done.got = bf16[8,200,128]{2,1,0:T(8,128)(2,1)S(1)} async-done(((bf16[8,200,128]{2,1,0:T(8,128)(2,1)}), bf16[8,200,128]{2,1,0:T(8,128)(2,1)S(1)}, u32[]{:S(2)}, u32[]{:S(2)}) %all-to-all-start) | async-done | bytes 409632 | tf_op jit(solution)/shard_map/all_to_all | solution.py:453
  (54 shorter events, 12.0 us)
Async XLA Ops:
  0.6 8.0 %collective-permute-start.3 = (bf16[257,320]{1,0:T(8,128)(2,1)}, bf16[257,320]{1,0:T(8,128)(2,1)S(1)}, u32[]{:S(2)}, u32[]{:S(2)}) collective-permute-start(bf16[257,320]{1,0:T(8,128)(2,1)} %bitcast.11), channel_id=1, source_target_pairs={{0,2},{2,0},{1,3},{3,1},{4,6},{6,4},{5,7},{7,5},{8,10},{10,8},{9,1... | collective-permute-start | bytes 493448 | tf_op jit(solution)/shard_map/ppermute | solution.py:304
  2.9 3.6 %copy-start.2 = (bf16[1,257,320]{2,1,0:T(8,128)(2,1)S(1)}, bf16[1,257,320]{2,1,0:T(8,128)(2,1)}, u32[]{:S(2)}) copy-start(bf16[1,257,320]{2,1,0:T(8,128)(2,1)} %param.4) | copy-start | bytes 493444
  3.9 1.7 %copy-start = (bf16[3,1280,320]{1,2,0:T(8,128)(2,1)S(1)}, bf16[3,1280,320]{1,2,0:T(8,128)(2,1)}, u32[]{:S(2)}) copy-start(bf16[3,1280,320]{1,2,0:T(8,128)(2,1)} %param.6) | copy-start | bytes 7372804
  5.6 6.6 %copy-start.1 = (bf16[320,1280]{1,0:T(8,128)(2,1)S(1)}, bf16[320,1280]{1,0:T(8,128)(2,1)}, u32[]{:S(2)}) copy-start(bf16[320,1280]{1,0:T(8,128)(2,1)} %w_out.1) | copy-start | bytes 2457604
  6.4 5.8 %collective-permute-start = (bf16[257,320]{1,0:T(8,128)(2,1)S(1)}, bf16[257,320]{1,0:T(8,128)(2,1)S(1)}, u32[]{:S(2)}, u32[]{:S(2)}) collective-permute-start(bf16[257,320]{1,0:T(8,128)(2,1)S(1)} %get-tuple-element.25.t0), channel_id=1, source_target_pairs={{0,2},{2,0},{1,3},{3,1},{4,6},{6,4},{5,7},{7,5},{8,10},{10,8},{9,1... | collective-permute-start | bytes 493448 | tf_op jit(solution)/shard_map/ppermute | solution.py:315
  6.5 6.0 %collective-permute-start.4 = (bf16[257,320]{1,0:T(8,128)(2,1)S(1)}, bf16[257,320]{1,0:T(8,128)(2,1)S(1)}, u32[]{:S(2)}, u32[]{:S(2)}) collective-permute-start(bf16[257,320]{1,0:T(8,128)(2,1)S(1)} %bitcast.12), channel_id=1, source_target_pairs={{0,1},{1,0},{2,3},{3,2},{4,5},{5,4},{6,7},{7,6},{8,9},{9,8},{10,11... | collective-permute-start | bytes 493448 | tf_op jit(solution)/shard_map/ppermute | solution.py:305
  8.6 3.8 %collective-permute-start.5 = (bf16[257,320]{1,0:T(8,128)(2,1)S(1)}, bf16[257,320]{1,0:T(8,128)(2,1)S(1)}, u32[]{:S(2)}, u32[]{:S(2)}) collective-permute-start(bf16[257,320]{1,0:T(8,128)(2,1)S(1)} %collective-permute-done.3.zy), channel_id=1, source_target_pairs={{0,1},{1,0},{2,3},{3,2},{4,5},{5,4},{6,7},{7,6},{8,9},{9,8},{10,11... | collective-permute-start | bytes 493448 | tf_op jit(solution)/shard_map/ppermute | solution.py:314
  8.6 6.8 %collective-permute-start.1 = (bf16[257,320]{1,0:T(8,128)(2,1)S(1)}, bf16[257,320]{1,0:T(8,128)(2,1)S(1)}, u32[]{:S(2)}, u32[]{:S(2)}) collective-permute-start(bf16[257,320]{1,0:T(8,128)(2,1)S(1)} %get-tuple-element.25.t0), channel_id=1, source_target_pairs={{0,1},{1,0},{2,3},{3,2},{4,5},{5,4},{6,7},{7,6},{8,9},{9,8},{10,11... | collective-permute-start | bytes 493448 | tf_op jit(solution)/shard_map/ppermute | solution.py:313
  12.2 3.2 %collective-permute-start.2 = (bf16[257,320]{1,0:T(8,128)(2,1)S(1)}, bf16[257,320]{1,0:T(8,128)(2,1)S(1)}, u32[]{:S(2)}, u32[]{:S(2)}) collective-permute-start(bf16[257,320]{1,0:T(8,128)(2,1)S(1)} %collective-permute-done.ty), channel_id=1, source_target_pairs={{0,1},{1,0},{2,3},{3,2},{4,5},{5,4},{6,7},{7,6},{8,9},{9,8},{10,11... | collective-permute-start | bytes 493448 | tf_op jit(solution)/shard_map/ppermute | solution.py:316
  18.3 1.9 %collective-permute-start.6 = (bf16[257,640]{1,0:T(8,128)(2,1)S(1)}, bf16[257,640]{1,0:T(8,128)(2,1)S(1)}, u32[]{:S(2)}, u32[]{:S(2)}) collective-permute-start(bf16[257,640]{1,0:T(8,128)(2,1)S(1)} %get-tuple-element.30), channel_id=1, source_target_pairs={{0,1},{1,0},{2,3},{3,2},{4,5},{5,4},{6,7},{7,6},{8,9},{9,8},{10,11... | collective-permute-start | bytes 986888 | tf_op jit(solution)/shard_map/ppermute | solution.py:284
  20.3 10.3 %collective-permute-start.7 = (bf16[257,640]{1,0:T(8,128)(2,1)S(1)}, bf16[257,640]{1,0:T(8,128)(2,1)S(1)}, u32[]{:S(2)}, u32[]{:S(2)}) collective-permute-start(bf16[257,640]{1,0:T(8,128)(2,1)S(1)} %add_convert_fusion.1.chip), channel_id=1, source_target_pairs={{0,2},{2,0},{1,3},{3,1},{4,6},{6,4},{5,7},{7,5},{8,10},{10,8},{9,1... | collective-permute-start | bytes 986888 | tf_op jit(solution)/shard_map/ppermute | solution.py:285
  21.3 9.3 %collective-permute-start.8 = (bf16[257,640]{1,0:T(8,128)(2,1)S(1)}, bf16[257,640]{1,0:T(8,128)(2,1)S(1)}, u32[]{:S(2)}, u32[]{:S(2)}) collective-permute-start(bf16[257,640]{1,0:T(8,128)(2,1)S(1)} %add_convert_fusion.1.chip), channel_id=1, source_target_pairs={{0,1},{1,0},{2,3},{3,2},{4,5},{5,4},{6,7},{7,6},{8,9},{9,8},{10,11... | collective-permute-start | bytes 986888 | tf_op jit(solution)/shard_map/ppermute | solution.py:287
  30.6 1.6 %collective-permute-start.9 = (bf16[257,640]{1,0:T(8,128)(2,1)S(1)}, bf16[257,640]{1,0:T(8,128)(2,1)S(1)}, u32[]{:S(2)}, u32[]{:S(2)}) collective-permute-start(bf16[257,640]{1,0:T(8,128)(2,1)S(1)} %collective-permute-done.7.far), channel_id=1, source_target_pairs={{0,1},{1,0},{2,3},{3,2},{4,5},{5,4},{6,7},{7,6},{8,9},{9,8},{10,11... | collective-permute-start | bytes 986888 | tf_op jit(solution)/shard_map/ppermute | solution.py:286
  35.6 1.7 %collective-permute-start.10 = (bf16[257,640]{1,0:T(8,128)(2,1)S(1)}, bf16[257,640]{1,0:T(8,128)(2,1)S(1)}, u32[]{:S(2)}, u32[]{:S(2)}) collective-permute-start(bf16[257,640]{1,0:T(8,128)(2,1)S(1)} %get-tuple-element.34), channel_id=1, source_target_pairs={{0,1},{1,0},{2,3},{3,2},{4,5},{5,4},{6,7},{7,6},{8,9},{9,8},{10,11... | collective-permute-start | bytes 986888 | tf_op jit(solution)/shard_map/ppermute | solution.py:284
  37.4 10.1 %collective-permute-start.11 = (bf16[257,640]{1,0:T(8,128)(2,1)S(1)}, bf16[257,640]{1,0:T(8,128)(2,1)S(1)}, u32[]{:S(2)}, u32[]{:S(2)}) collective-permute-start(bf16[257,640]{1,0:T(8,128)(2,1)S(1)} %add_convert_fusion.chip), channel_id=1, source_target_pairs={{0,2},{2,0},{1,3},{3,1},{4,6},{6,4},{5,7},{7,5},{8,10},{10,8},{9,1... | collective-permute-start | bytes 986888 | tf_op jit(solution)/shard_map/ppermute | solution.py:285
  38.5 9.0 %collective-permute-start.12 = (bf16[257,640]{1,0:T(8,128)(2,1)S(1)}, bf16[257,640]{1,0:T(8,128)(2,1)S(1)}, u32[]{:S(2)}, u32[]{:S(2)}) collective-permute-start(bf16[257,640]{1,0:T(8,128)(2,1)S(1)} %add_convert_fusion.chip), channel_id=1, source_target_pairs={{0,1},{1,0},{2,3},{3,2},{4,5},{5,4},{6,7},{7,6},{8,9},{9,8},{10,11... | collective-permute-start | bytes 986888 | tf_op jit(solution)/shard_map/ppermute | solution.py:287
  47.5 1.6 %collective-permute-start.13 = (bf16[257,640]{1,0:T(8,128)(2,1)S(1)}, bf16[257,640]{1,0:T(8,128)(2,1)S(1)}, u32[]{:S(2)}, u32[]{:S(2)}) collective-permute-start(bf16[257,640]{1,0:T(8,128)(2,1)S(1)} %collective-permute-done.11.far), channel_id=1, source_target_pairs={{0,1},{1,0},{2,3},{3,2},{4,5},{5,4},{6,7},{7,6},{8,9},{9,8},{10,11... | collective-permute-start | bytes 986888 | tf_op jit(solution)/shard_map/ppermute | solution.py:286
  51.0 27.8 %collective-permute-start.22 = (bf16[1600,128]{1,0:T(8,128)(2,1)S(1)}, bf16[1600,128]{1,0:T(8,128)(2,1)S(1)}, u32[]{:S(2)}, u32[]{:S(2)}) collective-permute-start(bf16[1600,128]{1,0:T(8,128)(2,1)S(1)} %get-tuple-element.44), channel_id=1, source_target_pairs={{0,32},{32,0},{1,33},{33,1},{2,34},{34,2},{3,35},{35,3},{4,36},{36... | collective-permute-start | bytes 1228808 | tf_op jit(solution)/shard_map/ppermute | solution.py:366
  53.2 14.2 %collective-permute-start.14 = (bf16[640,257]{1,0:T(8,128)(2,1)S(1)}, bf16[640,257]{1,0:T(8,128)(2,1)S(1)}, u32[]{:S(2)}, u32[]{:S(2)}) collective-permute-start(bf16[640,257]{1,0:T(8,128)(2,1)S(1)} %shard_map.77), channel_id=1, source_target_pairs={{0,64},{64,0},{128,192},{192,128},{1,65},{65,1},{129,193},{193,129... | collective-permute-start | bytes 986888 | tf_op jit(solution)/shard_map/ppermute | solution.py:363
  54.9 21.9 %collective-permute-start.18 = (bf16[640,257]{1,0:T(8,128)(2,1)S(1)}, bf16[640,257]{1,0:T(8,128)(2,1)S(1)}, u32[]{:S(2)}, u32[]{:S(2)}) collective-permute-start(bf16[640,257]{1,0:T(8,128)(2,1)S(1)} %shard_map.81), channel_id=1, source_target_pairs={{0,192},{64,128},{128,64},{192,0},{1,193},{65,129},{129,65},{193,1... | collective-permute-start | bytes 986888 | tf_op jit(solution)/shard_map/ppermute | solution.py:363
  59.5 12.6 %collective-permute-start.15 = (bf16[257,448]{1,0:T(8,128)(2,1)S(1)}, bf16[257,448]{1,0:T(8,128)(2,1)S(1)}, u32[]{:S(2)}, u32[]{:S(2)}) collective-permute-start(bf16[257,448]{1,0:T(8,128)(2,1)S(1)} %get-tuple-element.41.g), channel_id=1, source_target_pairs={{0,64},{64,0},{128,192},{192,128},{1,65},{65,1},{129,193},{193,129... | collective-permute-start | bytes 690824 | tf_op jit(solution)/shard_map/ppermute | solution.py:363
  60.2 16.6 %collective-permute-start.19 = (bf16[257,512]{1,0:T(8,128)(2,1)S(1)}, bf16[257,512]{1,0:T(8,128)(2,1)S(1)}, u32[]{:S(2)}, u32[]{:S(2)}) collective-permute-start(bf16[257,512]{1,0:T(8,128)(2,1)S(1)} %get-tuple-element.42.g), channel_id=1, source_target_pairs={{0,192},{64,128},{128,64},{192,0},{1,193},{65,129},{129,65},{193,1... | collective-permute-start | bytes 789512 | tf_op jit(solution)/shard_map/ppermute | solution.py:363
  72.5 9.0 %collective-permute-start.16 = (bf16[1120,128]{1,0:T(8,128)(2,1)S(1)}, bf16[1120,128]{1,0:T(8,128)(2,1)S(1)}, u32[]{:S(2)}, u32[]{:S(2)}) collective-permute-start(bf16[1120,128]{1,0:T(8,128)(2,1)S(1)} %shard_map.79), channel_id=1, source_target_pairs={{0,192},{64,128},{128,64},{192,0},{1,193},{65,129},{129,65},{193,1... | collective-permute-start | bytes 860168 | tf_op jit(solution)/shard_map/ppermute | solution.py:363
  77.1 11.5 %collective-permute-start.20 = (bf16[1280,128]{1,0:T(8,128)(2,1)S(1)}, bf16[1280,128]{1,0:T(8,128)(2,1)S(1)}, u32[]{:S(2)}, u32[]{:S(2)}) collective-permute-start(bf16[1280,128]{1,0:T(8,128)(2,1)S(1)} %shard_map.83), channel_id=1, source_target_pairs={{0,32},{32,0},{1,33},{33,1},{2,34},{34,2},{3,35},{35,3},{4,36},{36... | collective-permute-start | bytes 983048 | tf_op jit(solution)/shard_map/ppermute | solution.py:366
  78.9 10.1 %collective-permute-start.23 = (bf16[800,128]{1,0:T(8,128)(2,1)S(1)}, bf16[800,128]{1,0:T(8,128)(2,1)S(1)}, u32[]{:S(2)}, u32[]{:S(2)}) collective-permute-start(bf16[800,128]{1,0:T(8,128)(2,1)S(1)} %get-tuple-element.51), channel_id=1, source_target_pairs={{0,64},{64,0},{128,192},{192,128},{1,65},{65,1},{129,193},{193,129... | collective-permute-start | bytes 614408 | tf_op jit(solution)/shard_map/ppermute | solution.py:363
  81.6 8.7 %collective-permute-start.17 = (bf16[560,128]{1,0:T(8,128)(2,1)S(1)}, bf16[560,128]{1,0:T(8,128)(2,1)S(1)}, u32[]{:S(2)}, u32[]{:S(2)}) collective-permute-start(bf16[560,128]{1,0:T(8,128)(2,1)S(1)} %get-tuple-element.54), channel_id=1, source_target_pairs={{0,32},{32,0},{1,33},{33,1},{2,34},{34,2},{3,35},{35,3},{4,36},{36... | collective-permute-start | bytes 430088 | tf_op jit(solution)/shard_map/ppermute | solution.py:366
  88.7 6.3 %collective-permute-start.21 = (bf16[640,128]{1,0:T(8,128)(2,1)S(1)}, bf16[640,128]{1,0:T(8,128)(2,1)S(1)}, u32[]{:S(2)}, u32[]{:S(2)}) collective-permute-start(bf16[640,128]{1,0:T(8,128)(2,1)S(1)} %get-tuple-element.52), channel_id=1, source_target_pairs={{0,64},{64,0},{128,192},{192,128},{1,65},{65,1},{129,193},{193,129... | collective-permute-start | bytes 491528 | tf_op jit(solution)/shard_map/ppermute | solution.py:363
  89.1 6.0 %collective-permute-start.24 = (bf16[400,128]{1,0:T(8,128)(2,1)S(1)}, bf16[400,128]{1,0:T(8,128)(2,1)S(1)}, u32[]{:S(2)}, u32[]{:S(2)}) collective-permute-start(bf16[400,128]{1,0:T(8,128)(2,1)S(1)} %get-tuple-element.56), channel_id=1, source_target_pairs={{0,192},{64,128},{128,64},{192,0},{1,193},{65,129},{129,65},{193,1... | collective-permute-start | bytes 307208 | tf_op jit(solution)/shard_map/ppermute | solution.py:363
  96.1 20.5 %all-to-all-start = ((bf16[8,200,128]{2,1,0:T(8,128)(2,1)}), bf16[8,200,128]{2,1,0:T(8,128)(2,1)S(1)}, u32[]{:S(2)}, u32[]{:S(2)}) async-start(bf16[8,200,128]{2,1,0:T(8,128)(2,1)} %shard_map.85), calls=%async_computation | async-start | bytes 819200 | tf_op jit(solution)/shard_map/all_to_all | solution.py:453

commit v6 on v5

--- a/solution.py
+++ b/solution.py
@@ -115,14 +115,16 @@
         grads[:, at : at + HD] = got.astype(bf16)
 
     dps = [dot(each[h], qkv[2 * heads + h], COLS) for h in range(heads)]
-    for h in range(heads):
-        put(2, h, dot(probs[h].astype(bf16), each[h], ROWS))
+    dss = []
     for h in range(heads):
         p = probs[h]
         along = jnp.sum(p * dps[h], axis=-1, keepdims=True)
-        ds = (p * (dps[h] - along) * SCALE).astype(bf16)
-        put(0, h, dot(ds, qkv[heads + h]))
-        put(1, h, dot(ds, qkv[h], ROWS))
+        dss.append((p * (dps[h] - along) * SCALE).astype(bf16))
+        put(2, h, dot(probs[h].astype(bf16), each[h], ROWS))
+    for h in range(heads):
+        put(0, h, dot(dss[h], qkv[heads + h]))
+    for h in range(heads):
+        put(1, h, dot(dss[h], qkv[h], ROWS))
 
 
 def input_back(half, grads, w):
@@ -351,7 +353,7 @@
     each = rows // nz
     tall = pltpu.VMEM((4 * rows, tokens), bf16)
     tall_like = like((4 * rows, tokens), bf16)
-    one, two, three = 448, 512, narrow
+    one, two, three = 512, 448, narrow
     give_one = ((1, 0), (1, 1), (2, 0), (2, 1))
     keep_one = ((0, 0), (0, 1), (3, 0), (3, 1))
     give_two = ((3, 0), (2, 0), (3, 1), (2, 1))

time: 118 us -> 118 us (level)
  the two profiles are of different devices: /device:TPU:8 before, /device:TPU:6 now
where the time goes in v6:
time: 118 us
  waiting for transfers between devices  64.6 us (55%)
  starting transfers between devices  28 us (24%)
  Pallas kernels  19.9 us (17%)
  local copies, waits for them, and re-layouts  3.91 us (3%)
    ppermute x8, waiting for transfers between devices, swap_x(): return lax.ppermute(value, 'x', [(i, i ^ by) for i in range(nx)])  20.5 us
    pallas_call x20, Pallas kernels, call(): pl.pallas_call(body, out_shape=outs, in_specs=[vmem] * len(ins), out_spec...  19.9 us
    ppermute x2, waiting for transfers between devices, mp_sum(): far = lax.ppermute(chip, 'yl', SWAP)  17.6 us
    all_to_all x1, waiting for transfers between devices, shards(): got = lax.all_to_all(packed, 'z', 0, 0, tiled=True)  10.9 us
    all_to_all x1, starting transfers between devices, shards(): got = lax.all_to_all(packed, 'z', 0, 0, tiled=True)  8.46 us
    ppermute x3, starting transfers between devices, swap_yh(): return lax.ppermute(value, 'yh', SWAP)  6.66 us
    ppermute x8, starting transfers between devices, swap_x(): return lax.ppermute(value, 'x', [(i, i ^ by) for i in range(nx)])  6.58 us
    ppermute x3, waiting for transfers between devices, swap_yh(): return lax.ppermute(value, 'yh', SWAP)  5.31 us
  transfers between devices with their start and end apart: 26, of which 14 were waited for; matrix products, arithmetic and copies ran while one was open for 2% of the time, Pallas kernels for 9%

profile of v6, /device:TPU:6, one launch (start us, length us, event | category | flops | bytes accessed | tf_op | source)
XLA Modules:
  0.0 117.8 jit_solution(3987864348511710732)
XLA Ops:
  0.6 1.7 %collective-permute-start.3 = (bf16[257,320]{1,0:T(8,128)(2,1)}, bf16[257,320]{1,0:T(8,128)(2,1)S(1)}, u32[]{:S(2)}, u32[]{:S(2)}) collective-permute-start(bf16[257,320]{1,0:T(8,128)(2,1)} %bitcast.11), channel_id=1, source_target_pairs={{0,2},{2,0},{1,3},{3,1},{4,6},{6,4},{5,7},{7,5},{8,10},{10,8},{9,1... | collective-permute-start | bytes 493448 | tf_op jit(solution)/shard_map/ppermute | solution.py:306
  2.3 1.1 copy.10
  3.4 1.7 %copy-done = bf16[3,1280,320]{1,2,0:T(8,128)(2,1)S(1)} copy-done((bf16[3,1280,320]{1,2,0:T(8,128)(2,1)S(1)}, bf16[3,1280,320]{1,2,0:T(8,128)(2,1)}, u32[]{:S(2)}) %copy-start) | copy-done | bytes 2457624
  6.3 1.4 %collective-permute-done.3.zy = bf16[257,320]{1,0:T(8,128)(2,1)S(1)} collective-permute-done((bf16[257,320]{1,0:T(8,128)(2,1)}, bf16[257,320]{1,0:T(8,128)(2,1)S(1)}, u32[]{:S(2)}, u32[]{:S(2)}) %collective-permute-start.3) | collective-permute-done | bytes 164512 | tf_op jit(solution)/shard_map/ppermute | solution.py:306
  8.2 4.2 %collective-permute-done.ty = bf16[257,320]{1,0:T(8,128)(2,1)S(1)} collective-permute-done((bf16[257,320]{1,0:T(8,128)(2,1)S(1)}, bf16[257,320]{1,0:T(8,128)(2,1)S(1)}, u32[]{:S(2)}, u32[]{:S(2)}) %collective-permute-start) | collective-permute-done | bytes 164512 | tf_op jit(solution)/shard_map/ppermute | solution.py:317
  12.6 2.9 %shard_map.69 = (bf16[257,1280]{1,0:T(8,128)(2,1)S(1)}, bf16[1280,257]{1,0:T(8,128)(2,1)S(1)}, f32[257,128]{1,0:T(8,128)S(1)}, bf16[12,257,80]{2,1,0:T(8,128)(2,...) custom-call(bf16[257,320]{1,0:T(8,128)(2,1)S(1)} %bitcast.13, ...), custom_call_target="tpu_custom_call" | custom-call | flops 716145920 | bytes 6277648 | tf_op jit(solution)/shard_map/pallas_call | solution.py:35
  15.6 2.8 %shard_map.70 = (bf16[257,1280]{1,0:T(8,128)(2,1)S(1)}, bf16[257,960]{1,0:T(8,128)(2,1)S(1)}, bf16[257,640]{1,0:T(8,128)(2,1)S(1)}) custom-call(bf16[257,320]{1,0:T(8,128)(2,1)S(1)} %get-tuple-element.25.t0, bf16[257,320]{1,0:T(8,128)(2,1)S(1)} %collective-permute-done.ty, bf16[257,320]{1,0:T(8,128)(2,1)S(1)} %collective-permute-done.1.tc, ...), custom_call_target="tpu_custom_call" | custom-call | flops 800688640 | bytes 6965264 | tf_op jit(solution)/shard_map/pallas_call | solution.py:35
  20.3 1.4 %collective-permute-start.7 = (bf16[257,640]{1,0:T(8,128)(2,1)S(1)}, bf16[257,640]{1,0:T(8,128)(2,1)S(1)}, u32[]{:S(2)}, u32[]{:S(2)}) collective-permute-start(bf16[257,640]{1,0:T(8,128)(2,1)S(1)} %add_convert_fusion.1.chip), channel_id=1, source_target_pairs={{0,2},{2,0},{1,3},{3,1},{4,6},{6,4},{5,7},{7,5},{8,10},{10,8},{9,1... | collective-permute-start | bytes 986888 | tf_op jit(solution)/shard_map/ppermute | solution.py:287
  21.8 8.8 %collective-permute-done.7.far = bf16[257,640]{1,0:T(8,128)(2,1)S(1)} collective-permute-done((bf16[257,640]{1,0:T(8,128)(2,1)S(1)}, bf16[257,640]{1,0:T(8,128)(2,1)S(1)}, u32[]{:S(2)}, u32[]{:S(2)}) %collective-permute-start.7) | collective-permute-done | bytes 328992 | tf_op jit(solution)/shard_map/ppermute | solution.py:287
  30.6 1.6 %collective-permute-done.9.far_c = bf16[257,640]{1,0:T(8,128)(2,1)S(1)} collective-permute-done((bf16[257,640]{1,0:T(8,128)(2,1)S(1)}, bf16[257,640]{1,0:T(8,128)(2,1)S(1)}, u32[]{:S(2)}, u32[]{:S(2)}) %collective-permute-start.9) | collective-permute-done | bytes 328992 | tf_op jit(solution)/shard_map/ppermute | solution.py:288
  32.3 3.2 %shard_map.72 = (f32[257,1280]{1,0:T(8,128)S(1)}, bf16[257,960]{1,0:T(8,128)(2,1)S(1)}, bf16[257,640]{1,0:T(8,128)(2,1)S(1)}) custom-call(bf16[257,640]{1,0:T(8,128)(2,1)S(1)} %add_convert_fusion.1.chip, bf16[257,640]{1,0:T(8,128)(2,1)S(1)} %collective-permute-done.7.far, bf16[257,640]{1,0:T(8,128)(2,1)S(1)} %collective-permute-done.8.chip_c, ...), custom_call_target="tpu_custom_call" | custom-call | flops 800688640 | bytes 9070608 | tf_op jit(solution)/shard_map/pallas_call | solution.py:35
  36.4 0.9 collective-permute-done.10
  37.3 1.4 %collective-permute-start.11 = (bf16[257,640]{1,0:T(8,128)(2,1)S(1)}, bf16[257,640]{1,0:T(8,128)(2,1)S(1)}, u32[]{:S(2)}, u32[]{:S(2)}) collective-permute-start(bf16[257,640]{1,0:T(8,128)(2,1)S(1)} %add_convert_fusion.chip), channel_id=1, source_target_pairs={{0,2},{2,0},{1,3},{3,1},{4,6},{6,4},{5,7},{7,5},{8,10},{10,8},{9,1... | collective-permute-start | bytes 986888 | tf_op jit(solution)/shard_map/ppermute | solution.py:287
  38.7 8.7 %collective-permute-done.11.far = bf16[257,640]{1,0:T(8,128)(2,1)S(1)} collective-permute-done((bf16[257,640]{1,0:T(8,128)(2,1)S(1)}, bf16[257,640]{1,0:T(8,128)(2,1)S(1)}, u32[]{:S(2)}, u32[]{:S(2)}) %collective-permute-start.11) | collective-permute-done | bytes 328992 | tf_op jit(solution)/shard_map/ppermute | solution.py:287
  47.4 1.6 %collective-permute-done.13.far_c = bf16[257,640]{1,0:T(8,128)(2,1)S(1)} collective-permute-done((bf16[257,640]{1,0:T(8,128)(2,1)S(1)}, bf16[257,640]{1,0:T(8,128)(2,1)S(1)}, u32[]{:S(2)}, u32[]{:S(2)}) %collective-permute-start.13) | collective-permute-done | bytes 328992 | tf_op jit(solution)/shard_map/ppermute | solution.py:288
  49.0 1.7 %shard_map.74 = (f32[257,320]{1,0:T(8,128)S(1)}, bf16[257,1280]{1,0:T(8,128)(2,1)S(1)}, bf16[1280,257]{1,0:T(8,128)(2,1)S(1)}, bf16[1600,128]{1,0:T(8,128)(2,1)S(1)}) custom-call(bf16[257,640]{1,0:T(8,128)(2,1)S(1)} %add_convert_fusion.chip, bf16[257,640]{1,0:T(8,128)(2,1)S(1)} %collective-permute-done.11.far, ...), custom_call_target="tpu_custom_call" | custom-call | flops 210534400 | bytes 6626944 | tf_op jit(solution)/shard_map/pallas_call | solution.py:35
  50.7 3.0 %collective-permute-start.22 = (bf16[1600,128]{1,0:T(8,128)(2,1)S(1)}, bf16[1600,128]{1,0:T(8,128)(2,1)S(1)}, u32[]{:S(2)}, u32[]{:S(2)}) collective-permute-start(bf16[1600,128]{1,0:T(8,128)(2,1)S(1)} %get-tuple-element.44), channel_id=1, source_target_pairs={{0,32},{32,0},{1,33},{33,1},{2,34},{34,2},{3,35},{35,3},{4,36},{36... | collective-permute-start | bytes 1228808 | tf_op jit(solution)/shard_map/ppermute | solution.py:368
  54.4 1.0 collective-permute-start.14
  55.4 2.2 %shard_map.75 = (bf16[257,512]{1,0:T(8,128)(2,1)S(1)}, bf16[257,448]{1,0:T(8,128)(2,1)S(1)}) custom-call(bf16[257,1280]{1,0:T(8,128)(2,1)S(1)} %get-tuple-element.40.total, bf16[320,1280]{1,0:T(8,128)(2,1)S(1)} %shard_map.68.w_out, bf16[12,257,80]{2,1,0:T(8,128)(2,1)S(1)} %get-tuple-element.27.qkv, f32[4,257,257]{2,1,0:T(8,128)S(1)} %get-tuple-element.28.probs), custom_call_target="tpu_custom_call" | custom-call | flops 379619840 | bytes 3520784 | tf_op jit(solution)/shard_map/pallas_call | solution.py:35
  57.5 2.2 %collective-permute-start.19 = (bf16[257,448]{1,0:T(8,128)(2,1)S(1)}, bf16[257,448]{1,0:T(8,128)(2,1)S(1)}, u32[]{:S(2)}, u32[]{:S(2)}) collective-permute-start(bf16[257,448]{1,0:T(8,128)(2,1)S(1)} %get-tuple-element.42.g), channel_id=1, source_target_pairs={{0,192},{64,128},{128,64},{192,0},{1,193},{65,129},{129,65},{193,1... | collective-permute-start | bytes 690824 | tf_op jit(solution)/shard_map/ppermute | solution.py:365
  59.7 1.2 %collective-permute-start.15 = (bf16[257,512]{1,0:T(8,128)(2,1)S(1)}, bf16[257,512]{1,0:T(8,128)(2,1)S(1)}, u32[]{:S(2)}, u32[]{:S(2)}) collective-permute-start(bf16[257,512]{1,0:T(8,128)(2,1)S(1)} %get-tuple-element.41.g), channel_id=1, source_target_pairs={{0,64},{64,0},{128,192},{192,128},{1,65},{65,1},{129,193},{193,129... | collective-permute-start | bytes 789512 | tf_op jit(solution)/shard_map/ppermute | solution.py:365
  61.4 7.7 %collective-permute-done.18.x = bf16[640,257]{1,0:T(8,128)(2,1)S(1)} collective-permute-done((bf16[640,257]{1,0:T(8,128)(2,1)S(1)}, bf16[640,257]{1,0:T(8,128)(2,1)S(1)}, u32[]{:S(2)}, u32[]{:S(2)}) %collective-permute-start.18) | collective-permute-done | bytes 328992 | tf_op jit(solution)/shard_map/ppermute | solution.py:365
  69.2 4.7 %collective-permute-done.19.g = bf16[257,448]{1,0:T(8,128)(2,1)S(1)} collective-permute-done((bf16[257,448]{1,0:T(8,128)(2,1)S(1)}, bf16[257,448]{1,0:T(8,128)(2,1)S(1)}, u32[]{:S(2)}, u32[]{:S(2)}) %collective-permute-start.19) | collective-permute-done | bytes 230304 | tf_op jit(solution)/shard_map/ppermute | solution.py:365
  76.8 0.9 collective-permute-start.16
  78.3 5.3 %collective-permute-done.20 = bf16[1120,128]{1,0:T(8,128)(2,1)S(1)} collective-permute-done((bf16[1120,128]{1,0:T(8,128)(2,1)S(1)}, bf16[1120,128]{1,0:T(8,128)(2,1)S(1)}, u32[]{:S(2)}, u32[]{:S(2)}) %collective-permute-start.20) | collective-permute-done | bytes 286752 | tf_op jit(solution)/shard_map/ppermute | solution.py:368
  83.8 2.7 %collective-permute-done.16 = bf16[1280,128]{1,0:T(8,128)(2,1)S(1)} collective-permute-done((bf16[1280,128]{1,0:T(8,128)(2,1)S(1)}, bf16[1280,128]{1,0:T(8,128)(2,1)S(1)}, u32[]{:S(2)}, u32[]{:S(2)}) %collective-permute-start.16) | collective-permute-done | bytes 327712 | tf_op jit(solution)/shard_map/ppermute | solution.py:365
  86.5 3.0 %collective-permute-start.17 = (bf16[640,128]{1,0:T(8,128)(2,1)S(1)}, bf16[640,128]{1,0:T(8,128)(2,1)S(1)}, u32[]{:S(2)}, u32[]{:S(2)}) collective-permute-start(bf16[640,128]{1,0:T(8,128)(2,1)S(1)} %get-tuple-element.52), channel_id=1, source_target_pairs={{0,32},{32,0},{1,33},{33,1},{2,34},{34,2},{3,35},{35,3},{4,36},{36... | collective-permute-start | bytes 491528 | tf_op jit(solution)/shard_map/ppermute | solution.py:368
  90.1 5.4 %collective-permute-done.24.g3 = bf16[400,128]{1,0:T(8,128)(2,1)S(1)} collective-permute-done((bf16[400,128]{1,0:T(8,128)(2,1)S(1)}, bf16[400,128]{1,0:T(8,128)(2,1)S(1)}, u32[]{:S(2)}, u32[]{:S(2)}) %collective-permute-start.24) | collective-permute-done | bytes 102432 | tf_op jit(solution)/shard_map/ppermute | solution.py:365
  95.5 1.0 shard_map.85
  96.5 8.5 %all-to-all-start = ((bf16[8,200,128]{2,1,0:T(8,128)(2,1)}), bf16[8,200,128]{2,1,0:T(8,128)(2,1)S(1)}, u32[]{:S(2)}, u32[]{:S(2)}) async-start(bf16[8,200,128]{2,1,0:T(8,128)(2,1)} %shard_map.85), calls=%async_computation | async-start | bytes 819200 | tf_op jit(solution)/shard_map/all_to_all | solution.py:455
  105.0 1.2 copy.7
  106.1 10.9 %all-to-all-done.got = bf16[8,200,128]{2,1,0:T(8,128)(2,1)S(1)} async-done(((bf16[8,200,128]{2,1,0:T(8,128)(2,1)}), bf16[8,200,128]{2,1,0:T(8,128)(2,1)S(1)}, u32[]{:S(2)}, u32[]{:S(2)}) %all-to-all-start) | async-done | bytes 409632 | tf_op jit(solution)/shard_map/all_to_all | solution.py:455
  (54 shorter events, 11.3 us)
Async XLA Ops:
  0.6 7.1 %collective-permute-start.3 = (bf16[257,320]{1,0:T(8,128)(2,1)}, bf16[257,320]{1,0:T(8,128)(2,1)S(1)}, u32[]{:S(2)}, u32[]{:S(2)}) collective-permute-start(bf16[257,320]{1,0:T(8,128)(2,1)} %bitcast.11), channel_id=1, source_target_pairs={{0,2},{2,0},{1,3},{3,1},{4,6},{6,4},{5,7},{7,5},{8,10},{10,8},{9,1... | collective-permute-start | bytes 493448 | tf_op jit(solution)/shard_map/ppermute | solution.py:306
  2.3 4.0 %copy-start.2 = (bf16[1,257,320]{2,1,0:T(8,128)(2,1)S(1)}, bf16[1,257,320]{2,1,0:T(8,128)(2,1)}, u32[]{:S(2)}) copy-start(bf16[1,257,320]{2,1,0:T(8,128)(2,1)} %param.4) | copy-start | bytes 493444
  3.4 1.7 %copy-start = (bf16[3,1280,320]{1,2,0:T(8,128)(2,1)S(1)}, bf16[3,1280,320]{1,2,0:T(8,128)(2,1)}, u32[]{:S(2)}) copy-start(bf16[3,1280,320]{1,2,0:T(8,128)(2,1)} %param.6) | copy-start | bytes 7372804
  5.1 7.3 %copy-start.1 = (bf16[320,1280]{1,0:T(8,128)(2,1)S(1)}, bf16[320,1280]{1,0:T(8,128)(2,1)}, u32[]{:S(2)}) copy-start(bf16[320,1280]{1,0:T(8,128)(2,1)} %w_out.1) | copy-start | bytes 2457604
  5.8 6.6 %collective-permute-start = (bf16[257,320]{1,0:T(8,128)(2,1)S(1)}, bf16[257,320]{1,0:T(8,128)(2,1)S(1)}, u32[]{:S(2)}, u32[]{:S(2)}) collective-permute-start(bf16[257,320]{1,0:T(8,128)(2,1)S(1)} %get-tuple-element.25.t0), channel_id=1, source_target_pairs={{0,2},{2,0},{1,3},{3,1},{4,6},{6,4},{5,7},{7,5},{8,10},{10,8},{9,1... | collective-permute-start | bytes 493448 | tf_op jit(solution)/shard_map/ppermute | solution.py:317
  6.3 6.3 %collective-permute-start.4 = (bf16[257,320]{1,0:T(8,128)(2,1)S(1)}, bf16[257,320]{1,0:T(8,128)(2,1)S(1)}, u32[]{:S(2)}, u32[]{:S(2)}) collective-permute-start(bf16[257,320]{1,0:T(8,128)(2,1)S(1)} %bitcast.12), channel_id=1, source_target_pairs={{0,1},{1,0},{2,3},{3,2},{4,5},{5,4},{6,7},{7,6},{8,9},{9,8},{10,11... | collective-permute-start | bytes 493448 | tf_op jit(solution)/shard_map/ppermute | solution.py:307
  7.7 4.9 %collective-permute-start.5 = (bf16[257,320]{1,0:T(8,128)(2,1)S(1)}, bf16[257,320]{1,0:T(8,128)(2,1)S(1)}, u32[]{:S(2)}, u32[]{:S(2)}) collective-permute-start(bf16[257,320]{1,0:T(8,128)(2,1)S(1)} %collective-permute-done.3.zy), channel_id=1, source_target_pairs={{0,1},{1,0},{2,3},{3,2},{4,5},{5,4},{6,7},{7,6},{8,9},{9,8},{10,11... | collective-permute-start | bytes 493448 | tf_op jit(solution)/shard_map/ppermute | solution.py:316
  7.7 7.9 %collective-permute-start.1 = (bf16[257,320]{1,0:T(8,128)(2,1)S(1)}, bf16[257,320]{1,0:T(8,128)(2,1)S(1)}, u32[]{:S(2)}, u32[]{:S(2)}) collective-permute-start(bf16[257,320]{1,0:T(8,128)(2,1)S(1)} %get-tuple-element.25.t0), channel_id=1, source_target_pairs={{0,1},{1,0},{2,3},{3,2},{4,5},{5,4},{6,7},{7,6},{8,9},{9,8},{10,11... | collective-permute-start | bytes 493448 | tf_op jit(solution)/shard_map/ppermute | solution.py:315
  12.4 3.2 %collective-permute-start.2 = (bf16[257,320]{1,0:T(8,128)(2,1)S(1)}, bf16[257,320]{1,0:T(8,128)(2,1)S(1)}, u32[]{:S(2)}, u32[]{:S(2)}) collective-permute-start(bf16[257,320]{1,0:T(8,128)(2,1)S(1)} %collective-permute-done.ty), channel_id=1, source_target_pairs={{0,1},{1,0},{2,3},{3,2},{4,5},{5,4},{6,7},{7,6},{8,9},{9,8},{10,11... | collective-permute-start | bytes 493448 | tf_op jit(solution)/shard_map/ppermute | solution.py:318
  18.4 1.9 %collective-permute-start.6 = (bf16[257,640]{1,0:T(8,128)(2,1)S(1)}, bf16[257,640]{1,0:T(8,128)(2,1)S(1)}, u32[]{:S(2)}, u32[]{:S(2)}) collective-permute-start(bf16[257,640]{1,0:T(8,128)(2,1)S(1)} %get-tuple-element.30), channel_id=1, source_target_pairs={{0,1},{1,0},{2,3},{3,2},{4,5},{5,4},{6,7},{7,6},{8,9},{9,8},{10,11... | collective-permute-start | bytes 986888 | tf_op jit(solution)/shard_map/ppermute | solution.py:286
  20.3 10.3 %collective-permute-start.7 = (bf16[257,640]{1,0:T(8,128)(2,1)S(1)}, bf16[257,640]{1,0:T(8,128)(2,1)S(1)}, u32[]{:S(2)}, u32[]{:S(2)}) collective-permute-start(bf16[257,640]{1,0:T(8,128)(2,1)S(1)} %add_convert_fusion.1.chip), channel_id=1, source_target_pairs={{0,2},{2,0},{1,3},{3,1},{4,6},{6,4},{5,7},{7,5},{8,10},{10,8},{9,1... | collective-permute-start | bytes 986888 | tf_op jit(solution)/shard_map/ppermute | solution.py:287
  21.7 9.0 %collective-permute-start.8 = (bf16[257,640]{1,0:T(8,128)(2,1)S(1)}, bf16[257,640]{1,0:T(8,128)(2,1)S(1)}, u32[]{:S(2)}, u32[]{:S(2)}) collective-permute-start(bf16[257,640]{1,0:T(8,128)(2,1)S(1)} %add_convert_fusion.1.chip), channel_id=1, source_target_pairs={{0,1},{1,0},{2,3},{3,2},{4,5},{5,4},{6,7},{7,6},{8,9},{9,8},{10,11... | collective-permute-start | bytes 986888 | tf_op jit(solution)/shard_map/ppermute | solution.py:289
  30.6 1.6 %collective-permute-start.9 = (bf16[257,640]{1,0:T(8,128)(2,1)S(1)}, bf16[257,640]{1,0:T(8,128)(2,1)S(1)}, u32[]{:S(2)}, u32[]{:S(2)}) collective-permute-start(bf16[257,640]{1,0:T(8,128)(2,1)S(1)} %collective-permute-done.7.far), channel_id=1, source_target_pairs={{0,1},{1,0},{2,3},{3,2},{4,5},{5,4},{6,7},{7,6},{8,9},{9,8},{10,11... | collective-permute-start | bytes 986888 | tf_op jit(solution)/shard_map/ppermute | solution.py:288
  35.5 1.7 %collective-permute-start.10 = (bf16[257,640]{1,0:T(8,128)(2,1)S(1)}, bf16[257,640]{1,0:T(8,128)(2,1)S(1)}, u32[]{:S(2)}, u32[]{:S(2)}) collective-permute-start(bf16[257,640]{1,0:T(8,128)(2,1)S(1)} %get-tuple-element.34), channel_id=1, source_target_pairs={{0,1},{1,0},{2,3},{3,2},{4,5},{5,4},{6,7},{7,6},{8,9},{9,8},{10,11... | collective-permute-start | bytes 986888 | tf_op jit(solution)/shard_map/ppermute | solution.py:286
  37.3 10.1 %collective-permute-start.11 = (bf16[257,640]{1,0:T(8,128)(2,1)S(1)}, bf16[257,640]{1,0:T(8,128)(2,1)S(1)}, u32[]{:S(2)}, u32[]{:S(2)}) collective-permute-start(bf16[257,640]{1,0:T(8,128)(2,1)S(1)} %add_convert_fusion.chip), channel_id=1, source_target_pairs={{0,2},{2,0},{1,3},{3,1},{4,6},{6,4},{5,7},{7,5},{8,10},{10,8},{9,1... | collective-permute-start | bytes 986888 | tf_op jit(solution)/shard_map/ppermute | solution.py:287
  38.7 8.7 %collective-permute-start.12 = (bf16[257,640]{1,0:T(8,128)(2,1)S(1)}, bf16[257,640]{1,0:T(8,128)(2,1)S(1)}, u32[]{:S(2)}, u32[]{:S(2)}) collective-permute-start(bf16[257,640]{1,0:T(8,128)(2,1)S(1)} %add_convert_fusion.chip), channel_id=1, source_target_pairs={{0,1},{1,0},{2,3},{3,2},{4,5},{5,4},{6,7},{7,6},{8,9},{9,8},{10,11... | collective-permute-start | bytes 986888 | tf_op jit(solution)/shard_map/ppermute | solution.py:289
  47.4 1.6 %collective-permute-start.13 = (bf16[257,640]{1,0:T(8,128)(2,1)S(1)}, bf16[257,640]{1,0:T(8,128)(2,1)S(1)}, u32[]{:S(2)}, u32[]{:S(2)}) collective-permute-start(bf16[257,640]{1,0:T(8,128)(2,1)S(1)} %collective-permute-done.11.far), channel_id=1, source_target_pairs={{0,1},{1,0},{2,3},{3,2},{4,5},{5,4},{6,7},{7,6},{8,9},{9,8},{10,11... | collective-permute-start | bytes 986888 | tf_op jit(solution)/shard_map/ppermute | solution.py:288
  50.7 27.3 %collective-permute-start.22 = (bf16[1600,128]{1,0:T(8,128)(2,1)S(1)}, bf16[1600,128]{1,0:T(8,128)(2,1)S(1)}, u32[]{:S(2)}, u32[]{:S(2)}) collective-permute-start(bf16[1600,128]{1,0:T(8,128)(2,1)S(1)} %get-tuple-element.44), channel_id=1, source_target_pairs={{0,32},{32,0},{1,33},{33,1},{2,34},{34,2},{3,35},{35,3},{4,36},{36... | collective-permute-start | bytes 1228808 | tf_op jit(solution)/shard_map/ppermute | solution.py:368
  53.8 15.4 %collective-permute-start.18 = (bf16[640,257]{1,0:T(8,128)(2,1)S(1)}, bf16[640,257]{1,0:T(8,128)(2,1)S(1)}, u32[]{:S(2)}, u32[]{:S(2)}) collective-permute-start(bf16[640,257]{1,0:T(8,128)(2,1)S(1)} %shard_map.81), channel_id=1, source_target_pairs={{0,192},{64,128},{128,64},{192,0},{1,193},{65,129},{129,65},{193,1... | collective-permute-start | bytes 986888 | tf_op jit(solution)/shard_map/ppermute | solution.py:365
  54.4 22.0 %collective-permute-start.14 = (bf16[640,257]{1,0:T(8,128)(2,1)S(1)}, bf16[640,257]{1,0:T(8,128)(2,1)S(1)}, u32[]{:S(2)}, u32[]{:S(2)}) collective-permute-start(bf16[640,257]{1,0:T(8,128)(2,1)S(1)} %shard_map.77), channel_id=1, source_target_pairs={{0,64},{64,0},{128,192},{192,128},{1,65},{65,1},{129,193},{193,129... | collective-permute-start | bytes 986888 | tf_op jit(solution)/shard_map/ppermute | solution.py:365
  57.5 16.3 %collective-permute-start.19 = (bf16[257,448]{1,0:T(8,128)(2,1)S(1)}, bf16[257,448]{1,0:T(8,128)(2,1)S(1)}, u32[]{:S(2)}, u32[]{:S(2)}) collective-permute-start(bf16[257,448]{1,0:T(8,128)(2,1)S(1)} %get-tuple-element.42.g), channel_id=1, source_target_pairs={{0,192},{64,128},{128,64},{192,0},{1,193},{65,129},{129,65},{193,1... | collective-permute-start | bytes 690824 | tf_op jit(solution)/shard_map/ppermute | solution.py:365
  59.7 16.7 %collective-permute-start.15 = (bf16[257,512]{1,0:T(8,128)(2,1)S(1)}, bf16[257,512]{1,0:T(8,128)(2,1)S(1)}, u32[]{:S(2)}, u32[]{:S(2)}) collective-permute-start(bf16[257,512]{1,0:T(8,128)(2,1)S(1)} %get-tuple-element.41.g), channel_id=1, source_target_pairs={{0,64},{64,0},{128,192},{192,128},{1,65},{65,1},{129,193},{193,129... | collective-permute-start | bytes 789512 | tf_op jit(solution)/shard_map/ppermute | solution.py:365
  74.3 9.3 %collective-permute-start.20 = (bf16[1120,128]{1,0:T(8,128)(2,1)S(1)}, bf16[1120,128]{1,0:T(8,128)(2,1)S(1)}, u32[]{:S(2)}, u32[]{:S(2)}) collective-permute-start(bf16[1120,128]{1,0:T(8,128)(2,1)S(1)} %shard_map.83), channel_id=1, source_target_pairs={{0,32},{32,0},{1,33},{33,1},{2,34},{34,2},{3,35},{35,3},{4,36},{36... | collective-permute-start | bytes 860168 | tf_op jit(solution)/shard_map/ppermute | solution.py:368
  76.8 9.6 %collective-permute-start.16 = (bf16[1280,128]{1,0:T(8,128)(2,1)S(1)}, bf16[1280,128]{1,0:T(8,128)(2,1)S(1)}, u32[]{:S(2)}, u32[]{:S(2)}) collective-permute-start(bf16[1280,128]{1,0:T(8,128)(2,1)S(1)} %shard_map.79), channel_id=1, source_target_pairs={{0,192},{64,128},{128,64},{192,0},{1,193},{65,129},{129,65},{193,1... | collective-permute-start | bytes 983048 | tf_op jit(solution)/shard_map/ppermute | solution.py:365
  78.2 11.3 %collective-permute-start.23 = (bf16[800,128]{1,0:T(8,128)(2,1)S(1)}, bf16[800,128]{1,0:T(8,128)(2,1)S(1)}, u32[]{:S(2)}, u32[]{:S(2)}) collective-permute-start(bf16[800,128]{1,0:T(8,128)(2,1)S(1)} %get-tuple-element.51), channel_id=1, source_target_pairs={{0,64},{64,0},{128,192},{192,128},{1,65},{65,1},{129,193},{193,129... | collective-permute-start | bytes 614408 | tf_op jit(solution)/shard_map/ppermute | solution.py:365
  83.7 6.5 %collective-permute-start.21 = (bf16[560,128]{1,0:T(8,128)(2,1)S(1)}, bf16[560,128]{1,0:T(8,128)(2,1)S(1)}, u32[]{:S(2)}, u32[]{:S(2)}) collective-permute-start(bf16[560,128]{1,0:T(8,128)(2,1)S(1)} %get-tuple-element.54), channel_id=1, source_target_pairs={{0,64},{64,0},{128,192},{192,128},{1,65},{65,1},{129,193},{193,129... | collective-permute-start | bytes 430088 | tf_op jit(solution)/shard_map/ppermute | solution.py:365
  86.5 9.0 %collective-permute-start.17 = (bf16[640,128]{1,0:T(8,128)(2,1)S(1)}, bf16[640,128]{1,0:T(8,128)(2,1)S(1)}, u32[]{:S(2)}, u32[]{:S(2)}) collective-permute-start(bf16[640,128]{1,0:T(8,128)(2,1)S(1)} %get-tuple-element.52), channel_id=1, source_target_pairs={{0,32},{32,0},{1,33},{33,1},{2,34},{34,2},{3,35},{35,3},{4,36},{36... | collective-permute-start | bytes 491528 | tf_op jit(solution)/shard_map/ppermute | solution.py:368
  89.5 6.0 %collective-permute-start.24 = (bf16[400,128]{1,0:T(8,128)(2,1)S(1)}, bf16[400,128]{1,0:T(8,128)(2,1)S(1)}, u32[]{:S(2)}, u32[]{:S(2)}) collective-permute-start(bf16[400,128]{1,0:T(8,128)(2,1)S(1)} %get-tuple-element.56), channel_id=1, source_target_pairs={{0,192},{64,128},{128,64},{192,0},{1,193},{65,129},{129,65},{193,1... | collective-permute-start | bytes 307208 | tf_op jit(solution)/shard_map/ppermute | solution.py:365
  96.5 20.6 %all-to-all-start = ((bf16[8,200,128]{2,1,0:T(8,128)(2,1)}), bf16[8,200,128]{2,1,0:T(8,128)(2,1)S(1)}, u32[]{:S(2)}, u32[]{:S(2)}) async-start(bf16[8,200,128]{2,1,0:T(8,128)(2,1)} %shard_map.85), calls=%async_computation | async-start | bytes 819200 | tf_op jit(solution)/shard_map/all_to_all | solution.py:455
